TPU v7x, 32 devices: a whole 2x2x4 slice. The times are simulated.
32 devices in a mesh: dp: 4 (over z), ep: 8 (over y, x, core).
Axes of the slice: x: 2, y: 2, z: 4, core: 2. Of those that a mesh axis runs over, the one named last changes fastest.
Arguments:
- x_in: bfloat16 [32, 256, 1536], P(('dp', 'ep'))
- dy_in: bfloat16 [32, 256, 1536], P(('dp', 'ep'))
- route_idx: int32 [32, 256, 6], P(('dp', 'ep'))
- gain_attn: bfloat16 [1536], replicated
- w_qkv: bfloat16 [1536, 4608], replicated
- w_o: bfloat16 [1536, 1536], replicated
- gain_ffn: bfloat16 [1536], replicated
- w_router: bfloat16 [1536, 64], replicated
- w_up: bfloat16 [64, 1536, 512], P('ep')
- w_lin: bfloat16 [64, 1536, 512], P('ep')
- w_down: bfloat16 [64, 512, 1536], P('ep')
Outputs:
- output 1: bfloat16 [32, 256, 1536], P(('dp', 'ep'))
- output 2: float32 [1536], replicated
- output 3: float32 [1536, 4608], replicated
- output 4: float32 [1536, 1536], replicated
- output 5: float32 [1536], replicated
- output 6: float32 [1536, 64], replicated
- output 7: float32 [64, 1536, 512], P('ep')
- output 8: float32 [64, 1536, 512], P('ep')
- output 9: float32 [64, 512, 1536], P('ep')
All inputs are finite; a program needn't handle non-finite values.
Results may differ from a plain program's by a relative error of at most 0.017496.
Values are sent between devices in bfloat16 or wider.
A program may use at most 1 GiB of HBM per device.

v0:
```python
import functools

import jax
import jax.numpy as jnp
from jax import lax
from jax.experimental import pallas as pl
from jax.experimental.pallas import tpu as pltpu
from jax.sharding import PartitionSpec as P


EPS = 1e-6
HEAD = 128
DROPPED = 64.0
UNCHOSEN = 128.0
F32 = jnp.float32
BF16 = jnp.bfloat16


def mm(spec, a, b):
    return jnp.einsum(spec, a, b, preferred_element_type=F32)


def rms_norm(values, gain):
    scale = lax.rsqrt(jnp.mean(values * values, axis=-1, keepdims=True) + EPS)
    return (values * scale * gain).astype(BF16)


def attn_core(qkv_rows):
    num_seqs, seq_len, width = qkv_rows.shape
    heads = width // (3 * HEAD)
    split = qkv_rows.reshape(num_seqs, seq_len, 3, heads, HEAD)
    scores = mm('bqhc,bkhc->bhqk', split[:, :, 0], split[:, :, 1]) * (HEAD ** -0.5)
    rows = lax.broadcasted_iota(jnp.int32, (seq_len, seq_len), 0)
    cols = lax.broadcasted_iota(jnp.int32, (seq_len, seq_len), 1)
    scores = jnp.where(rows >= cols, scores, -1e30)
    prob_rows = jax.nn.softmax(scores, axis=-1).astype(BF16)
    mixed = mm('bhqk,bkhc->bqhc', prob_rows, split[:, :, 2])
    return mixed.astype(BF16).reshape(num_seqs, seq_len, heads * HEAD)


def slot_codes(idx_rows, experts, cap):
    tokens = idx_rows.shape[0]
    chosen = jnp.any(idx_rows[:, :, None] == jnp.arange(experts, dtype=jnp.int32), axis=1).astype(BF16)
    rows = lax.broadcasted_iota(jnp.int32, (tokens, tokens), 0)
    cols = lax.broadcasted_iota(jnp.int32, (tokens, tokens), 1)
    prior = mm('se,st->et', chosen, (rows < cols).astype(BF16))
    taken = mm('se,st->et', chosen, (rows == cols).astype(BF16))
    return jnp.where(taken > 0.5, jnp.where(prior < cap, prior, DROPPED), UNCHOSEN).astype(BF16)


def one_hot(codes, cap):
    slots = lax.broadcasted_iota(jnp.int32, codes.shape[:-1] + (cap, codes.shape[-1]), codes.ndim - 1)
    return (codes[..., None, :].astype(F32) == slots.astype(F32)).astype(BF16)


def gates_of(xn, codes, w_router):
    logits = mm('...td,de->...et', xn, w_router)
    prob = jax.nn.softmax(logits, axis=-2)
    mask = (codes.astype(F32) < UNCHOSEN - 1.0).astype(F32)
    picked = prob * mask
    total = jnp.sum(picked, axis=-2, keepdims=True)
    return prob, mask, picked / total, total


def after(value, *deps):
    return lax.optimization_barrier((value,) + deps)[0]


HALF = 768
CHUNK = 128
STEPS = HALF // CHUNK
MESH = pl.DeviceIdType.MESH


def dot_tn(a, b):
    return lax.dot_general(a, b, (((0,), (0,)), ((), ())), preferred_element_type=jnp.float32)


def dense_kernel(xn_ref, ao_ref, dsend_ref, gains_ref, low_ref, high_ref, gains_out_ref,
                 dall, part, z_in, total, gain_buf,
                 d_send, d_recv, dp_send, dp_recv, z_send, z_recv, own_sem, g_send, g_recv):
    z = lax.axis_index('dp')
    ep = lax.axis_index('ep')
    core = lax.rem(ep, 2)
    quarter = ep // 2
    width = dsend_ref.shape[2]
    split = width * 3 // 4
    tokens = dsend_ref.shape[1]
    partner = ep + 1 - 2 * core
    bit_x = lax.rem(quarter, 2)
    bit_y = quarter // 2
    flip = lambda bx, by: 2 * ((bit_x + bx - 2 * bit_x * bx) + 2 * (bit_y + by - 2 * bit_y * by)) + core
    x_dev, y_dev, xy_dev = flip(1, 0), flip(0, 1), flip(1, 1)
    inner = jnp.logical_or(z == 1, z == 2)
    z_mate = jnp.where(z == 0, 1, jnp.where(z == 1, 0, jnp.where(z == 2, 3, 2)))
    z_cross = 3 - z

    def copy(src, dst, s_sem, r_sem, dp, e):
        return pltpu.make_async_remote_copy(src_ref=src, dst_ref=dst, send_sem=s_sem, recv_sem=r_sem,
                                            device_id=(dp, e), device_id_type=MESH)

    rows_of = lambda e: pl.ds(pl.multiple_of(e * tokens, tokens), tokens)
    far = (x_dev, y_dev, xy_dev)
    for i, dev in enumerate(far):
        copy(dsend_ref.at[dev // 2], dall.at[rows_of(ep)], d_send.at[i], d_recv.at[i], z, dev).start()
    copy(dsend_ref.at[quarter], dall.at[rows_of(ep)], dp_send.at[3], dp_recv.at[3], z, partner).start()

    world = 32
    me = z * 8 + ep

    def gain_copy(d, target):
        return copy(gains_ref, gain_buf.at[d], g_send.at[d], g_recv.at[d], target // 8, lax.rem(target, 8))

    def gain_start(d, _):
        gain_copy(d, lax.rem(me + d, world)).start()
        return 0

    lax.fori_loop(1, world, gain_start, 0)

    dall[rows_of(ep), :] = dsend_ref[quarter]
    for i, dev in enumerate(far):
        copy(dsend_ref.at[dev // 2], dall.at[rows_of(dev)], d_send.at[i], d_recv.at[i], z, dev).wait_recv()
        copy(dall.at[rows_of(dev)], dall.at[rows_of(dev)], dp_send.at[i], dp_recv.at[i], z, partner).start()
    for i, dev in enumerate(far + (ep,)):
        other = dev + 1 - 2 * core
        copy(dsend_ref.at[0], dall.at[rows_of(other)], dp_send.at[i], dp_recv.at[i], z, partner).wait_recv()

    up_copy = lambda k: copy(part.at[k], z_in.at[k], z_send.at[0, k], z_recv.at[0, k], z_mate, ep)
    cross_copy = lambda k: copy(part.at[k], total.at[k], z_send.at[1, k], z_recv.at[1, k], z_cross, ep)
    down_copy = lambda k: copy(total.at[k], total.at[k], z_send.at[2, k], z_recv.at[2, k], z_mate, ep)

    def own_copy(k):
        ref = low_ref if k < STEPS // 2 else high_ref
        return pltpu.make_async_copy(total.at[k], ref.at[pl.ds(k % (STEPS // 2) * CHUNK, CHUNK), :], own_sem.at[k])

    for i in range(STEPS + 3):
        k = i
        if k < STEPS:
            cols = slice(k * CHUNK, (k + 1) * CHUNK)
            part[k, :, :split] = dot_tn(xn_ref[:, cols], dall[:, :split])
            part[k, :, split:] = dot_tn(ao_ref[:, cols], dall[:, split:])
        a = i - 1
        t = i - 2

        @pl.when(inner)
        def _():
            if 0 <= a < STEPS:
                up_copy(a).wait_recv()
                part[a] = part[a] + z_in[a]
            if 0 <= t < STEPS:
                cross_copy(t).wait_recv()
                total[t] = part[t] + total[t]
            if 0 <= a < STEPS:
                cross_copy(a).start()
            if 0 <= t < STEPS:
                down_copy(t).start()
                own_copy(t).start()

        @pl.when(jnp.logical_not(inner))
        def _():
            if k < STEPS:
                up_copy(k).start()
            if 0 <= i - 3 < STEPS:
                down_copy(i - 3).wait_recv()
                own_copy(i - 3).start()

    for k in range(STEPS):
        own_copy(k).wait()

    @pl.when(inner)
    def _():
        for k in range(STEPS):
            cross_copy(k).wait_send()
            down_copy(k).wait_send()

    @pl.when(jnp.logical_not(inner))
    def _():
        for k in range(STEPS):
            up_copy(k).wait_send()

    for i, dev in enumerate(far):
        copy(dsend_ref.at[dev // 2], dall.at[rows_of(ep)], d_send.at[i], d_recv.at[i], z, dev).wait_send()
        copy(dall.at[rows_of(dev)], dall.at[rows_of(dev)], dp_send.at[i], dp_recv.at[i], z, partner).wait_send()
    copy(dsend_ref.at[quarter], dall.at[rows_of(ep)], dp_send.at[3], dp_recv.at[3], z, partner).wait_send()

    def gain_wait(d, _):
        gain_copy(d, me).wait()
        return 0

    lax.fori_loop(1, world, gain_wait, 0)
    gain_buf[0] = gains_ref[...]

    def gain_add(s, acc):
        d = lax.rem(me - s + world, world)
        return acc + gain_buf[d]

    gains_out_ref[...] = lax.fori_loop(0, world, gain_add, jnp.zeros(gains_ref.shape, jnp.float32))


def dense_sums(xn, ao, dsend, gains):
    rows, width = xn.shape[0], dsend.shape[2]
    any_spec = pl.BlockSpec(memory_space=pl.ANY)
    vmem = pl.BlockSpec(memory_space=pltpu.VMEM)
    dma = pltpu.SemaphoreType.DMA
    half = jax.ShapeDtypeStruct((HALF // 2, width), jnp.float32)
    return pl.pallas_call(
        dense_kernel,
        out_shape=(half, half, jax.ShapeDtypeStruct(gains.shape, jnp.float32)),
        in_specs=[vmem, vmem, vmem, vmem],
        out_specs=(any_spec, any_spec, vmem),
        scratch_shapes=[
            pltpu.VMEM((rows, width), jnp.bfloat16),
            pltpu.VMEM((STEPS, CHUNK, width), jnp.float32),
            pltpu.VMEM((STEPS, CHUNK, width), jnp.float32),
            pltpu.VMEM((STEPS, CHUNK, width), jnp.float32),
            pltpu.VMEM((32,) + gains.shape, jnp.float32),
            dma((3,)), dma((3,)), dma((4,)), dma((4,)), dma((3, STEPS)), dma((3, STEPS)), dma((STEPS,)), dma((32,)), dma((32,)),
        ],
        compiler_params=pltpu.CompilerParams(has_side_effects=True, vmem_limit_bytes=48 << 20),
        cost_estimate=pl.CostEstimate(flops=100 * 10**9, bytes_accessed=40 << 20, transcendentals=0),
        name='dense_sums',
    )(xn, ao, dsend, gains)


def assemble_kernel(*refs):
    pieces, (qkv_ref, wo_ref, buf, in_sem, out_sem) = refs[:16], refs[16:]
    ep = lax.axis_index('ep')
    bits = (lax.rem(ep, 2), lax.rem(ep // 2, 2), ep // 4)
    size = HALF // 2
    width = buf.shape[2]
    split = width * 3 // 4

    def load(n):
        return pltpu.make_async_copy(pieces[n], buf.at[n % 4], in_sem.at[n % 4])

    def stores(n):
        flips = (n // 2 % 2, n // 4 % 2, n // 8)
        core, bx, by = [b + f - 2 * b * f for b, f in zip(bits, flips)]
        rows = pl.ds(pl.multiple_of(core * HALF + n % 2 * size, size), size)
        q = bx + 2 * by
        return [pltpu.make_async_copy(buf.at[n % 4, :, pl.ds(lo, cols)],
                                      ref.at[rows, pl.ds(pl.multiple_of(q * cols, 128), cols)], out_sem.at[n % 4, i])
                for i, (ref, lo, cols) in enumerate(((qkv_ref, 0, split), (wo_ref, split, width - split)))]

    for n in range(16 + 2):
        if n < 16:
            if n >= 4:
                for c in stores(n - 4):
                    c.wait()
            load(n).start()
        if n >= 2:
            load(n - 2).wait()
            for c in stores(n - 2):
                c.start()
    for n in range(12, 16):
        for c in stores(n):
            c.wait()


def assemble(pieces):
    width = pieces[0].shape[1]
    any_spec = pl.BlockSpec(memory_space=pl.ANY)
    return pl.pallas_call(
        assemble_kernel,
        out_shape=(jax.ShapeDtypeStruct((2 * HALF, 3 * width), F32), jax.ShapeDtypeStruct((2 * HALF, width), F32)),
        in_specs=[any_spec] * 16,
        out_specs=(any_spec, any_spec),
        scratch_shapes=[pltpu.VMEM((4, HALF // 2, width), F32), pltpu.SemaphoreType.DMA((4,)), pltpu.SemaphoreType.DMA((4, 2))],
        compiler_params=pltpu.CompilerParams(vmem_limit_bytes=24 << 20),
        cost_estimate=pl.CostEstimate(flops=20 * 10**9, bytes_accessed=80 << 20, transcendentals=0),
        name='assemble',
    )(*pieces)


def dot_nn(a, b):
    return lax.dot_general(a, b, (((1,), (0,)), ((), ())), preferred_element_type=jnp.float32)


def dot_nt(a, b):
    return lax.dot_general(a, b, (((1,), (1,)), ((), ())), preferred_element_type=jnp.float32)


def slot_select(codes_t, gates, first, local_exp, cap, codes_buf, gates_buf):
    tokens = codes_t.shape[1]
    codes_buf[...] = codes_t
    gates_buf[...] = gates
    my_codes = codes_buf[pl.ds(first, local_exp), :]
    my_gates = gates_buf[pl.ds(first, local_exp), :]
    slots = lax.broadcasted_iota(jnp.int32, (local_exp, cap, tokens), 1).astype(F32)
    select = jnp.where(my_codes[:, None, :] == slots, 1.0, 0.0)
    gate_slot = jnp.sum(select * my_gates[:, None, :], axis=-1, keepdims=True).reshape(local_exp * cap, 1)
    return select.reshape(local_exp * cap, tokens).astype(BF16), gate_slot


def slot_rows(xn, dyc, router, first, local_exp, cap, codes_buf, gates_buf):
    experts = router.shape[0]
    width = xn.shape[1]
    codes = dyc[:, width:].astype(F32).T[:experts]
    logits = dot_nt(router, xn)
    prob = jnp.exp(logits - jnp.max(logits, axis=0, keepdims=True))
    prob = prob / jnp.sum(prob, axis=0, keepdims=True)
    picked = jnp.where(codes < UNCHOSEN - 1.0, prob, 0.0)
    gates = picked / jnp.sum(picked, axis=0, keepdims=True)
    select, gate_slot = slot_select(codes, gates, first, local_exp, cap, codes_buf, gates_buf)
    return dot_nn(select, xn).astype(BF16), dot_nn(select, dyc[:, :width]), gate_slot


def dispatch_kernel(local_exp, cap, place_ref, xn_ref, dyc_ref, router_ref, recv_in, d_recv_in, recv_ref, d_recv_ref, codes_buf, gates_buf):
    first = pl.multiple_of(lax.axis_index('ep') * local_exp, local_exp)
    router = router_ref[...]
    width = xn_ref.shape[2]
    for i in range(xn_ref.shape[0]):
        recv, dy_rows, gate_slot = slot_rows(xn_ref[i], dyc_ref[i], router, first, local_exp, cap, codes_buf.at[i], gates_buf.at[i])
        at = slice(i * cap, (i + 1) * cap)
        recv_ref[:, at, :] = recv.reshape(local_exp, cap, width)
        d_recv_ref[:, at, :] = (gate_slot * dy_rows).astype(BF16).reshape(local_exp, cap, width)


def dispatch_rows(place, xn, dyc, router_t, recv, d_recv, cap):
    planes, sources, tokens, lanes = dyc.shape
    local_exp, _, width = recv.shape
    experts = router_t.shape[0]
    step = 4
    any_spec = pl.BlockSpec(memory_space=pl.ANY)
    plane = lambda r, t: lax.rem(t[0] + r + 1, planes)
    out_spec = pl.BlockSpec((local_exp, step * cap, width), lambda r, s, t: (0, (r + 1) * (sources // step) + s, 0))
    same = lambda arr: jax.ShapeDtypeStruct(arr.shape, arr.dtype)
    return pl.pallas_call(
        functools.partial(dispatch_kernel, local_exp, cap),
        grid_spec=pltpu.PrefetchScalarGridSpec(
            num_scalar_prefetch=1,
            grid=(planes - 1, sources // step),
            in_specs=[pl.BlockSpec((None, step, tokens, width), lambda r, s, t: (plane(r, t), s, 0, 0)),
                      pl.BlockSpec((None, step, tokens, lanes), lambda r, s, t: (plane(r, t), s, 0, 0)),
                      pl.BlockSpec(router_t.shape, lambda r, s, t: (0, 0)), any_spec, any_spec],
            out_specs=(out_spec, out_spec),
            scratch_shapes=[pltpu.VMEM((step, experts, tokens), F32), pltpu.VMEM((step, experts, tokens), F32)]),
        out_shape=(same(recv), same(d_recv)),
        input_output_aliases={4: 0, 5: 1},
        compiler_params=pltpu.CompilerParams(vmem_limit_bytes=56 << 20),
        cost_estimate=pl.CostEstimate(flops=planes * sources * 4 * local_exp * cap * tokens * width, transcendentals=0,
                                      bytes_accessed=planes * sources * tokens * width * 8),
        name='dispatch_rows',
    )(place, xn, dyc, router_t, recv, d_recv)


def hidden_grads(recv, d_recv, up, lin, down):
    u = dot_nn(recv, up).astype(BF16).astype(F32)
    v = dot_nn(recv, lin).astype(BF16).astype(F32)
    d_act = dot_nt(d_recv, down).astype(BF16).astype(F32)
    sig = jax.nn.sigmoid(u)
    act = u * sig
    d_u = d_act * v * (sig + act * (1.0 - sig))
    return (act * v).astype(BF16), d_u.astype(BF16), (d_act * act).astype(BF16)


def moe_kernel(cap, xn_ref, dyc_ref, router_ref, up_ref, lin_ref, down_ref, back_ref, gate_back_ref, recv_out, d_recv_out,
               xn_all, recv, d_recv, dy_rows, d_tok, gate_send, up_buf, lin_buf, down_buf, codes_buf, gates_buf,
               w_sem, x_send, x_recv, p_send, p_recv, own_sem, row_sem, b_send, b_recv, g_send, g_recv):
    z = lax.axis_index('dp')
    ep = lax.axis_index('ep')
    local_exp = up_ref.shape[0]
    plane = xn_all.shape[0]
    width = xn_ref.shape[1]
    first = pl.multiple_of(ep * local_exp, local_exp)
    bits = (lax.rem(ep, 2), lax.rem(ep // 2, 2), ep // 4)

    def flipped(d):
        flags = (lax.rem(d, 2), lax.rem(d // 2, 2), d // 4)
        both = [b + f - 2 * b * f for b, f in zip(bits, flags)]
        return both[0] + 2 * both[1] + 4 * both[2]

    def copy(src, dst, s_sem, r_sem, dev):
        return pltpu.make_async_remote_copy(src_ref=src, dst_ref=dst, send_sem=s_sem, recv_sem=r_sem,
                                            device_id=(z, dev), device_id_type=MESH)

    def weights(e, slot):
        return [pltpu.make_async_copy(src.at[e], dst.at[slot], w_sem.at[i, slot])
                for i, (src, dst) in enumerate(((up_ref, up_buf), (lin_ref, lin_buf), (down_ref, down_buf)))]

    for i in (1, 2, 3):
        copy(xn_ref, xn_all.at[ep], x_send.at[i], x_recv.at[i], flipped(2 * i)).start()
    copy(xn_ref, xn_all.at[ep], p_send.at[0], p_recv.at[0], flipped(1)).start()
    for c in weights(0, 0):
        c.start()
    xn_all[ep] = xn_ref[...]
    router = router_ref[...]

    def pair(i, _):
        near = flipped(2 * i)
        other = flipped(2 * i + 1)

        @pl.when(i > 0)
        def _():
            copy(xn_ref, xn_all.at[near], x_send.at[i], x_recv.at[i], near).wait_recv()
            copy(xn_all.at[near], xn_all.at[near], p_send.at[i], p_recv.at[i], flipped(1)).start()

        copy(xn_ref, xn_all.at[other], p_send.at[i], p_recv.at[i], flipped(1)).wait_recv()
        for j, src in enumerate((near, other)):
            rows, dy, gate_slot = slot_rows(xn_all[src], dyc_ref[src], router, first, local_exp, cap, codes_buf.at[j], gates_buf.at[j])
            at = pl.ds(pl.multiple_of(src * cap, cap), cap)
            recv[:, at, :] = rows.reshape(local_exp, cap, width)
            dy_rows[:, at, :] = dy.astype(BF16).reshape(local_exp, cap, width)
            d_recv[:, at, :] = (gate_slot * dy).astype(BF16).reshape(local_exp, cap, width)
        return 0

    lax.fori_loop(0, plane // 2, pair, 0)

    keep = [pltpu.make_async_copy(src, dst.at[:, pl.ds(0, plane * cap), :], row_sem.at[i])
            for i, (src, dst) in enumerate(((recv, recv_out), (d_recv, d_recv_out)))]
    for c in keep:
        c.start()

    def home(d, e):
        dev = flipped(d)
        src = d_tok.at[e, pl.ds(pl.multiple_of(dev * cap, cap), cap), :]
        return copy(src, back_ref.at[first + e], b_send.at[d, e], b_recv.at[d, e], dev)

    def stay(e):
        return pltpu.make_async_copy(d_tok.at[e, pl.ds(pl.multiple_of(ep * cap, cap), cap), :], back_ref.at[first + e], own_sem.at[e])

    def expert(e, _):
        slot = lax.rem(e, 2)

        @pl.when(e + 1 < local_exp)
        def _():
            for c in weights(e + 1, 1 - slot):
                c.start()

        for c in weights(e, slot):
            c.wait()
        up, lin, down = up_buf[slot], lin_buf[slot], down_buf[slot]
        act, d_u, d_v = hidden_grads(recv[e], d_recv[e], up, lin, down)
        d_tok[e] = (dot_nt(d_u, up) + dot_nt(d_v, lin)).astype(BF16)
        y = dot_nn(act, down).astype(BF16).astype(F32)
        d_gate = jnp.sum(dy_rows[e].astype(F32) * y, axis=-1, keepdims=True)
        lane = lax.broadcasted_iota(jnp.int32, (plane, cap, 128), 2)
        row = lax.broadcasted_iota(jnp.int32, (plane, cap, 128), 1)
        wide = jnp.broadcast_to(d_gate, (plane * cap, 128)).reshape(plane, cap, 128)
        gate_send[:, pl.ds(e, 1), :] = jnp.sum(jnp.where(lane == row, wide, 0.0), axis=1, keepdims=True)
        for d in (6, 7, 2, 3, 4, 5, 1):
            home(d, e).start()
        stay(e).start()
        return 0

    lax.fori_loop(0, local_exp, expert, 0)

    for c in keep:
        c.wait()

    def gate_home(d):
        dev = flipped(d)
        return copy(gate_send.at[dev], gate_back_ref.at[ep], g_send.at[d], g_recv.at[d], dev)

    for d in range(1, plane):
        gate_home(d).start()
    gate_back_ref[ep] = gate_send[ep]

    def drain(e, _):
        for d in range(1, plane):
            src = d_tok.at[0, pl.ds(0, cap), :]
            copy(src, back_ref.at[flipped(d) * local_exp + e], b_send.at[d, e], b_recv.at[d, e], flipped(d)).wait_recv()
            home(d, e).wait_send()
        stay(e).wait()
        return 0

    lax.fori_loop(0, local_exp, drain, 0)
    for d in range(1, plane):
        copy(gate_send.at[0], gate_back_ref.at[flipped(d)], g_send.at[d], g_recv.at[d], flipped(d)).wait_recv()
        gate_home(d).wait_send()
    for i in (1, 2, 3):
        copy(xn_ref, xn_all.at[ep], x_send.at[i], x_recv.at[i], flipped(2 * i)).wait_send()
        copy(xn_all.at[flipped(2 * i)], xn_all.at[flipped(2 * i)], p_send.at[i], p_recv.at[i], flipped(1)).wait_send()
    copy(xn_ref, xn_all.at[ep], p_send.at[0], p_recv.at[0], flipped(1)).wait_send()


def moe_backward(xn, dyc_plane, router_t, w_up, w_lin, w_down, cap, planes):
    plane, tokens = dyc_plane.shape[:2]
    local_exp, width, hid = w_up.shape
    experts = router_t.shape[0]
    rows = pltpu.VMEM((local_exp, plane * cap, width), BF16)
    vmem = pl.BlockSpec(memory_space=pltpu.VMEM)
    any_spec = pl.BlockSpec(memory_space=pl.ANY)
    dma = pltpu.SemaphoreType.DMA
    return pl.pallas_call(
        functools.partial(moe_kernel, cap),
        out_shape=(jax.ShapeDtypeStruct((experts, cap, width), BF16), jax.ShapeDtypeStruct((plane, local_exp, 128), F32),
                   jax.ShapeDtypeStruct((local_exp, planes * plane * cap, width), BF16),
                   jax.ShapeDtypeStruct((local_exp, planes * plane * cap, width), BF16)),
        in_specs=[vmem, vmem, vmem, any_spec, any_spec, any_spec],
        out_specs=(any_spec, vmem, any_spec, any_spec),
        scratch_shapes=[
            pltpu.VMEM((plane, tokens, width), BF16), rows, rows, rows, rows, pltpu.VMEM((plane, local_exp, 128), F32),
            pltpu.VMEM((2, width, hid), BF16), pltpu.VMEM((2, width, hid), BF16), pltpu.VMEM((2, hid, width), BF16),
            pltpu.VMEM((2, experts, tokens), F32), pltpu.VMEM((2, experts, tokens), F32),
            dma((3, 2)), dma((4,)), dma((4,)), dma((4,)), dma((4,)), dma((local_exp,)), dma((2,)),
            dma((plane, local_exp)), dma((plane, local_exp)), dma((plane,)), dma((plane,)),
        ],
        compiler_params=pltpu.CompilerParams(has_side_effects=True, vmem_limit_bytes=60 << 20),
        cost_estimate=pl.CostEstimate(flops=60 * 10**9, bytes_accessed=64 << 20, transcendentals=0),
        name='moe_backward',
    )(xn, dyc_plane, router_t, w_up, w_lin, w_down)


def weight_kernel(recv_ref, d_recv_ref, up_ref, lin_ref, down_ref, *rest):
    g_up_ref, g_lin_ref, g_down_ref, act_buf, du_buf, dv_buf = rest[-6:]
    total = recv_ref.shape[1]
    block = 256

    @pl.loop(0, total // block)
    def _(i):
        rows = pl.ds(pl.multiple_of(i * block, block), block)
        act, d_u, d_v = hidden_grads(recv_ref[0, rows, :], d_recv_ref[0, rows, :], up_ref[0], lin_ref[0], down_ref[0])
        act_buf[rows, :] = act
        du_buf[rows, :] = d_u
        dv_buf[rows, :] = d_v

    width = recv_ref.shape[2]
    cols = 512

    @pl.loop(0, width // cols)
    def _(i):
        c = pl.ds(pl.multiple_of(i * cols, cols), cols)
        g_up_ref[0, c, :] = dot_tn(recv_ref[0, :, c], du_buf[...])
        g_lin_ref[0, c, :] = dot_tn(recv_ref[0, :, c], dv_buf[...])
        g_down_ref[0, :, c] = dot_tn(act_buf[...], d_recv_ref[0, :, c])


def weight_grads(recv, d_recv, w_up, w_lin, w_down, first, count, grads=()):
    _, total, width = recv.shape
    hid = w_up.shape[2]
    rows = pl.BlockSpec((1, total, width), lambda e: (first + e, 0, 0))
    wide = pl.BlockSpec((1, width, hid), lambda e: (first + e, 0, 0))
    tall = pl.BlockSpec((1, hid, width), lambda e: (first + e, 0, 0))
    f32 = lambda arr: jax.ShapeDtypeStruct(arr.shape, F32)
    return pl.pallas_call(
        weight_kernel,
        grid=(count,),
        out_shape=(f32(w_up), f32(w_lin), f32(w_down)),
        in_specs=[rows, rows, wide, wide, tall] + [pl.BlockSpec(memory_space=pl.ANY)] * len(grads),
        out_specs=(wide, wide, tall),
        scratch_shapes=[pltpu.VMEM((total, hid), BF16)] * 3,
        input_output_aliases={5 + i: i for i in range(len(grads))},
        compiler_params=pltpu.CompilerParams(vmem_limit_bytes=60 << 20),
        cost_estimate=pl.CostEstimate(flops=12 * count * total * width * hid, transcendentals=0, bytes_accessed=count * (20 << 20)),
        name='weight_grads',
    )(recv, d_recv, w_up, w_lin, w_down, *grads)


def solution(mesh):
    tok_spec = P(('dp', 'ep'))
    exp_spec = P('ep')
    rep_spec = P()
    world = ('dp', 'ep')

    def local(x_in, dy_in, route_idx, gain_attn, w_qkv, w_o, gain_ffn, w_router, w_up, w_lin, w_down):
        num_seqs, seq_len, width = x_in.shape
        tokens = num_seqs * seq_len
        top = route_idx.shape[-1]
        experts = w_router.shape[1]
        local_exp = w_up.shape[0]
        cap = ((tokens * top * 5) // (experts * 4) + 7) // 8 * 8
        ep_size = mesh.shape['ep']

        codes = slot_codes(route_idx.reshape(tokens, top), experts, cap)
        dy_own = dy_in.reshape(tokens, width)
        lanes = jnp.zeros((tokens, HEAD - experts), BF16)
        dyc_own = jnp.concatenate([dy_own, codes.T, lanes], axis=1)
        dyc_plane = lax.all_gather(dyc_own, 'ep')
        dyc_all = lax.all_gather(dyc_own, world)
        router_t = w_router.T
        planes = mesh.shape['dp']
        my_z = lax.axis_index('dp')

        def spread(act):
            halves = jnp.moveaxis(act.reshape(tokens, 2, width // 2), 1, 0)
            send = jnp.broadcast_to(halves[None], (ep_size // 2, 2, tokens, width // 2)).reshape(ep_size, tokens, width // 2)
            return lax.all_to_all(send, 'ep', 0, 0).reshape(ep_size * tokens, width // 2)

        x_f = x_in.astype(F32)
        xn_one, norm_one_pull = jax.vjp(rms_norm, x_f, gain_attn.astype(F32))
        acts_xn = spread(xn_one)
        qkv_all = mm('bsd,de->bse', xn_one, w_qkv).astype(BF16)
        attn_out, attn_pull = jax.vjp(attn_core, qkv_all)
        attn_proj = mm('bsd,de->bse', attn_out, w_o)
        hidden = (x_f + attn_proj).astype(BF16).astype(F32).reshape(tokens, width)
        xn_two, norm_two_pull = jax.vjp(rms_norm, hidden, gain_ffn.astype(F32))

        xn_all = lax.all_gather(xn_two, world)
        d_back, gate_back, recv, d_recv = moe_backward(after(xn_two, acts_xn), dyc_plane, router_t, w_up, w_lin, w_down, cap, planes)
        acts_ao = spread(after(attn_out, gate_back))
        d_gate_back = gate_back[:, :, :cap].reshape(experts, cap)

        select_own = one_hot(codes, cap)
        d_moe_in = mm('ect,ecd->td', select_own, d_back)
        prob, mask, gates, total = gates_of(xn_two, codes, w_router)
        d_gates = jnp.sum(select_own.astype(F32) * d_gate_back[:, :, None], axis=1)
        d_picked = (d_gates - jnp.sum(d_gates * gates, axis=0, keepdims=True)) / total * mask
        d_logits = (prob * (d_picked - jnp.sum(prob * d_picked, axis=0, keepdims=True))).astype(BF16)
        d_xn_two = (d_moe_in + mm('et,de->td', d_logits, w_router)).astype(BF16)
        d_logits_all = lax.all_gather(d_logits.T, world)
        d_hidden, grad_gain_ffn = norm_two_pull(d_xn_two)
        d_resid = (d_hidden + dy_own.astype(F32)).astype(BF16).reshape(num_seqs, seq_len, width)
        d_attn_out = mm('bse,de->bsd', d_resid, w_o).astype(BF16)
        d_qkv = attn_pull(d_attn_out)[0]
        d_xn_one = mm('bse,de->bsd', d_qkv, w_qkv).astype(BF16)
        d_x_norm, grad_gain_attn = norm_one_pull(d_xn_one)
        dx_out = (d_x_norm + d_resid.astype(F32)).astype(BF16)
        quarters = lambda arr: jnp.moveaxis(arr.reshape(tokens, 4, -1), 1, 0)
        dsend = jnp.concatenate([quarters(d_qkv), quarters(d_resid)], axis=2)
        gains = jnp.concatenate([grad_gain_attn, grad_gain_ffn]).reshape(-1, 128)
        low, high, gains = dense_sums(acts_xn, acts_ao, dsend, gains)
        grad_gain_attn, grad_gain_ffn = gains.reshape(2, width)

        flip = lambda arr, bit: lax.ppermute(arr, 'ep', [(e, e ^ bit) for e in range(ep_size)])
        low_x, high_y = flip(low, 2), flip(high, 4)
        low_y, high_x = flip(low, 4), flip(high, 2)
        low_xy, high_xy = flip(low_x, 4), flip(high_y, 2)
        pieces = [low, high, low_x, high_x, low_y, high_y, low_xy, high_xy]
        swapped = [flip(arr, 1) for arr in pieces[:6]]
        swapped += [flip(arr, 1) for arr in pieces[6:]]
        pieces = [arr for i in range(4) for arr in (pieces[2 * i], pieces[2 * i + 1], swapped[2 * i], swapped[2 * i + 1])]

        xn_late, dyc_late, d_logits_late = lax.optimization_barrier((xn_all, dyc_all, d_logits_all, gains))[:3]
        grad_router = mm('ntd,nte->de', xn_late, d_logits_late)
        xn_late = xn_late.reshape(planes, ep_size, tokens, width)
        dyc_late = dyc_late.reshape(planes, ep_size, tokens, -1)
        recv, d_recv = dispatch_rows(my_z.reshape(1), xn_late, dyc_late, router_t, recv, d_recv, cap)
        grads = weight_grads(recv, d_recv, w_up, w_lin, w_down, 0, local_exp // 2)
        grad_up, grad_lin, grad_down = weight_grads(recv, d_recv, w_up, w_lin, w_down, local_exp // 2, local_exp // 2, grads)
        grad_wqkv, grad_wo = assemble(pieces)
        return (dx_out, grad_gain_attn, grad_wqkv, grad_wo, grad_gain_ffn, grad_router, grad_up, grad_lin, grad_down)

    in_specs = (tok_spec, tok_spec, tok_spec, rep_spec, rep_spec, rep_spec, rep_spec, rep_spec, exp_spec, exp_spec, exp_spec)
    out_specs = (tok_spec, rep_spec, rep_spec, rep_spec, rep_spec, rep_spec, exp_spec, exp_spec, exp_spec)

    return jax.shard_map(local, mesh=mesh, in_specs=in_specs, out_specs=out_specs, check_vma=False)
```

profile of v0, /device:TPU:0, one launch (start us, length us, event | category | flops | bytes accessed | tf_op | source)
XLA Modules:
  0.0 1052.4 jit_solution(3763604834891736617)
XLA Ops:
  9.2 2.0 concatenate.14
  12.1 1.9 broadcast_in_dim.80
  14.0 5.2 all-to-all-start
  19.2 11.0 %convolution_convert_fusion = bf16[256,4608]{1,0:T(8,128)(2,1)} fusion(bf16[1536,4608]{1,0:T(8,128)(2,1)} %param.15, bf16[1,256,1536]{2,1,0:T(8,128)(2,1)S(1)} %fusion.21), kind=kOutput, calls=%fused_computation.1 | convolution fusion | flops 3625058304 | bytes 17301504 | tf_op jit(solution)/shard_map/bsd,de->bse/dot_general | solution.py:20
  30.2 2.8 copy.106
  47.0 19.2 %all-to-all-done = bf16[8,256,768]{2,1,0:T(8,128)(2,1)} async-done(((bf16[8,256,768]{2,1,0:T(8,128)(2,1)}), bf16[8,256,768]{2,1,0:T(8,128)(2,1)}, u32[]{:S(2)}, u32[]{:S(2)}) %all-to-all-start) | async-done | bytes 3145760 | tf_op jit(solution)/shard_map/all_to_all | solution.py:578
  66.2 20.1 %all-gather.10.cloned.1.call-done = bf16[2048,1664]{1,0:T(8,128)(2,1)} async-done(((bf16[256,1664]{1,0:T(8,128)(2,1)}), bf16[2048,1664]{1,0:T(8,128)(2,1)}) %all-gather.10.cloned.1.call-update) | async-done | bytes 6815760 | tf_op jit(solution)/shard_map/all_gather | solution.py:569
  86.3 124.7 %moe_backward.1 = (bf16[64,32,1536]{2,1,0:T(8,128)(2,1)}, f32[8,8,128]{2,1,0:T(8,128)}, bf16[8,1024,1536]{2,1,0:T(8,128)(2,1)}, bf16[8,1024,1536]{2,1,0:T(8,128)(2,1)}) custom-call(bf16[256,1536]{1,0:T(8,128)(2,1)} %copy-done.21, bf16[8,256,1664]{2,1,0:T(8,128)(2,1)} %bitcast.192, bf16[64,1536]{1,0:T(8,128)(2,1)} %bitcast.187, bf16[8,1536,512]{2,1,0:T(8,128)(2,1)} %up_ref.5, ...), custom_call_target="tpu_custom_call" | custom-call | flops 60000002048 | bytes 67108864 | tf_op jit(solution)/shard_map/moe_backward/pallas_call | solution.py:485
  219.9 10.2 fusion.9
  232.7 3.8 convolution_convert_fusion.2
  236.7 4.0 fusion.8
  241.9 3.0 broadcast_in_dim.92
  244.9 15.7 %all-to-all-start.1 = ((bf16[8,256,768]{2,1,0:T(8,128)(2,1)}), bf16[8,256,768]{2,1,0:T(8,128)(2,1)}, u32[]{:S(2)}, u32[]{:S(2)}) async-start(bf16[8,256,768]{2,1,0:T(8,128)(2,1)} %bitcast.175), calls=%async_computation.1 | async-start | bytes 6291456 | tf_op jit(solution)/shard_map/all_to_all | solution.py:578
  260.7 4.5 fusion.36
  268.2 2.7 fusion.35
  272.5 3.1 copy.125
  275.6 2.3 copy.127
  277.9 10.9 %fusion.22 = (f32[1536]{0:T(1024)S(1)}, f32[256]{0:T(256)S(1)}, f32[256,1536]{1,0:T(8,128)}) fusion(bf16[1,256,1536]{2,1,0:T(8,128)(2,1)S(1)} %copy-done.15, f32[256]{0:T(256)S(1)} %copy-done.47, f32[1536]{0:T(1024)S(1)} %convert_element_type.151, bf16[256,4608]{0,1:T(8,128)(2,1)} %bitcast.180, bf16[1536,4608]{1,0:T(8,128)(2,1)} %param.15), kind=kOutput, calls=%fused_computation.43 | convolution fusion | flops 3627415808 | bytes 18888704 | tf_op jit(solution)/shard_map/bse,de->bsd/dot_general | solution.py:20
  288.9 2.0 pad_maximum_fusion.dsend_ref
  290.8 9.6 all-to-all-done.1
  300.5 347.8 %dense_sums.1 = (f32[384,1536]{1,0:T(8,128)S(1)}, f32[384,1536]{1,0:T(8,128)S(1)}, f32[24,128]{1,0:T(8,128)S(1)}) custom-call(bf16[2048,768]{1,0:T(8,128)(2,1)} %bitcast.12.xn_ref, bf16[2048,768]{1,0:T(8,128)(2,1)} %bitcast.44.ao_ref, bf16[4,256,1536]{2,1,0:T(8,128)(2,1)} %pad_maximum_fusion.dsend_ref, f32[24,128]{1,0:T(8,128)S(1)} %pad_maximum_fusion.1.gains_ref), custom_call_target="tpu_custom_call" | custom-call | flops 99999997952 | bytes 41943040 | tf_op jit(solution)/shard_map/dense_sums/pallas_call | solution.py:206
  648.3 1.8 collective-permute-start.2
  652.4 98.1 %collective-permute-done.2.refs_4_ = f32[384,1536]{1,0:T(8,128)S(1)} collective-permute-done((f32[384,1536]{1,0:T(8,128)S(1)}, f32[384,1536]{1,0:T(8,128)S(1)}, u32[]{:S(2)}, u32[]{:S(2)}) %collective-permute-start.2) | collective-permute-done | bytes 2359328 | tf_op jit(solution)/shard_map/ppermute | solution.py:615
  753.4 46.9 %collective-permute-done.3.refs_5_ = f32[384,1536]{1,0:T(8,128)} collective-permute-done((f32[384,1536]{1,0:T(8,128)S(1)}, f32[384,1536]{1,0:T(8,128)}, u32[]{:S(2)}, u32[]{:S(2)}) %collective-permute-start.3) | collective-permute-done | bytes 2359328 | tf_op jit(solution)/shard_map/ppermute | solution.py:615
  806.4 45.2 %collective-permute-done.10.refs_12_ = f32[384,1536]{1,0:T(8,128)} collective-permute-done((f32[384,1536]{1,0:T(8,128)S(1)}, f32[384,1536]{1,0:T(8,128)}, u32[]{:S(2)}, u32[]{:S(2)}) %collective-permute-start.10) | collective-permute-done | bytes 2359328 | tf_op jit(solution)/shard_map/ppermute | solution.py:615
  854.9 3.2 fusion.26
  859.8 3.4 collective-permute-done.13.refs_15_
  869.8 21.8 %assemble.1 = (f32[1536,4608]{1,0:T(8,128)}, f32[1536,1536]{1,0:T(8,128)}) custom-call(f32[384,1536]{1,0:T(8,128)S(1)} %get-tuple-element.36.refs_0_, f32[384,1536]{1,0:T(8,128)S(1)} %copy-done.1, f32[384,1536]{1,0:T(8,128)S(1)} %copy-done.5, f32[384,1536]{1,0:T(8,128)S(1)} %copy-done.7, f32[384,1536]{1,0:T(8,128)S(1)} %copy-done.3, ...), custom_call_target="tpu_custom_call" | custom-call | flops 20000000000 | bytes 83886080 | tf_op jit(solution)/shard_map/assemble/pallas_call | solution.py:263
  891.7 14.0 %convolution_bitcast_fusion.1 = f32[1536,64]{0,1:T(8,128)} fusion(bf16[32,256,1536]{2,1,0:T(8,128)(2,1)} %all-gather.8.cloned.1.call-done, bf16[32,256,64]{2,1,0:T(8,128)(2,1)} %bitcast.193), kind=kOutput, calls=%fused_computation.37 | convolution fusion | flops 1610612736 | bytes 26607616 | tf_op jit(solution)/shard_map/ntd,nte->de/dot_general | solution.py:20
  905.8 31.8 %dispatch_rows.1 = (bf16[8,1024,1536]{2,1,0:T(8,128)(2,1)}, bf16[8,1024,1536]{2,1,0:T(8,128)(2,1)}) custom-call(s32[1]{0:T(128)} %bitcast.58.place_ref, bf16[4,8,256,1536]{3,2,1,0:T(8,128)(2,1)} %bitcast.167, bf16[4,8,256,1664]{3,2,1,0:T(8,128)(2,1)} %bitcast.166, bf16[64,1536]{1,0:T(8,128)(2,1)} %bitcast.188, ...), custom_call_target="tpu_custom_call", output_to_operand_aliasing={{0}: (4, {}), {1}: (5, {})} | custom-call | flops 12884901888 | bytes 100663296 | tf_op jit(solution)/shard_map/dispatch_rows/pallas_call | solution.py:328
  937.5 54.0 %weight_grads.2 = (f32[8,1536,512]{2,1,0:T(8,128)}, f32[8,1536,512]{2,1,0:T(8,128)}, f32[8,512,1536]{2,1,0:T(8,128)}) custom-call(bf16[8,1024,1536]{2,1,0:T(8,128)(2,1)} %get-tuple-element.45.recv_ref, bf16[8,1024,1536]{2,1,0:T(8,128)(2,1)} %get-tuple-element.46.d_recv_ref, bf16[8,1536,512]{2,1,0:T(8,128)(2,1)} %up_ref.5, bf16[8,1536,512]{2,1,0:T(8,128)(2,1)} %lin_ref.5, ...), custom_call_target="tpu_custom_call" | custom-call | flops 38654705664 | bytes 83886080 | tf_op jit(solution)/shard_map/weight_grads/pallas_call | solution.py:536
  991.5 54.0 %weight_grads.3 = (f32[8,1536,512]{2,1,0:T(8,128)}, f32[8,1536,512]{2,1,0:T(8,128)}, f32[8,512,1536]{2,1,0:T(8,128)}) custom-call(bf16[8,1024,1536]{2,1,0:T(8,128)(2,1)} %get-tuple-element.45.recv_ref, bf16[8,1024,1536]{2,1,0:T(8,128)(2,1)} %get-tuple-element.46.d_recv_ref, ...), custom_call_target="tpu_custom_call", output_to_operand_aliasing={{0}: (5, {}), {1}: (6, {}), {2}: (7, {})} | custom-call | flops 38654705664 | bytes 83886080 | tf_op jit(solution)/shard_map/weight_grads/pallas_call | solution.py:536
  (188 shorter events, 57.0 us)
Async XLA Ops:
  7.2 79.1 %all-gather.10.cloned.1.call-start = ((), (), s32[]{:S(2)}) async-start(), calls=%async_computation.3 | async-start | bytes 7667712 | tf_op jit(solution)/shard_map/all_gather | solution.py:569
  14.0 52.2 %all-to-all-start = ((bf16[8,256,768]{2,1,0:T(8,128)(2,1)}), bf16[8,256,768]{2,1,0:T(8,128)(2,1)}, u32[]{:S(2)}, u32[]{:S(2)}) async-start(bf16[8,256,768]{2,1,0:T(8,128)(2,1)} %bitcast.11), calls=%async_computation | async-start | bytes 6291456 | tf_op jit(solution)/shard_map/all_to_all | solution.py:578
  19.2 872.5 %all-gather.14.cloned.1.call-start = ((), (), s32[]{:S(2)}) async-start(), calls=%async_computation.5 | async-start | bytes 2162688 | tf_op jit(solution)/shard_map/all_gather | solution.py:601
  44.6 166.4 %copy-start.32 = (f32[256]{0:T(256)}, f32[256]{0:T(256)S(1)}, u32[]{:S(2)}) copy-start(f32[256]{0:T(256)S(1)} %fusion.53) | copy-start | bytes 3076
  47.0 164.8 %copy-start.50 = (f32[32]{0:T(128)}, f32[32]{0:T(128)S(1)}, u32[]{:S(2)}) copy-start(f32[32]{0:T(128)S(1)} %iota_convert_fusion) | copy-start | bytes 388
  86.3 125.6 %copy-start.26 = (f32[64,256]{1,0:T(8,128)S(1)}, f32[64,256]{1,0:T(8,128)}, u32[]{:S(2)}) copy-start(f32[64,256]{1,0:T(8,128)} %copy.105) | copy-start | bytes 196612
  217.4 674.3 %all-gather.8.cloned.1.call-start = ((), (), s32[]{:S(2)}) async-start(), calls=%async_computation.2 | async-start | bytes 25952256 | tf_op jit(solution)/shard_map/all_gather | solution.py:589
  219.2 672.5 %all-gather.12.cloned.1.call-start = ((), (), s32[]{:S(2)}) async-start(), calls=%async_computation.4 | async-start | bytes 28114944 | tf_op jit(solution)/shard_map/all_gather | solution.py:570
  219.8 10.3 copy-start.24
  219.8 10.3 copy-start.31
  219.8 10.3 copy-start.33
  219.8 10.3 copy-start.35
  219.9 10.2 copy-start.37
  219.9 10.2 copy-start.39
  244.9 15.7 %copy-start.30 = (pred[256,256]{0,1:T(8,128)(4,1)S(1)}, pred[256,256]{0,1:T(8,128)(4,1)}, u32[]{:S(2)}) copy-start(pred[256,256]{0,1:T(8,128)(4,1)} %copy-done.29) | copy-start | bytes 196612
  244.9 55.6 %all-to-all-start.1 = ((bf16[8,256,768]{2,1,0:T(8,128)(2,1)}), bf16[8,256,768]{2,1,0:T(8,128)(2,1)}, u32[]{:S(2)}, u32[]{:S(2)}) async-start(bf16[8,256,768]{2,1,0:T(8,128)(2,1)} %bitcast.175), calls=%async_computation.1 | async-start | bytes 6291456 | tf_op jit(solution)/shard_map/all_to_all | solution.py:578
  277.9 10.9 %copy-start.20 = (bf16[256,4,384]{2,0,1:T(8,128)(2,1)S(1)}, bf16[256,4,384]{2,0,1:T(8,128)(2,1)}, u32[]{:S(2)}) copy-start(bf16[256,4,384]{2,0,1:T(8,128)(2,1)} %copy.127) | copy-start | bytes 2359300
  300.5 554.4 %copy-start.43 = (f32[256]{0:T(256)S(1)}, f32[256]{0:T(256)}, u32[]{:S(2)}) copy-start(f32[256]{0:T(256)} %copy-done.42) | copy-start | bytes 3076
  648.3 102.2 %collective-permute-start.2 = (f32[384,1536]{1,0:T(8,128)S(1)}, f32[384,1536]{1,0:T(8,128)S(1)}, u32[]{:S(2)}, u32[]{:S(2)}) collective-permute-start(f32[384,1536]{1,0:T(8,128)S(1)} %get-tuple-element.36.refs_0_), channel_id=1, source_target_pairs={{0,2},{1,3},{2,0},{3,1},{4,6},{5,7},{6,4},{7,5},{8,10},{9,11},{10,... | collective-permute-start | bytes 7077896 | tf_op jit(solution)/shard_map/ppermute | solution.py:615
  650.1 101.8 %collective-permute-start.7 = (f32[384,1536]{1,0:T(8,128)S(1)}, f32[384,1536]{1,0:T(8,128)}, u32[]{:S(2)}, u32[]{:S(2)}) collective-permute-start(f32[384,1536]{1,0:T(8,128)S(1)} %get-tuple-element.37.refs_1_), channel_id=1, source_target_pairs={{0,4},{1,5},{2,6},{3,7},{4,0},{5,1},{6,2},{7,3},{8,12},{9,13},{10,... | collective-permute-start | bytes 7077896 | tf_op jit(solution)/shard_map/ppermute | solution.py:615
  650.9 149.4 %collective-permute-start.3 = (f32[384,1536]{1,0:T(8,128)S(1)}, f32[384,1536]{1,0:T(8,128)}, u32[]{:S(2)}, u32[]{:S(2)}) collective-permute-start(f32[384,1536]{1,0:T(8,128)S(1)} %get-tuple-element.37.refs_1_), channel_id=1, source_target_pairs={{0,2},{1,3},{2,0},{3,1},{4,6},{5,7},{6,4},{7,5},{8,10},{9,11},{10,... | collective-permute-start | bytes 7077896 | tf_op jit(solution)/shard_map/ppermute | solution.py:615
  651.9 149.8 %collective-permute-start.6 = (f32[384,1536]{1,0:T(8,128)S(1)}, f32[384,1536]{1,0:T(8,128)}, u32[]{:S(2)}, u32[]{:S(2)}) collective-permute-start(f32[384,1536]{1,0:T(8,128)S(1)} %get-tuple-element.36.refs_0_), channel_id=1, source_target_pairs={{0,4},{1,5},{2,6},{3,7},{4,0},{5,1},{6,2},{7,3},{8,12},{9,13},{10,... | collective-permute-start | bytes 7077896 | tf_op jit(solution)/shard_map/ppermute | solution.py:615
  652.4 150.6 %collective-permute-start = (f32[384,1536]{1,0:T(8,128)S(1)}, f32[384,1536]{1,0:T(8,128)S(1)}, u32[]{:S(2)}, u32[]{:S(2)}) collective-permute-start(f32[384,1536]{1,0:T(8,128)S(1)} %get-tuple-element.36.refs_0_), channel_id=1, source_target_pairs={{0,1},{1,0},{2,3},{3,2},{4,5},{5,4},{6,7},{7,6},{8,9},{9,8},{10,11... | collective-permute-start | bytes 7077896 | tf_op jit(solution)/shard_map/ppermute | solution.py:615
  750.5 54.4 %collective-permute-start.1 = (f32[384,1536]{1,0:T(8,128)S(1)}, f32[384,1536]{1,0:T(8,128)S(1)}, u32[]{:S(2)}, u32[]{:S(2)}) collective-permute-start(f32[384,1536]{1,0:T(8,128)S(1)} %get-tuple-element.37.refs_1_), channel_id=1, source_target_pairs={{0,1},{1,0},{2,3},{3,2},{4,5},{5,4},{6,7},{7,6},{8,9},{9,8},{10,11... | collective-permute-start | bytes 7077896 | tf_op jit(solution)/shard_map/ppermute | solution.py:615
  751.9 99.6 %collective-permute-start.10 = (f32[384,1536]{1,0:T(8,128)S(1)}, f32[384,1536]{1,0:T(8,128)}, u32[]{:S(2)}, u32[]{:S(2)}) collective-permute-start(f32[384,1536]{1,0:T(8,128)S(1)} %collective-permute-done.2.refs_4_), channel_id=1, source_target_pairs={{0,4},{1,5},{2,6},{3,7},{4,0},{5,1},{6,2},{7,3},{8,12},{9,13},{10,... | collective-permute-start | bytes 7077896 | tf_op jit(solution)/shard_map/ppermute | solution.py:615
  800.3 52.7 %collective-permute-start.11 = (f32[384,1536]{1,0:T(8,128)}, f32[384,1536]{1,0:T(8,128)}, u32[]{:S(2)}, u32[]{:S(2)}) collective-permute-start(f32[384,1536]{1,0:T(8,128)} %collective-permute-done.7.refs_9_), channel_id=1, source_target_pairs={{0,2},{1,3},{2,0},{3,1},{4,6},{5,7},{6,4},{7,5},{8,10},{9,11},{10,... | collective-permute-start | bytes 7077896 | tf_op jit(solution)/shard_map/ppermute | solution.py:615
  801.6 51.4 %collective-permute-start.4 = (f32[384,1536]{1,0:T(8,128)S(1)}, f32[384,1536]{1,0:T(8,128)S(1)}, u32[]{:S(2)}, u32[]{:S(2)}) collective-permute-start(f32[384,1536]{1,0:T(8,128)S(1)} %collective-permute-done.2.refs_4_), channel_id=1, source_target_pairs={{0,1},{1,0},{2,3},{3,2},{4,5},{5,4},{6,7},{7,6},{8,9},{9,8},{10,11... | collective-permute-start | bytes 7077896 | tf_op jit(solution)/shard_map/ppermute | solution.py:615
  804.5 54.2 %collective-permute-start.9 = (f32[384,1536]{1,0:T(8,128)}, f32[384,1536]{1,0:T(8,128)}, u32[]{:S(2)}, u32[]{:S(2)}) collective-permute-start(f32[384,1536]{1,0:T(8,128)} %collective-permute-done.7.refs_9_), channel_id=1, source_target_pairs={{0,1},{1,0},{2,3},{3,2},{4,5},{5,4},{6,7},{7,6},{8,9},{9,8},{10,11... | collective-permute-start | bytes 7077896 | tf_op jit(solution)/shard_map/ppermute | solution.py:615
  806.4 52.3 %collective-permute-start.5 = (f32[384,1536]{1,0:T(8,128)}, f32[384,1536]{1,0:T(8,128)}, u32[]{:S(2)}, u32[]{:S(2)}) collective-permute-start(f32[384,1536]{1,0:T(8,128)} %collective-permute-done.3.refs_5_), channel_id=1, source_target_pairs={{0,1},{1,0},{2,3},{3,2},{4,5},{5,4},{6,7},{7,6},{8,9},{9,8},{10,11... | collective-permute-start | bytes 7077896 | tf_op jit(solution)/shard_map/ppermute | solution.py:615
  851.5 7.2 collective-permute-start.8
  853.0 6.8 collective-permute-start.12
  854.4 8.8 collective-permute-start.13
  (41 other events, 108.2 us)
Sparse Core Ops, SparseCore 0:
  11.4 74.8 all-gather.9
  217.5 56.8 all-gather.13
  277.3 258.5 all-gather.7
  538.6 241.3 all-gather.11
where the time goes:
time: 1060 us; the launch traced here: 1050 us
  Pallas kernels  634 us (60%)
  waiting for transfers between devices  246 us (23%)
  matrix products  68.9 us (7%)
  local copies, waits for them, and re-layouts  41.8 us (4%)
  starting transfers between devices  29 us (3%)
  other arithmetic  18.2 us (2%)
  between operations  14.9 us (1%)
    pallas_call x1, Pallas kernels, dense_sums(): pl.pallas_call(dense_kernel, out_shape=(half, half, jax.ShapeDtypeStruct(...  348 us
    ppermute x14, waiting for transfers between devices, local(): lax.ppermute(arr, 'ep', [(e, e ^ bit) for e in range(ep_size)])  196 us
    pallas_call x1, Pallas kernels, moe_backward(): pl.pallas_call(functools.partial(moe_kernel, cap), out_shape=(jax.ShapeDt...  125 us
    pallas_call x2, Pallas kernels, weight_grads(): pl.pallas_call(weight_kernel, grid=(count,), out_shape=(f32(w_up), f32(w_...  108 us
    dot_general x16, matrix products, mm(): return jnp.einsum(spec, a, b, preferred_element_type=F32)  68.9 us
    pallas_call x1, Pallas kernels, dispatch_rows(): pl.pallas_call(functools.partial(dispatch_kernel, local_exp, cap), grid_s...  31.8 us
    all_to_all x2, waiting for transfers between devices, spread(): lax.all_to_all(send, 'ep', 0, 0).reshape(ep_size * tokens, width // 2)  28.8 us
    pallas_call x1, Pallas kernels, assemble(): pl.pallas_call(assemble_kernel, out_shape=(jax.ShapeDtypeStruct((2 * HALF...  21.8 us
  transfers between devices with their start and end apart: 20, of which 10 were waited for; matrix products, arithmetic and copies ran while one was open for 8% of the time, Pallas kernels for 35%

commit v1 on v0

--- a/solution.py
+++ b/solution.py
@@ -76,9 +76,9 @@
     return lax.dot_general(a, b, (((0,), (0,)), ((), ())), preferred_element_type=jnp.float32)
 
 
-def dense_kernel(xn_ref, ao_ref, dsend_ref, gains_ref, low_ref, high_ref, gains_out_ref,
-                 dall, part, z_in, total, gain_buf,
-                 d_send, d_recv, dp_send, dp_recv, z_send, z_recv, own_sem, g_send, g_recv):
+def dense_kernel(acts_ref, dsend_ref, gains_ref, router_ref, low_ref, high_ref, gains_out_ref, router_out_ref,
+                 dall, part, z_in, total, gain_buf, router_buf,
+                 d_send, d_recv, dp_send, dp_recv, z_send, z_recv, own_sem, g_send, g_recv, r_send, r_recv, s_send, s_recv):
     z = lax.axis_index('dp')
     ep = lax.axis_index('ep')
     core = lax.rem(ep, 2)
@@ -105,17 +105,34 @@
         copy(dsend_ref.at[dev // 2], dall.at[rows_of(ep)], d_send.at[i], d_recv.at[i], z, dev).start()
     copy(dsend_ref.at[quarter], dall.at[rows_of(ep)], dp_send.at[3], dp_recv.at[3], z, partner).start()
 
-    world = 32
+    world = router_ref.shape[0]
     me = z * 8 + ep
 
-    def gain_copy(d, target):
-        return copy(gains_ref, gain_buf.at[d], g_send.at[d], g_recv.at[d], target // 8, lax.rem(target, 8))
-
-    def gain_start(d, _):
-        gain_copy(d, lax.rem(me + d, world)).start()
-        return 0
-
-    lax.fori_loop(1, world, gain_start, 0)
+    def push(pick, buf, s_sem, r_sem, d, target):
+        return copy(pick(target), buf.at[me], s_sem.at[d], r_sem.at[d], target // 8, lax.rem(target, 8))
+
+    def push_all(*args):
+        def body(d, _):
+            push(*args, d, lax.rem(me + d, world)).start()
+            return 0
+
+        lax.fori_loop(1, world, body, 0)
+
+    def wait_all(pick, buf, s_sem, r_sem):
+        def body(d, _):
+            push(pick, buf, s_sem, r_sem, d, lax.rem(me + d, world)).wait()
+            return 0
+
+        lax.fori_loop(1, world, body, 0)
+
+    def device_sum(buf):
+        return lax.fori_loop(0, world, lambda s, acc: acc + buf[s], jnp.zeros(buf.shape[1:], jnp.float32))
+
+    gain_push = (lambda t: gains_ref, gain_buf, g_send, g_recv)
+    share_push = (lambda t: router_ref.at[t], router_buf, r_send, r_recv)
+    total_push = (lambda t: router_out_ref.at[me], router_out_ref, s_send, s_recv)
+    push_all(*gain_push)
+    push_all(*share_push)
 
     dall[rows_of(ep), :] = dsend_ref[quarter]
     for i, dev in enumerate(far):
@@ -137,8 +154,15 @@
         k = i
         if k < STEPS:
             cols = slice(k * CHUNK, (k + 1) * CHUNK)
-            part[k, :, :split] = dot_tn(xn_ref[:, cols], dall[:, :split])
-            part[k, :, split:] = dot_tn(ao_ref[:, cols], dall[:, split:])
+            cols_o = slice(HALF + k * CHUNK, HALF + (k + 1) * CHUNK)
+            part[k, :, :split] = dot_tn(acts_ref[:, cols], dall[:, :split])
+            part[k, :, split:] = dot_tn(acts_ref[:, cols_o], dall[:, split:])
+        if i == 3:
+            wait_all(*share_push)
+            router_buf[me] = router_ref[me]
+            router_out_ref[me] = device_sum(router_buf)
+        if i == 4:
+            push_all(*total_push)
         a = i - 1
         t = i - 2
 
@@ -183,43 +207,38 @@
         copy(dall.at[rows_of(dev)], dall.at[rows_of(dev)], dp_send.at[i], dp_recv.at[i], z, partner).wait_send()
     copy(dsend_ref.at[quarter], dall.at[rows_of(ep)], dp_send.at[3], dp_recv.at[3], z, partner).wait_send()
 
-    def gain_wait(d, _):
-        gain_copy(d, me).wait()
-        return 0
-
-    lax.fori_loop(1, world, gain_wait, 0)
-    gain_buf[0] = gains_ref[...]
-
-    def gain_add(s, acc):
-        d = lax.rem(me - s + world, world)
-        return acc + gain_buf[d]
-
-    gains_out_ref[...] = lax.fori_loop(0, world, gain_add, jnp.zeros(gains_ref.shape, jnp.float32))
-
-
-def dense_sums(xn, ao, dsend, gains):
-    rows, width = xn.shape[0], dsend.shape[2]
+    wait_all(*gain_push)
+    gain_buf[me] = gains_ref[...]
+    gains_out_ref[...] = device_sum(gain_buf)
+    wait_all(*total_push)
+
+
+def dense_sums(acts, dsend, gains, router):
+    rows, width = acts.shape[0], dsend.shape[2]
     any_spec = pl.BlockSpec(memory_space=pl.ANY)
     vmem = pl.BlockSpec(memory_space=pltpu.VMEM)
     dma = pltpu.SemaphoreType.DMA
-    half = jax.ShapeDtypeStruct((HALF // 2, width), jnp.float32)
+    f32 = lambda *shape: jax.ShapeDtypeStruct(shape, jnp.float32)
+    world = router.shape[0]
     return pl.pallas_call(
         dense_kernel,
-        out_shape=(half, half, jax.ShapeDtypeStruct(gains.shape, jnp.float32)),
+        out_shape=(f32(HALF // 2, width), f32(HALF // 2, width), f32(*gains.shape), f32(*router.shape)),
         in_specs=[vmem, vmem, vmem, vmem],
-        out_specs=(any_spec, any_spec, vmem),
+        out_specs=(any_spec, any_spec, vmem, vmem),
         scratch_shapes=[
             pltpu.VMEM((rows, width), jnp.bfloat16),
             pltpu.VMEM((STEPS, CHUNK, width), jnp.float32),
             pltpu.VMEM((STEPS, CHUNK, width), jnp.float32),
             pltpu.VMEM((STEPS, CHUNK, width), jnp.float32),
-            pltpu.VMEM((32,) + gains.shape, jnp.float32),
-            dma((3,)), dma((3,)), dma((4,)), dma((4,)), dma((3, STEPS)), dma((3, STEPS)), dma((STEPS,)), dma((32,)), dma((32,)),
+            pltpu.VMEM((world,) + gains.shape, jnp.float32),
+            pltpu.VMEM(router.shape, jnp.float32),
+            dma((3,)), dma((3,)), dma((4,)), dma((4,)), dma((3, STEPS)), dma((3, STEPS)), dma((STEPS,)),
+            dma((world,)), dma((world,)), dma((world,)), dma((world,)), dma((world,)), dma((world,)),
         ],
         compiler_params=pltpu.CompilerParams(has_side_effects=True, vmem_limit_bytes=48 << 20),
         cost_estimate=pl.CostEstimate(flops=100 * 10**9, bytes_accessed=40 << 20, transcendentals=0),
         name='dense_sums',
-    )(xn, ao, dsend, gains)
+    )(acts, dsend, gains, router)
 
 
 def assemble_kernel(*refs):
@@ -305,43 +324,39 @@
     return dot_nn(select, xn).astype(BF16), dot_nn(select, dyc[:, :width]), gate_slot
 
 
-def dispatch_kernel(local_exp, cap, place_ref, xn_ref, dyc_ref, router_ref, recv_in, d_recv_in, recv_ref, d_recv_ref, codes_buf, gates_buf):
+def dispatch_kernel(local_exp, cap, rows_ref, router_ref, recv_in, d_recv_in, recv_ref, d_recv_ref, codes_buf, gates_buf):
     first = pl.multiple_of(lax.axis_index('ep') * local_exp, local_exp)
     router = router_ref[...]
-    width = xn_ref.shape[2]
-    for i in range(xn_ref.shape[0]):
-        recv, dy_rows, gate_slot = slot_rows(xn_ref[i], dyc_ref[i], router, first, local_exp, cap, codes_buf.at[i], gates_buf.at[i])
+    width = router.shape[1]
+    for i in range(rows_ref.shape[0]):
+        recv, dy_rows, gate_slot = slot_rows(rows_ref[i, :, :width], rows_ref[i, :, width:], router, first, local_exp, cap,
+                                             codes_buf.at[i], gates_buf.at[i])
         at = slice(i * cap, (i + 1) * cap)
         recv_ref[:, at, :] = recv.reshape(local_exp, cap, width)
         d_recv_ref[:, at, :] = (gate_slot * dy_rows).astype(BF16).reshape(local_exp, cap, width)
 
 
-def dispatch_rows(place, xn, dyc, router_t, recv, d_recv, cap):
-    planes, sources, tokens, lanes = dyc.shape
+def dispatch_rows(rows, router_t, recv, d_recv, skip, cap):
+    sources, tokens, lanes = rows.shape
     local_exp, _, width = recv.shape
     experts = router_t.shape[0]
     step = 4
     any_spec = pl.BlockSpec(memory_space=pl.ANY)
-    plane = lambda r, t: lax.rem(t[0] + r + 1, planes)
-    out_spec = pl.BlockSpec((local_exp, step * cap, width), lambda r, s, t: (0, (r + 1) * (sources // step) + s, 0))
+    out_spec = pl.BlockSpec((local_exp, step * cap, width), lambda s: (0, skip // (step * cap) + s, 0))
     same = lambda arr: jax.ShapeDtypeStruct(arr.shape, arr.dtype)
     return pl.pallas_call(
         functools.partial(dispatch_kernel, local_exp, cap),
-        grid_spec=pltpu.PrefetchScalarGridSpec(
-            num_scalar_prefetch=1,
-            grid=(planes - 1, sources // step),
-            in_specs=[pl.BlockSpec((None, step, tokens, width), lambda r, s, t: (plane(r, t), s, 0, 0)),
-                      pl.BlockSpec((None, step, tokens, lanes), lambda r, s, t: (plane(r, t), s, 0, 0)),
-                      pl.BlockSpec(router_t.shape, lambda r, s, t: (0, 0)), any_spec, any_spec],
-            out_specs=(out_spec, out_spec),
-            scratch_shapes=[pltpu.VMEM((step, experts, tokens), F32), pltpu.VMEM((step, experts, tokens), F32)]),
+        grid=(sources // step,),
+        in_specs=[pl.BlockSpec((step, tokens, lanes), lambda s: (s, 0, 0)), pl.BlockSpec(router_t.shape, lambda s: (0, 0)), any_spec, any_spec],
+        out_specs=(out_spec, out_spec),
+        scratch_shapes=[pltpu.VMEM((step, experts, tokens), F32), pltpu.VMEM((step, experts, tokens), F32)],
         out_shape=(same(recv), same(d_recv)),
-        input_output_aliases={4: 0, 5: 1},
+        input_output_aliases={2: 0, 3: 1},
         compiler_params=pltpu.CompilerParams(vmem_limit_bytes=56 << 20),
-        cost_estimate=pl.CostEstimate(flops=planes * sources * 4 * local_exp * cap * tokens * width, transcendentals=0,
-                                      bytes_accessed=planes * sources * tokens * width * 8),
+        cost_estimate=pl.CostEstimate(flops=sources * 4 * local_exp * cap * tokens * width, transcendentals=0,
+                                      bytes_accessed=sources * tokens * width * 8),
         name='dispatch_rows',
-    )(place, xn, dyc, router_t, recv, d_recv)
+    )(rows, router_t, recv, d_recv)
 
 
 def hidden_grads(recv, d_recv, up, lin, down):
@@ -551,7 +566,6 @@
     tok_spec = P(('dp', 'ep'))
     exp_spec = P('ep')
     rep_spec = P()
-    world = ('dp', 'ep')
 
     def local(x_in, dy_in, route_idx, gain_attn, w_qkv, w_o, gain_ffn, w_router, w_up, w_lin, w_down):
         num_seqs, seq_len, width = x_in.shape
@@ -567,28 +581,24 @@
         lanes = jnp.zeros((tokens, HEAD - experts), BF16)
         dyc_own = jnp.concatenate([dy_own, codes.T, lanes], axis=1)
         dyc_plane = lax.all_gather(dyc_own, 'ep')
-        dyc_all = lax.all_gather(dyc_own, world)
         router_t = w_router.T
         planes = mesh.shape['dp']
-        my_z = lax.axis_index('dp')
-
-        def spread(act):
-            halves = jnp.moveaxis(act.reshape(tokens, 2, width // 2), 1, 0)
-            send = jnp.broadcast_to(halves[None], (ep_size // 2, 2, tokens, width // 2)).reshape(ep_size, tokens, width // 2)
-            return lax.all_to_all(send, 'ep', 0, 0).reshape(ep_size * tokens, width // 2)
 
         x_f = x_in.astype(F32)
         xn_one, norm_one_pull = jax.vjp(rms_norm, x_f, gain_attn.astype(F32))
-        acts_xn = spread(xn_one)
         qkv_all = mm('bsd,de->bse', xn_one, w_qkv).astype(BF16)
         attn_out, attn_pull = jax.vjp(attn_core, qkv_all)
         attn_proj = mm('bsd,de->bse', attn_out, w_o)
         hidden = (x_f + attn_proj).astype(BF16).astype(F32).reshape(tokens, width)
         xn_two, norm_two_pull = jax.vjp(rms_norm, hidden, gain_ffn.astype(F32))
 
-        xn_all = lax.all_gather(xn_two, world)
-        d_back, gate_back, recv, d_recv = moe_backward(after(xn_two, acts_xn), dyc_plane, router_t, w_up, w_lin, w_down, cap, planes)
-        acts_ao = spread(after(attn_out, gate_back))
+        rows_own = jnp.concatenate([xn_two, dyc_own], axis=1)
+        foreign = [lax.ppermute(rows_own, 'dp', [((z + r) % planes, z) for z in range(planes)]) for r in range(1, planes)]
+        d_back, gate_back, recv, d_recv = moe_backward(xn_two, dyc_plane, router_t, w_up, w_lin, w_down, cap, planes)
+        both = jnp.stack([xn_one.reshape(tokens, width), attn_out.reshape(tokens, width)], axis=1)
+        halves = jnp.moveaxis(both.reshape(tokens, 2, 2, width // 2), 2, 0).reshape(1, 2, tokens, width)
+        send = jnp.broadcast_to(after(halves, gate_back), (ep_size // 2, 2, tokens, width)).reshape(ep_size, tokens, width)
+        acts = lax.all_to_all(send, 'ep', 0, 0).reshape(ep_size * tokens, width)
         d_gate_back = gate_back[:, :, :cap].reshape(experts, cap)
 
         select_own = one_hot(codes, cap)
@@ -598,18 +608,21 @@
         d_picked = (d_gates - jnp.sum(d_gates * gates, axis=0, keepdims=True)) / total * mask
         d_logits = (prob * (d_picked - jnp.sum(prob * d_picked, axis=0, keepdims=True))).astype(BF16)
         d_xn_two = (d_moe_in + mm('et,de->td', d_logits, w_router)).astype(BF16)
-        d_logits_all = lax.all_gather(d_logits.T, world)
+        grad_router = mm('td,et->de', xn_two, d_logits)
         d_hidden, grad_gain_ffn = norm_two_pull(d_xn_two)
         d_resid = (d_hidden + dy_own.astype(F32)).astype(BF16).reshape(num_seqs, seq_len, width)
         d_attn_out = mm('bse,de->bsd', d_resid, w_o).astype(BF16)
         d_qkv = attn_pull(d_attn_out)[0]
+        foreign = lax.all_gather(after(jnp.stack(foreign), acts, d_qkv), 'ep')
         d_xn_one = mm('bse,de->bsd', d_qkv, w_qkv).astype(BF16)
         d_x_norm, grad_gain_attn = norm_one_pull(d_xn_one)
         dx_out = (d_x_norm + d_resid.astype(F32)).astype(BF16)
         quarters = lambda arr: jnp.moveaxis(arr.reshape(tokens, 4, -1), 1, 0)
         dsend = jnp.concatenate([quarters(d_qkv), quarters(d_resid)], axis=2)
         gains = jnp.concatenate([grad_gain_attn, grad_gain_ffn]).reshape(-1, 128)
-        low, high, gains = dense_sums(acts_xn, acts_ao, dsend, gains)
+        world_size = planes * ep_size
+        low, high, gains, grad_router = dense_sums(acts, dsend, gains, grad_router.reshape(world_size, -1, 128))
+        grad_router = grad_router.reshape(width, experts)
         grad_gain_attn, grad_gain_ffn = gains.reshape(2, width)
 
         flip = lambda arr, bit: lax.ppermute(arr, 'ep', [(e, e ^ bit) for e in range(ep_size)])
@@ -621,11 +634,8 @@
         swapped += [flip(arr, 1) for arr in pieces[6:]]
         pieces = [arr for i in range(4) for arr in (pieces[2 * i], pieces[2 * i + 1], swapped[2 * i], swapped[2 * i + 1])]
 
-        xn_late, dyc_late, d_logits_late = lax.optimization_barrier((xn_all, dyc_all, d_logits_all, gains))[:3]
-        grad_router = mm('ntd,nte->de', xn_late, d_logits_late)
-        xn_late = xn_late.reshape(planes, ep_size, tokens, width)
-        dyc_late = dyc_late.reshape(planes, ep_size, tokens, -1)
-        recv, d_recv = dispatch_rows(my_z.reshape(1), xn_late, dyc_late, router_t, recv, d_recv, cap)
+        foreign = after(foreign, gains)
+        recv, d_recv = dispatch_rows(foreign.reshape(-1, tokens, foreign.shape[-1]), router_t, recv, d_recv, ep_size * cap, cap)
         grads = weight_grads(recv, d_recv, w_up, w_lin, w_down, 0, local_exp // 2)
         grad_up, grad_lin, grad_down = weight_grads(recv, d_recv, w_up, w_lin, w_down, local_exp // 2, local_exp // 2, grads)
         grad_wqkv, grad_wo = assemble(pieces)

time: 1060 us -> 1000 us (0.943)
  Pallas kernels: 634 us -> 532 us
  waiting for transfers between devices: 246 us -> 312 us
  matrix products: 68.9 us -> 51.2 us
  starting transfers between devices: 29 us -> 15 us
  local copies, waits for them, and re-layouts: 41.8 us -> 52.7 us
    ppermute x0 -> x3, waiting for transfers between devices: none -> 140 us  [local(): lax.ppermute(rows_own, 'dp', [((z + r) % planes, z) for z in range(planes)])]
    pallas_call x2, Pallas kernels: 380 us -> 278 us  [the longest x1 246 us: dense_sums(): pl.pallas_call(dense_kernel, out_shape=(f32(HALF // 2, width), f32(HALF /...]
    ppermute x14, waiting for transfers between devices: 196 us -> 146 us  [local(): lax.ppermute(arr, 'ep', [(e, e ^ bit) for e in range(ep_size)])]
    all_to_all x2 -> x1, waiting for transfers between devices: 28.8 us -> 0.01 us  [local(): acts = lax.all_to_all(send, 'ep', 0, 0).reshape(ep_size * tokens, width)]
    dot_general x16, matrix products: 68.9 us -> 51.2 us  [mm(): return jnp.einsum(spec, a, b, preferred_element_type=F32)]
    all_to_all x2 -> x1, starting transfers between devices: 20.9 us -> 4.88 us  [local(): acts = lax.all_to_all(send, 'ep', 0, 0).reshape(ep_size * tokens, width)]
    unnamed x107 -> x134, local copies, waits for them, and re-layouts: 19.8 us -> 23 us
  transfers between devices with their start and end apart: 20 -> 20, of which waited for: 10 -> 9; matrix products, arithmetic and copies ran while one was open for 8% -> 9% of each run, Pallas kernels for 35% -> 27%
where the time goes in v1:
time: 1000 us; the launch traced here: 997 us
  Pallas kernels  532 us (53%)
  waiting for transfers between devices  312 us (31%)
  local copies, waits for them, and re-layouts  52.7 us (5%)
  matrix products  51.2 us (5%)
  other arithmetic  19.2 us (2%)
  between operations  15.1 us (2%)
  starting transfers between devices  15 us (2%)
    pallas_call x1, Pallas kernels, dense_sums(): pl.pallas_call(dense_kernel, out_shape=(f32(HALF // 2, width), f32(HALF /...  246 us
    ppermute x14, waiting for transfers between devices, local(): lax.ppermute(arr, 'ep', [(e, e ^ bit) for e in range(ep_size)])  146 us
    ppermute x3, waiting for transfers between devices, local(): lax.ppermute(rows_own, 'dp', [((z + r) % planes, z) for z in range(planes)])  140 us
    pallas_call x1, Pallas kernels, moe_backward(): pl.pallas_call(functools.partial(moe_kernel, cap), out_shape=(jax.ShapeDt...  125 us
    pallas_call x2, Pallas kernels, weight_grads(): pl.pallas_call(weight_kernel, grid=(count,), out_shape=(f32(w_up), f32(w_...  108 us
    dot_general x16, matrix products, mm(): return jnp.einsum(spec, a, b, preferred_element_type=F32)  51.2 us
    pallas_call x1, Pallas kernels, dispatch_rows(): pl.pallas_call(functools.partial(dispatch_kernel, local_exp, cap), grid=(...  31.6 us
    all_gather x1, waiting for transfers between devices, local(): dyc_plane = lax.all_gather(dyc_own, 'ep')  26.2 us
  transfers between devices with their start and end apart: 20, of which 9 were waited for; matrix products, arithmetic and copies ran while one was open for 9% of the time, Pallas kernels for 27%

profile of v1, /device:TPU:0, one launch (start us, length us, event | category | flops | bytes accessed | tf_op | source)
XLA Modules:
  0.0 997.4 jit_solution(2944602729981026771)
XLA Ops:
  9.2 2.0 concatenate.19
  13.0 10.1 %convolution_convert_fusion = bf16[256,4608]{1,0:T(8,128)(2,1)} fusion(bf16[1536,4608]{1,0:T(8,128)(2,1)} %param.15, bf16[1,256,1536]{2,1,0:T(8,128)(2,1)S(1)} %fusion.23), kind=kOutput, calls=%fused_computation.1 | convolution fusion | flops 3625058304 | bytes 17301504 | tf_op jit(solution)/shard_map/bsd,de->bse/dot_general | solution.py:20
  23.1 2.8 copy.110
  35.6 26.2 %all-gather.5.cloned.1.call-done = bf16[2048,1664]{1,0:T(8,128)(2,1)} async-done(((bf16[256,1664]{1,0:T(8,128)(2,1)}), bf16[2048,1664]{1,0:T(8,128)(2,1)}) %all-gather.5.cloned.1.call-update) | async-done | bytes 6815760 | tf_op jit(solution)/shard_map/all_gather | solution.py:583
  61.8 124.7 %moe_backward.1 = (bf16[64,32,1536]{2,1,0:T(8,128)(2,1)}, f32[8,8,128]{2,1,0:T(8,128)}, bf16[8,1024,1536]{2,1,0:T(8,128)(2,1)}, bf16[8,1024,1536]{2,1,0:T(8,128)(2,1)}) custom-call(bf16[256,1536]{1,0:T(8,128)(2,1)} %fusion.25.xn_ref, bf16[8,256,1664]{2,1,0:T(8,128)(2,1)} %bitcast.172, bf16[64,1536]{1,0:T(8,128)(2,1)} %bitcast.164, ...), custom_call_target="tpu_custom_call" | custom-call | flops 60000002048 | bytes 67108864 | tf_op jit(solution)/shard_map/moe_backward/pallas_call | solution.py:500
  186.5 2.6 copy.129
  189.0 4.6 broadcast_in_dim.87
  193.7 4.9 all-to-all-start
  198.7 3.5 concatenate.24
  202.2 1.8 collective-permute-start.14
  205.3 36.0 %collective-permute-done.14 = bf16[256,3200]{1,0:T(8,128)(2,1)S(1)} collective-permute-done((bf16[256,3200]{1,0:T(8,128)(2,1)}, bf16[256,3200]{1,0:T(8,128)(2,1)S(1)}, u32[]{:S(2)}, u32[]{:S(2)}) %collective-permute-start.14) | collective-permute-done | bytes 1638432 | tf_op jit(solution)/shard_map/ppermute | solution.py:596
  241.3 103.9 %collective-permute-done.15 = bf16[256,3200]{1,0:T(8,128)(2,1)S(1)} collective-permute-done((bf16[256,3200]{1,0:T(8,128)(2,1)}, bf16[256,3200]{1,0:T(8,128)(2,1)S(1)}, u32[]{:S(2)}, u32[]{:S(2)}) %collective-permute-start.15) | collective-permute-done | bytes 1638432 | tf_op jit(solution)/shard_map/ppermute | solution.py:596
  345.2 2.9 pad_maximum_fusion
  358.6 2.9 fusion.63
  362.9 11.7 %fusion.9 = f32[256,1536]{1,0:T(8,128)S(1)} fusion(bf16[64,32,1536]{2,1,0:T(8,128)(2,1)} %get-tuple-element.30, f32[64,256]{1,0:T(8,128)} %copy-done.35, f32[32]{0:T(128)} %copy-done.63), kind=kOutput, calls=%fused_computation.27 | convolution fusion | flops 1611137024 | bytes 7929984 | tf_op jit(solution)/shard_map/ect,ecd->td/dot_general | solution.py:20
  379.0 5.1 convolution_convert_fusion.2
  385.5 2.9 fusion.8
  393.7 3.1 copy.130
  396.8 2.3 copy.132
  399.1 8.1 fusion.24
  407.3 2.0 pad_maximum_fusion.1.dsend_ref
  409.3 246.2 %dense_sums.1 = (f32[384,1536]{1,0:T(8,128)S(1)}, f32[384,1536]{1,0:T(8,128)S(1)}, f32[24,128]{1,0:T(8,128)S(1)}, f32[32,24,128]{2,1,0:T(8,128)S(1)}) custom-call(bf16[2048,1536]{1,0:T(8,128)(2,1)} %bitcast.45.acts_ref, bf16[4,256,1536]{2,1,0:T(8,128)(2,1)} %pad_maximum_fusion.1.dsend_ref, f32[24,128]{1,0:T(8,128)S(1)} %pad_maximum_fusion.3.gains_ref, ...), custom_call_target="tpu_custom_call" | custom-call | flops 99999997952 | bytes 41943040 | tf_op jit(solution)/shard_map/dense_sums/pallas_call | solution.py:223
  659.6 50.1 %collective-permute-done.2.refs_4_ = f32[384,1536]{1,0:T(8,128)S(1)} collective-permute-done((f32[384,1536]{1,0:T(8,128)S(1)}, f32[384,1536]{1,0:T(8,128)S(1)}, u32[]{:S(2)}, u32[]{:S(2)}) %collective-permute-start.2) | collective-permute-done | bytes 2359328 | tf_op jit(solution)/shard_map/ppermute | solution.py:628
  711.6 45.7 %collective-permute-done.3.refs_5_ = f32[384,1536]{1,0:T(8,128)} collective-permute-done((f32[384,1536]{1,0:T(8,128)S(1)}, f32[384,1536]{1,0:T(8,128)}, u32[]{:S(2)}, u32[]{:S(2)}) %collective-permute-start.3) | collective-permute-done | bytes 2359328 | tf_op jit(solution)/shard_map/ppermute | solution.py:628
  758.6 2.1 collective-permute-done.6.refs_8_
  765.4 43.4 %collective-permute-done.10.refs_12_ = f32[384,1536]{1,0:T(8,128)} collective-permute-done((f32[384,1536]{1,0:T(8,128)S(1)}, f32[384,1536]{1,0:T(8,128)}, u32[]{:S(2)}, u32[]{:S(2)}) %collective-permute-start.10) | collective-permute-done | bytes 2359328 | tf_op jit(solution)/shard_map/ppermute | solution.py:628
  813.3 2.1 copy.134
  817.1 3.4 collective-permute-done.13.refs_15_
  828.8 21.8 %assemble.1 = (f32[1536,4608]{1,0:T(8,128)}, f32[1536,1536]{1,0:T(8,128)}) custom-call(f32[384,1536]{1,0:T(8,128)S(1)} %get-tuple-element.34.refs_0_, f32[384,1536]{1,0:T(8,128)S(1)} %copy-done.1, f32[384,1536]{1,0:T(8,128)S(1)} %copy-done.5, f32[384,1536]{1,0:T(8,128)S(1)} %copy-done.7, f32[384,1536]{1,0:T(8,128)S(1)} %copy-done.3, ...), custom_call_target="tpu_custom_call" | custom-call | flops 20000000000 | bytes 83886080 | tf_op jit(solution)/shard_map/assemble/pallas_call | solution.py:282
  850.6 31.6 %dispatch_rows.1 = (bf16[8,1024,1536]{2,1,0:T(8,128)(2,1)}, bf16[8,1024,1536]{2,1,0:T(8,128)(2,1)}) custom-call(bf16[24,256,3200]{2,1,0:T(8,128)(2,1)} %all-gather.7.cloned.1.call-done, bf16[64,1536]{1,0:T(8,128)(2,1)} %bitcast.165, bf16[8,1024,1536]{2,1,0:T(8,128)(2,1)} %get-tuple-element.41.recv_in, ...), custom_call_target="tpu_custom_call", output_to_operand_aliasing={{0}: (2, {}), {1}: (3, {})} | custom-call | flops 9663676416 | bytes 75497472 | tf_op jit(solution)/shard_map/dispatch_rows/pallas_call | solution.py:347
  882.2 54.0 %weight_grads.2 = (f32[8,1536,512]{2,1,0:T(8,128)}, f32[8,1536,512]{2,1,0:T(8,128)}, f32[8,512,1536]{2,1,0:T(8,128)}) custom-call(bf16[8,1024,1536]{2,1,0:T(8,128)(2,1)} %get-tuple-element.43.recv_ref, bf16[8,1024,1536]{2,1,0:T(8,128)(2,1)} %get-tuple-element.44.d_recv_ref, bf16[8,1536,512]{2,1,0:T(8,128)(2,1)} %up_ref.5, bf16[8,1536,512]{2,1,0:T(8,128)(2,1)} %lin_ref.5, ...), custom_call_target="tpu_custom_call" | custom-call | flops 38654705664 | bytes 83886080 | tf_op jit(solution)/shard_map/weight_grads/pallas_call | solution.py:551
  936.2 54.1 %weight_grads.3 = (f32[8,1536,512]{2,1,0:T(8,128)}, f32[8,1536,512]{2,1,0:T(8,128)}, f32[8,512,1536]{2,1,0:T(8,128)}) custom-call(bf16[8,1024,1536]{2,1,0:T(8,128)(2,1)} %get-tuple-element.43.recv_ref, bf16[8,1024,1536]{2,1,0:T(8,128)(2,1)} %get-tuple-element.44.d_recv_ref, ...), custom_call_target="tpu_custom_call", output_to_operand_aliasing={{0}: (5, {}), {1}: (6, {}), {2}: (7, {})} | custom-call | flops 38654705664 | bytes 83886080 | tf_op jit(solution)/shard_map/weight_grads/pallas_call | solution.py:551
  (214 shorter events, 63.6 us)
Async XLA Ops:
  7.2 54.6 %all-gather.5.cloned.1.call-start = ((), (), s32[]{:S(2)}) async-start(), calls=%async_computation.1 | async-start | bytes 7667712 | tf_op jit(solution)/shard_map/all_gather | solution.py:583
  34.4 152.0 %copy-start.59 = (f32[256]{0:T(256)}, f32[256]{0:T(256)S(1)}, u32[]{:S(2)}) copy-start(f32[256]{0:T(256)S(1)} %get-tuple-element.98) | copy-start | bytes 3076
  34.4 340.2 %copy-start.20 = (bf16[256,1536]{1,0:T(8,128)(2,1)}, bf16[256,1536]{1,0:T(8,128)(2,1)S(1)}, u32[]{:S(2)}) copy-start(bf16[256,1536]{1,0:T(8,128)(2,1)S(1)} %get-tuple-element.99) | copy-start | bytes 2359300
  34.5 152.0 %copy-start.49 = (f32[256]{0:T(256)}, f32[256]{0:T(256)S(1)}, u32[]{:S(2)}) copy-start(f32[256]{0:T(256)S(1)} %fusion.58) | copy-start | bytes 3076
  193.7 154.4 %all-to-all-start = ((bf16[8,256,1536]{2,1,0:T(8,128)(2,1)}), bf16[8,256,1536]{2,1,0:T(8,128)(2,1)}, u32[]{:S(2)}, u32[]{:S(2)}) async-start(bf16[8,256,1536]{2,1,0:T(8,128)(2,1)} %bitcast.145), calls=%async_computation | async-start | bytes 12582912 | tf_op jit(solution)/shard_map/all_to_all | solution.py:601
  198.6 652.0 %all-gather.7.cloned.1.call-start = ((), (), s32[]{:S(2)}) async-start(), calls=%async_computation.2 | async-start | bytes 44236800 | tf_op jit(solution)/shard_map/all_gather | solution.py:616
  202.2 39.1 %collective-permute-start.14 = (bf16[256,3200]{1,0:T(8,128)(2,1)}, bf16[256,3200]{1,0:T(8,128)(2,1)S(1)}, u32[]{:S(2)}, u32[]{:S(2)}) collective-permute-start(bf16[256,3200]{1,0:T(8,128)(2,1)} %concatenate.24), channel_id=1, source_target_pairs={{8,0},{16,8},{24,16},{0,24},{9,1},{17,9},{25,17},{1,25},{10,2},{18... | collective-permute-start | bytes 4915208 | tf_op jit(solution)/shard_map/ppermute | solution.py:596
  204.1 141.1 %collective-permute-start.15 = (bf16[256,3200]{1,0:T(8,128)(2,1)}, bf16[256,3200]{1,0:T(8,128)(2,1)S(1)}, u32[]{:S(2)}, u32[]{:S(2)}) collective-permute-start(bf16[256,3200]{1,0:T(8,128)(2,1)} %concatenate.24), channel_id=1, source_target_pairs={{16,0},{24,8},{0,16},{8,24},{17,1},{25,9},{1,17},{9,25},{18,2},{26... | collective-permute-start | bytes 4915208 | tf_op jit(solution)/shard_map/ppermute | solution.py:596
  204.1 141.1 %collective-permute-start.16 = (bf16[256,3200]{1,0:T(8,128)(2,1)}, bf16[256,3200]{1,0:T(8,128)(2,1)S(1)}, u32[]{:S(2)}, u32[]{:S(2)}) collective-permute-start(bf16[256,3200]{1,0:T(8,128)(2,1)} %concatenate.24), channel_id=1, source_target_pairs={{24,0},{0,8},{8,16},{16,24},{25,1},{1,9},{9,17},{17,25},{26,2},{2,... | collective-permute-start | bytes 4915208 | tf_op jit(solution)/shard_map/ppermute | solution.py:596
  362.8 11.8 %copy-start.22 = (f32[256,64]{1,0:T(8,128)S(1)}, f32[256,64]{1,0:T(8,128)}, u32[]{:S(2)}) copy-start(f32[256,64]{1,0:T(8,128)} %copy-done.21) | copy-start | bytes 196612
  362.8 11.8 %copy-start.26 = (f32[64,256]{0,1:T(8,128)S(1)}, f32[64,256]{0,1:T(8,128)}, u32[]{:S(2)}) copy-start(f32[64,256]{0,1:T(8,128)} %copy-done.25) | copy-start | bytes 196612
  362.9 11.8 %copy-start.28 = (bf16[1536,64]{0,1:T(8,128)(2,1)S(1)}, bf16[1536,64]{0,1:T(8,128)(2,1)}, u32[]{:S(2)}) copy-start(bf16[1536,64]{0,1:T(8,128)(2,1)} %param.18) | copy-start | bytes 589828
  362.9 11.8 %copy-start.32 = (pred[64,256]{0,1:T(32,128)(4,1)S(1)}, pred[64,256]{0,1:T(32,128)(4,1)}, u32[]{:S(2)}) copy-start(pred[64,256]{0,1:T(32,128)(4,1)} %copy-done.31) | copy-start | bytes 49156
  362.9 11.8 %copy-start.42 = (f32[256]{0:T(256)S(1)}, f32[256]{0:T(256)}, u32[]{:S(2)}) copy-start(f32[256]{0:T(256)} %copy-done.41) | copy-start | bytes 3076
  409.3 401.5 %copy-start.52 = (f32[256]{0:T(256)S(1)}, f32[256]{0:T(256)}, u32[]{:S(2)}) copy-start(f32[256]{0:T(256)} %copy-done.51) | copy-start | bytes 3076
  409.3 401.5 %copy-start.15 = (bf16[256,1536]{1,0:T(8,128)(2,1)S(1)}, bf16[256,1536]{1,0:T(8,128)(2,1)}, u32[]{:S(2)}) copy-start(bf16[256,1536]{1,0:T(8,128)(2,1)} %copy-done.14) | copy-start | bytes 2359300
  409.3 401.5 %copy-start.19 = (bf16[1,256,1536]{2,1,0:T(8,128)(2,1)S(1)}, bf16[1,256,1536]{2,1,0:T(8,128)(2,1)}, u32[]{:S(2)}) copy-start(bf16[1,256,1536]{2,1,0:T(8,128)(2,1)} %param.11) | copy-start | bytes 2359300
  409.3 401.5 %copy-start.54 = (f32[256]{0:T(256)S(1)}, f32[256]{0:T(256)}, u32[]{:S(2)}) copy-start(f32[256]{0:T(256)} %copy-done.53) | copy-start | bytes 3076
  655.4 54.2 %collective-permute-start.2 = (f32[384,1536]{1,0:T(8,128)S(1)}, f32[384,1536]{1,0:T(8,128)S(1)}, u32[]{:S(2)}, u32[]{:S(2)}) collective-permute-start(f32[384,1536]{1,0:T(8,128)S(1)} %get-tuple-element.34.refs_0_), channel_id=1, source_target_pairs={{0,2},{1,3},{2,0},{3,1},{4,6},{5,7},{6,4},{7,5},{8,10},{9,11},{10,... | collective-permute-start | bytes 7077896 | tf_op jit(solution)/shard_map/ppermute | solution.py:628
  655.9 55.1 %collective-permute-start.7 = (f32[384,1536]{1,0:T(8,128)S(1)}, f32[384,1536]{1,0:T(8,128)}, u32[]{:S(2)}, u32[]{:S(2)}) collective-permute-start(f32[384,1536]{1,0:T(8,128)S(1)} %get-tuple-element.35.refs_1_), channel_id=1, source_target_pairs={{0,4},{1,5},{2,6},{3,7},{4,0},{5,1},{6,2},{7,3},{8,12},{9,13},{10,... | collective-permute-start | bytes 7077896 | tf_op jit(solution)/shard_map/ppermute | solution.py:628
  656.3 101.0 %collective-permute-start.3 = (f32[384,1536]{1,0:T(8,128)S(1)}, f32[384,1536]{1,0:T(8,128)}, u32[]{:S(2)}, u32[]{:S(2)}) collective-permute-start(f32[384,1536]{1,0:T(8,128)S(1)} %get-tuple-element.35.refs_1_), channel_id=1, source_target_pairs={{0,2},{1,3},{2,0},{3,1},{4,6},{5,7},{6,4},{7,5},{8,10},{9,11},{10,... | collective-permute-start | bytes 7077896 | tf_op jit(solution)/shard_map/ppermute | solution.py:628
  658.1 102.6 %collective-permute-start.6 = (f32[384,1536]{1,0:T(8,128)S(1)}, f32[384,1536]{1,0:T(8,128)}, u32[]{:S(2)}, u32[]{:S(2)}) collective-permute-start(f32[384,1536]{1,0:T(8,128)S(1)} %get-tuple-element.34.refs_0_), channel_id=1, source_target_pairs={{0,4},{1,5},{2,6},{3,7},{4,0},{5,1},{6,2},{7,3},{8,12},{9,13},{10,... | collective-permute-start | bytes 7077896 | tf_op jit(solution)/shard_map/ppermute | solution.py:628
  659.6 102.5 %collective-permute-start = (f32[384,1536]{1,0:T(8,128)S(1)}, f32[384,1536]{1,0:T(8,128)S(1)}, u32[]{:S(2)}, u32[]{:S(2)}) collective-permute-start(f32[384,1536]{1,0:T(8,128)S(1)} %get-tuple-element.34.refs_0_), channel_id=1, source_target_pairs={{0,1},{1,0},{2,3},{3,2},{4,5},{5,4},{6,7},{7,6},{8,9},{9,8},{10,11... | collective-permute-start | bytes 7077896 | tf_op jit(solution)/shard_map/ppermute | solution.py:628
  709.6 54.4 %collective-permute-start.1 = (f32[384,1536]{1,0:T(8,128)S(1)}, f32[384,1536]{1,0:T(8,128)S(1)}, u32[]{:S(2)}, u32[]{:S(2)}) collective-permute-start(f32[384,1536]{1,0:T(8,128)S(1)} %get-tuple-element.35.refs_1_), channel_id=1, source_target_pairs={{0,1},{1,0},{2,3},{3,2},{4,5},{5,4},{6,7},{7,6},{8,9},{9,8},{10,11... | collective-permute-start | bytes 7077896 | tf_op jit(solution)/shard_map/ppermute | solution.py:628
  711.0 97.8 %collective-permute-start.10 = (f32[384,1536]{1,0:T(8,128)S(1)}, f32[384,1536]{1,0:T(8,128)}, u32[]{:S(2)}, u32[]{:S(2)}) collective-permute-start(f32[384,1536]{1,0:T(8,128)S(1)} %collective-permute-done.2.refs_4_), channel_id=1, source_target_pairs={{0,4},{1,5},{2,6},{3,7},{4,0},{5,1},{6,2},{7,3},{8,12},{9,13},{10,... | collective-permute-start | bytes 7077896 | tf_op jit(solution)/shard_map/ppermute | solution.py:628
  757.3 51.6 %collective-permute-start.11 = (f32[384,1536]{1,0:T(8,128)}, f32[384,1536]{1,0:T(8,128)}, u32[]{:S(2)}, u32[]{:S(2)}) collective-permute-start(f32[384,1536]{1,0:T(8,128)} %collective-permute-done.7.refs_9_), channel_id=1, source_target_pairs={{0,2},{1,3},{2,0},{3,1},{4,6},{5,7},{6,4},{7,5},{8,10},{9,11},{10,... | collective-permute-start | bytes 7077896 | tf_op jit(solution)/shard_map/ppermute | solution.py:628
  760.7 48.7 %collective-permute-start.4 = (f32[384,1536]{1,0:T(8,128)S(1)}, f32[384,1536]{1,0:T(8,128)S(1)}, u32[]{:S(2)}, u32[]{:S(2)}) collective-permute-start(f32[384,1536]{1,0:T(8,128)S(1)} %collective-permute-done.2.refs_4_), channel_id=1, source_target_pairs={{0,1},{1,0},{2,3},{3,2},{4,5},{5,4},{6,7},{7,6},{8,9},{9,8},{10,11... | collective-permute-start | bytes 7077896 | tf_op jit(solution)/shard_map/ppermute | solution.py:628
  763.5 52.5 %collective-permute-start.9 = (f32[384,1536]{1,0:T(8,128)}, f32[384,1536]{1,0:T(8,128)}, u32[]{:S(2)}, u32[]{:S(2)}) collective-permute-start(f32[384,1536]{1,0:T(8,128)} %collective-permute-done.7.refs_9_), channel_id=1, source_target_pairs={{0,1},{1,0},{2,3},{3,2},{4,5},{5,4},{6,7},{7,6},{8,9},{9,8},{10,11... | collective-permute-start | bytes 7077896 | tf_op jit(solution)/shard_map/ppermute | solution.py:628
  765.4 50.6 %collective-permute-start.5 = (f32[384,1536]{1,0:T(8,128)}, f32[384,1536]{1,0:T(8,128)}, u32[]{:S(2)}, u32[]{:S(2)}) collective-permute-start(f32[384,1536]{1,0:T(8,128)} %collective-permute-done.3.refs_5_), channel_id=1, source_target_pairs={{0,1},{1,0},{2,3},{3,2},{4,5},{5,4},{6,7},{7,6},{8,9},{9,8},{10,11... | collective-permute-start | bytes 7077896 | tf_op jit(solution)/shard_map/ppermute | solution.py:628
  808.8 7.2 collective-permute-start.8
  808.9 8.2 collective-permute-start.12
  810.8 9.7 collective-permute-start.13
  (54 other events, 225.0 us)
Sparse Core Ops, SparseCore 0:
  11.4 50.3 all-gather.4
  348.2 225.9 all-gather.6

commit v2 on v1

--- a/solution.py
+++ b/solution.py
@@ -67,8 +67,9 @@
 
 
 HALF = 768
-CHUNK = 128
+CHUNK = 64
 STEPS = HALF // CHUNK
+BLOCK = 128
 MESH = pl.DeviceIdType.MESH
 
 
@@ -76,7 +77,7 @@
     return lax.dot_general(a, b, (((0,), (0,)), ((), ())), preferred_element_type=jnp.float32)
 
 
-def dense_kernel(acts_ref, dsend_ref, gains_ref, router_ref, low_ref, high_ref, gains_out_ref, router_out_ref,
+def dense_kernel(acts_xn_ref, acts_ao_ref, dsend_ref, gains_ref, router_ref, low_ref, high_ref, gains_out_ref, router_out_ref,
                  dall, part, z_in, total, gain_buf, router_buf,
                  d_send, d_recv, dp_send, dp_recv, z_send, z_recv, own_sem, g_send, g_recv, r_send, r_recv, s_send, s_recv):
     z = lax.axis_index('dp')
@@ -152,16 +153,16 @@
 
     for i in range(STEPS + 3):
         k = i
-        if k < STEPS:
-            cols = slice(k * CHUNK, (k + 1) * CHUNK)
-            cols_o = slice(HALF + k * CHUNK, HALF + (k + 1) * CHUNK)
-            part[k, :, :split] = dot_tn(acts_ref[:, cols], dall[:, :split])
-            part[k, :, split:] = dot_tn(acts_ref[:, cols_o], dall[:, split:])
-        if i == 3:
+        if k < STEPS and k * CHUNK % BLOCK == 0:
+            cols = slice(k * CHUNK, k * CHUNK + BLOCK)
+            many = BLOCK // CHUNK
+            part[k:k + many, :, :split] = dot_tn(acts_xn_ref[:, cols], dall[:, :split]).reshape(many, CHUNK, split)
+            part[k:k + many, :, split:] = dot_tn(acts_ao_ref[:, cols], dall[:, split:]).reshape(many, CHUNK, width - split)
+        if i == 6:
             wait_all(*share_push)
             router_buf[me] = router_ref[me]
             router_out_ref[me] = device_sum(router_buf)
-        if i == 4:
+        if i == 8:
             push_all(*total_push)
         a = i - 1
         t = i - 2
@@ -171,12 +172,10 @@
             if 0 <= a < STEPS:
                 up_copy(a).wait_recv()
                 part[a] = part[a] + z_in[a]
+                cross_copy(a).start()
             if 0 <= t < STEPS:
                 cross_copy(t).wait_recv()
                 total[t] = part[t] + total[t]
-            if 0 <= a < STEPS:
-                cross_copy(a).start()
-            if 0 <= t < STEPS:
                 down_copy(t).start()
                 own_copy(t).start()
 
@@ -213,8 +212,8 @@
     wait_all(*total_push)
 
 
-def dense_sums(acts, dsend, gains, router):
-    rows, width = acts.shape[0], dsend.shape[2]
+def dense_sums(acts_xn, acts_ao, dsend, gains, router):
+    rows, width = acts_xn.shape[0], dsend.shape[2]
     any_spec = pl.BlockSpec(memory_space=pl.ANY)
     vmem = pl.BlockSpec(memory_space=pltpu.VMEM)
     dma = pltpu.SemaphoreType.DMA
@@ -223,7 +222,7 @@
     return pl.pallas_call(
         dense_kernel,
         out_shape=(f32(HALF // 2, width), f32(HALF // 2, width), f32(*gains.shape), f32(*router.shape)),
-        in_specs=[vmem, vmem, vmem, vmem],
+        in_specs=[vmem, vmem, vmem, vmem, vmem],
         out_specs=(any_spec, any_spec, vmem, vmem),
         scratch_shapes=[
             pltpu.VMEM((rows, width), jnp.bfloat16),
@@ -238,7 +237,7 @@
         compiler_params=pltpu.CompilerParams(has_side_effects=True, vmem_limit_bytes=48 << 20),
         cost_estimate=pl.CostEstimate(flops=100 * 10**9, bytes_accessed=40 << 20, transcendentals=0),
         name='dense_sums',
-    )(acts, dsend, gains, router)
+    )(acts_xn, acts_ao, dsend, gains, router)
 
 
 def assemble_kernel(*refs):
@@ -584,8 +583,14 @@
         router_t = w_router.T
         planes = mesh.shape['dp']
 
+        def spread(act):
+            halves = jnp.moveaxis(act.reshape(tokens, 2, width // 2), 1, 0)
+            send = jnp.broadcast_to(halves[None], (ep_size // 2, 2, tokens, width // 2)).reshape(ep_size, tokens, width // 2)
+            return lax.all_to_all(send, 'ep', 0, 0).reshape(ep_size * tokens, width // 2)
+
         x_f = x_in.astype(F32)
         xn_one, norm_one_pull = jax.vjp(rms_norm, x_f, gain_attn.astype(F32))
+        acts_xn = spread(xn_one)
         qkv_all = mm('bsd,de->bse', xn_one, w_qkv).astype(BF16)
         attn_out, attn_pull = jax.vjp(attn_core, qkv_all)
         attn_proj = mm('bsd,de->bse', attn_out, w_o)
@@ -595,10 +600,7 @@
         rows_own = jnp.concatenate([xn_two, dyc_own], axis=1)
         foreign = [lax.ppermute(rows_own, 'dp', [((z + r) % planes, z) for z in range(planes)]) for r in range(1, planes)]
         d_back, gate_back, recv, d_recv = moe_backward(xn_two, dyc_plane, router_t, w_up, w_lin, w_down, cap, planes)
-        both = jnp.stack([xn_one.reshape(tokens, width), attn_out.reshape(tokens, width)], axis=1)
-        halves = jnp.moveaxis(both.reshape(tokens, 2, 2, width // 2), 2, 0).reshape(1, 2, tokens, width)
-        send = jnp.broadcast_to(after(halves, gate_back), (ep_size // 2, 2, tokens, width)).reshape(ep_size, tokens, width)
-        acts = lax.all_to_all(send, 'ep', 0, 0).reshape(ep_size * tokens, width)
+        acts_ao = spread(after(attn_out, gate_back))
         d_gate_back = gate_back[:, :, :cap].reshape(experts, cap)
 
         select_own = one_hot(codes, cap)
@@ -613,7 +615,7 @@
         d_resid = (d_hidden + dy_own.astype(F32)).astype(BF16).reshape(num_seqs, seq_len, width)
         d_attn_out = mm('bse,de->bsd', d_resid, w_o).astype(BF16)
         d_qkv = attn_pull(d_attn_out)[0]
-        foreign = lax.all_gather(after(jnp.stack(foreign), acts, d_qkv), 'ep')
+        foreign = lax.all_gather(jnp.stack(foreign), 'ep')
         d_xn_one = mm('bse,de->bsd', d_qkv, w_qkv).astype(BF16)
         d_x_norm, grad_gain_attn = norm_one_pull(d_xn_one)
         dx_out = (d_x_norm + d_resid.astype(F32)).astype(BF16)
@@ -621,7 +623,7 @@
         dsend = jnp.concatenate([quarters(d_qkv), quarters(d_resid)], axis=2)
         gains = jnp.concatenate([grad_gain_attn, grad_gain_ffn]).reshape(-1, 128)
         world_size = planes * ep_size
-        low, high, gains, grad_router = dense_sums(acts, dsend, gains, grad_router.reshape(world_size, -1, 128))
+        low, high, gains, grad_router = dense_sums(acts_xn, acts_ao, dsend, gains, grad_router.reshape(world_size, -1, 128))
         grad_router = grad_router.reshape(width, experts)
         grad_gain_attn, grad_gain_ffn = gains.reshape(2, width)
 
@@ -636,8 +638,11 @@
 
         foreign = after(foreign, gains)
         recv, d_recv = dispatch_rows(foreign.reshape(-1, tokens, foreign.shape[-1]), router_t, recv, d_recv, ep_size * cap, cap)
-        grads = weight_grads(recv, d_recv, w_up, w_lin, w_down, 0, local_exp // 2)
-        grad_up, grad_lin, grad_down = weight_grads(recv, d_recv, w_up, w_lin, w_down, local_exp // 2, local_exp // 2, grads)
+        grads, first = (), 0
+        for count in (local_exp // 4, local_exp // 4, local_exp // 2):
+            grads = weight_grads(recv, d_recv, w_up, w_lin, w_down, first, count, grads)
+            first += count
+        grad_up, grad_lin, grad_down = grads
         grad_wqkv, grad_wo = assemble(pieces)
         return (dx_out, grad_gain_attn, grad_wqkv, grad_wo, grad_gain_ffn, grad_router, grad_up, grad_lin, grad_down)
 

time: 1000 us -> 1110 us (1.11)
  Pallas kernels: 532 us -> 634 us
  waiting for transfers between devices: 312 us -> 298 us
    pallas_call x1, Pallas kernels: 125 us -> 272 us  [moe_backward(): pl.pallas_call(functools.partial(moe_kernel, cap), out_shape=(jax.ShapeDt...]
    pallas_call x1, Pallas kernels: 246 us -> 192 us  [dense_sums(): pl.pallas_call(dense_kernel, out_shape=(f32(HALF // 2, width), f32(HALF /...]
    all_gather x1, waiting for transfers between devices: 26.2 us -> 0.01 us  [local(): dyc_plane = lax.all_gather(dyc_own, 'ep')]
    transpose x0 -> x2, local copies, waits for them, and re-layouts: none -> 14.9 us  [spread(): halves = jnp.moveaxis(act.reshape(tokens, 2, width // 2), 1, 0)]
    pallas_call x2 -> x3, Pallas kernels: 108 us -> 116 us  [weight_grads(): pl.pallas_call(weight_kernel, grid=(count,), out_shape=(f32(w_up), f32(w_...]
    unnamed x134 -> x108, local copies, waits for them, and re-layouts: 23 us -> 21.9 us
  transfers between devices with their start and end apart: 20 -> 21, of which waited for: 9 -> 10; matrix products, arithmetic and copies ran while one was open for 9% -> 10% of each run, Pallas kernels for 27% -> 44%
where the time goes in v2:
time: 1110 us; the launch traced here: 1100 us
  Pallas kernels  634 us (57%)
  waiting for transfers between devices  298 us (27%)
  local copies, waits for them, and re-layouts  61.5 us (6%)
  matrix products  55 us (5%)
  starting transfers between devices  21.4 us (2%)
  between operations  15.2 us (1%)
  other arithmetic  14.2 us (1%)
    pallas_call x1, Pallas kernels, moe_backward(): pl.pallas_call(functools.partial(moe_kernel, cap), out_shape=(jax.ShapeDt...  272 us
    pallas_call x1, Pallas kernels, dense_sums(): pl.pallas_call(dense_kernel, out_shape=(f32(HALF // 2, width), f32(HALF /...  192 us
    ppermute x14, waiting for transfers between devices, local(): lax.ppermute(arr, 'ep', [(e, e ^ bit) for e in range(ep_size)])  149 us
    ppermute x3, waiting for transfers between devices, local(): lax.ppermute(rows_own, 'dp', [((z + r) % planes, z) for z in range(planes)])  139 us
    pallas_call x3, Pallas kernels, weight_grads(): pl.pallas_call(weight_kernel, grid=(count,), out_shape=(f32(w_up), f32(w_...  116 us
    dot_general x16, matrix products, mm(): return jnp.einsum(spec, a, b, preferred_element_type=F32)  55 us
    pallas_call x1, Pallas kernels, dispatch_rows(): pl.pallas_call(functools.partial(dispatch_kernel, local_exp, cap), grid=(...  31.6 us
  transfers between devices with their start and end apart: 21, of which 10 were waited for; matrix products, arithmetic and copies ran while one was open for 10% of the time, Pallas kernels for 44%

profile of v2, /device:TPU:0, one launch (start us, length us, event | category | flops | bytes accessed | tf_op | source)
XLA Modules:
  0.0 1098.9 jit_solution(16117298945689411783)
XLA Ops:
  9.2 2.0 concatenate.18
  12.7 10.2 convolution_convert_fusion
  22.9 2.9 copy.112
  34.2 2.1 concatenate.23
  36.3 5.1 collective-permute-start.14
  42.4 35.5 %collective-permute-done.14 = bf16[256,3200]{1,0:T(8,128)(2,1)S(1)} collective-permute-done((bf16[256,3200]{1,0:T(8,128)(2,1)}, bf16[256,3200]{1,0:T(8,128)(2,1)S(1)}, u32[]{:S(2)}, u32[]{:S(2)}) %collective-permute-start.14) | collective-permute-done | bytes 1638432 | tf_op jit(solution)/shard_map/ppermute | solution.py:601
  77.9 103.9 %collective-permute-done.15 = bf16[256,3200]{1,0:T(8,128)(2,1)S(1)} collective-permute-done((bf16[256,3200]{1,0:T(8,128)(2,1)}, bf16[256,3200]{1,0:T(8,128)(2,1)S(1)}, u32[]{:S(2)}, u32[]{:S(2)}) %collective-permute-start.15) | collective-permute-done | bytes 1638432 | tf_op jit(solution)/shard_map/ppermute | solution.py:601
  181.8 2.9 pad_maximum_fusion
  184.7 2.9 reshape.270
  190.8 4.7 all-to-all-start
  199.4 272.2 %moe_backward.1 = (bf16[64,32,1536]{2,1,0:T(8,128)(2,1)}, f32[8,8,128]{2,1,0:T(8,128)}, bf16[8,1024,1536]{2,1,0:T(8,128)(2,1)}, bf16[8,1024,1536]{2,1,0:T(8,128)(2,1)}) custom-call(bf16[256,1536]{1,0:T(8,128)(2,1)} %copy-done.20, bf16[8,256,1664]{2,1,0:T(8,128)(2,1)} %bitcast.171, bf16[64,1536]{1,0:T(8,128)(2,1)} %bitcast.163, bf16[8,1536,512]{2,1,0:T(8,128)(2,1)} %up_ref.7, ...), custom_call_target="tpu_custom_call" | custom-call | flops 60000002048 | bytes 67108864 | tf_op jit(solution)/shard_map/moe_backward/pallas_call | solution.py:499
  473.3 10.1 fusion.9
  485.8 2.3 convolution_convert_fusion.2
  489.5 4.2 fusion.8
  493.8 13.7 %copy.130 = bf16[2,256,768]{2,1,0:T(8,128)(2,1)S(1)} copy(bf16[2,256,768]{1,2,0:T(8,128)(2,1)} %bitcast.162) | data formatting | bytes 1572864 | tf_op jit(solution)/shard_map/transpose | solution.py:587
  507.5 4.4 fusion.40
  513.8 4.6 all-to-all-start.1
  524.5 2.7 fusion.39
  528.8 3.0 copy.131
  531.9 2.3 copy.133
  534.1 11.0 %fusion.24 = (f32[1536]{0:T(1024)S(1)}, f32[256]{0:T(256)S(1)}, f32[256,1536]{1,0:T(8,128)}) fusion(bf16[1,256,1536]{2,1,0:T(8,128)(2,1)} %param.11, f32[256]{0:T(256)S(1)} %copy-done.44, f32[1536]{0:T(1024)S(1)} %convert_element_type.139, bf16[256,4608]{0,1:T(8,128)(2,1)} %bitcast.153, bf16[1536,4608]{1,0:T(8,128)(2,1)} %param.15), kind=kOutput, calls=%fused_computation.49 | convolution fusion | flops 3627415808 | bytes 18888704 | tf_op jit(solution)/shard_map/bse,de->bsd/dot_general | solution.py:20
  547.2 9.1 all-to-all-done.1
  556.2 191.8 %dense_sums.1 = (f32[384,1536]{1,0:T(8,128)S(1)}, f32[384,1536]{1,0:T(8,128)S(1)}, f32[24,128]{1,0:T(8,128)S(1)}, f32[32,24,128]{2,1,0:T(8,128)S(1)}) custom-call(bf16[2048,768]{1,0:T(8,128)(2,1)} %bitcast.39.acts_xn_ref, bf16[2048,768]{1,0:T(8,128)(2,1)} %bitcast.45.acts_ao_ref, bf16[4,256,1536]{2,1,0:T(8,128)(2,1)} %pad_maximum_fusion.1.dsend_ref, ...), custom_call_target="tpu_custom_call" | custom-call | flops 99999997952 | bytes 41943040 | tf_op jit(solution)/shard_map/dense_sums/pallas_call | solution.py:222
  752.2 50.1 %collective-permute-done.2.refs_4_ = f32[384,1536]{1,0:T(8,128)S(1)} collective-permute-done((f32[384,1536]{1,0:T(8,128)S(1)}, f32[384,1536]{1,0:T(8,128)S(1)}, u32[]{:S(2)}, u32[]{:S(2)}) %collective-permute-start.2) | collective-permute-done | bytes 2359328 | tf_op jit(solution)/shard_map/ppermute | solution.py:630
  804.2 47.3 %collective-permute-done.3.refs_5_ = f32[384,1536]{1,0:T(8,128)} collective-permute-done((f32[384,1536]{1,0:T(8,128)S(1)}, f32[384,1536]{1,0:T(8,128)}, u32[]{:S(2)}, u32[]{:S(2)}) %collective-permute-start.3) | collective-permute-done | bytes 2359328 | tf_op jit(solution)/shard_map/ppermute | solution.py:630
  857.7 44.4 %collective-permute-done.10.refs_12_ = f32[384,1536]{1,0:T(8,128)} collective-permute-done((f32[384,1536]{1,0:T(8,128)S(1)}, f32[384,1536]{1,0:T(8,128)}, u32[]{:S(2)}, u32[]{:S(2)}) %collective-permute-start.10) | collective-permute-done | bytes 2359328 | tf_op jit(solution)/shard_map/ppermute | solution.py:630
  910.4 3.4 collective-permute-done.13.refs_15_
  922.1 21.8 %assemble.1 = (f32[1536,4608]{1,0:T(8,128)}, f32[1536,1536]{1,0:T(8,128)}) custom-call(f32[384,1536]{1,0:T(8,128)S(1)} %get-tuple-element.36.refs_0_, f32[384,1536]{1,0:T(8,128)S(1)} %copy-done.1, f32[384,1536]{1,0:T(8,128)S(1)} %copy-done.5, f32[384,1536]{1,0:T(8,128)S(1)} %copy-done.7, f32[384,1536]{1,0:T(8,128)S(1)} %copy-done.3, ...), custom_call_target="tpu_custom_call" | custom-call | flops 20000000000 | bytes 83886080 | tf_op jit(solution)/shard_map/assemble/pallas_call | solution.py:281
  943.9 31.6 %dispatch_rows.1 = (bf16[8,1024,1536]{2,1,0:T(8,128)(2,1)}, bf16[8,1024,1536]{2,1,0:T(8,128)(2,1)}) custom-call(bf16[24,256,3200]{2,1,0:T(8,128)(2,1)} %all-gather.7.cloned.1.call-done, bf16[64,1536]{1,0:T(8,128)(2,1)} %bitcast.164, bf16[8,1024,1536]{2,1,0:T(8,128)(2,1)} %get-tuple-element.42.recv_in, ...), custom_call_target="tpu_custom_call", output_to_operand_aliasing={{0}: (2, {}), {1}: (3, {})} | custom-call | flops 9663676416 | bytes 75497472 | tf_op jit(solution)/shard_map/dispatch_rows/pallas_call | solution.py:346
  975.6 30.9 %weight_grads.3 = (f32[8,1536,512]{2,1,0:T(8,128)}, f32[8,1536,512]{2,1,0:T(8,128)}, f32[8,512,1536]{2,1,0:T(8,128)}) custom-call(bf16[8,1024,1536]{2,1,0:T(8,128)(2,1)} %get-tuple-element.44.recv_ref, bf16[8,1024,1536]{2,1,0:T(8,128)(2,1)} %get-tuple-element.45.d_recv_ref, bf16[8,1536,512]{2,1,0:T(8,128)(2,1)} %up_ref.7, bf16[8,1536,512]{2,1,0:T(8,128)(2,1)} %lin_ref.7, ...), custom_call_target="tpu_custom_call" | custom-call | flops 19327352832 | bytes 41943040 | tf_op jit(solution)/shard_map/weight_grads/pallas_call | solution.py:550
  1006.5 30.9 %weight_grads.4 = (f32[8,1536,512]{2,1,0:T(8,128)}, f32[8,1536,512]{2,1,0:T(8,128)}, f32[8,512,1536]{2,1,0:T(8,128)}) custom-call(bf16[8,1024,1536]{2,1,0:T(8,128)(2,1)} %get-tuple-element.44.recv_ref, bf16[8,1024,1536]{2,1,0:T(8,128)(2,1)} %get-tuple-element.45.d_recv_ref, ...), custom_call_target="tpu_custom_call", output_to_operand_aliasing={{0}: (5, {}), {1}: (6, {}), {2}: (7, {})} | custom-call | flops 19327352832 | bytes 41943040 | tf_op jit(solution)/shard_map/weight_grads/pallas_call | solution.py:550
  1037.4 54.2 %weight_grads.5 = (f32[8,1536,512]{2,1,0:T(8,128)}, f32[8,1536,512]{2,1,0:T(8,128)}, f32[8,512,1536]{2,1,0:T(8,128)}) custom-call(bf16[8,1024,1536]{2,1,0:T(8,128)(2,1)} %get-tuple-element.44.recv_ref, bf16[8,1024,1536]{2,1,0:T(8,128)(2,1)} %get-tuple-element.45.d_recv_ref, ...), custom_call_target="tpu_custom_call", output_to_operand_aliasing={{0}: (5, {}), {1}: (6, {}), {2}: (7, {})} | custom-call | flops 38654705664 | bytes 83886080 | tf_op jit(solution)/shard_map/weight_grads/pallas_call | solution.py:550
  (193 shorter events, 65.4 us)
Async XLA Ops:
  7.2 192.2 %all-gather.5.cloned.1.call-start = ((), (), s32[]{:S(2)}) async-start(), calls=%async_computation.2 | async-start | bytes 7667712 | tf_op jit(solution)/shard_map/all_gather | solution.py:582
  11.2 932.7 %all-gather.7.cloned.1.call-start = ((), (), s32[]{:S(2)}) async-start(), calls=%async_computation.3 | async-start | bytes 44236800 | tf_op jit(solution)/shard_map/all_gather | solution.py:618
  11.6 11.4 %copy-start.41 = (f32[256]{0:T(256)}, f32[256]{0:T(256)S(1)}, u32[]{:S(2)}) copy-start(f32[256]{0:T(256)S(1)} %fusion.33) | copy-start | bytes 3076
  11.6 11.4 %copy-start.43 = (f32[256]{0:T(256)}, f32[256]{0:T(256)S(1)}, u32[]{:S(2)}) copy-start(f32[256]{0:T(256)S(1)} %fusion.57) | copy-start | bytes 3076
  34.2 161.3 %copy-start.20 = (bf16[256,1536]{1,0:T(8,128)(2,1)}, bf16[256,1536]{1,0:T(8,128)(2,1)S(1)}, u32[]{:S(2)}) copy-start(bf16[256,1536]{1,0:T(8,128)(2,1)S(1)} %fusion.25.xn_ref) | copy-start | bytes 2359300
  36.3 41.6 %collective-permute-start.14 = (bf16[256,3200]{1,0:T(8,128)(2,1)}, bf16[256,3200]{1,0:T(8,128)(2,1)S(1)}, u32[]{:S(2)}, u32[]{:S(2)}) collective-permute-start(bf16[256,3200]{1,0:T(8,128)(2,1)} %concatenate.23), channel_id=1, source_target_pairs={{8,0},{16,8},{24,16},{0,24},{9,1},{17,9},{25,17},{1,25},{10,2},{18... | collective-permute-start | bytes 4915208 | tf_op jit(solution)/shard_map/ppermute | solution.py:601
  41.3 140.5 %collective-permute-start.15 = (bf16[256,3200]{1,0:T(8,128)(2,1)}, bf16[256,3200]{1,0:T(8,128)(2,1)S(1)}, u32[]{:S(2)}, u32[]{:S(2)}) collective-permute-start(bf16[256,3200]{1,0:T(8,128)(2,1)} %concatenate.23), channel_id=1, source_target_pairs={{16,0},{24,8},{0,16},{8,24},{17,1},{25,9},{1,17},{9,25},{18,2},{26... | collective-permute-start | bytes 4915208 | tf_op jit(solution)/shard_map/ppermute | solution.py:601
  41.3 140.5 %collective-permute-start.16 = (bf16[256,3200]{1,0:T(8,128)(2,1)}, bf16[256,3200]{1,0:T(8,128)(2,1)S(1)}, u32[]{:S(2)}, u32[]{:S(2)}) collective-permute-start(bf16[256,3200]{1,0:T(8,128)(2,1)} %concatenate.23), channel_id=1, source_target_pairs={{24,0},{0,8},{8,16},{16,24},{25,1},{1,9},{9,17},{17,25},{26,2},{2,... | collective-permute-start | bytes 4915208 | tf_op jit(solution)/shard_map/ppermute | solution.py:601
  190.8 321.1 %all-to-all-start = ((bf16[8,256,768]{2,1,0:T(8,128)(2,1)}), bf16[8,256,768]{2,1,0:T(8,128)(2,1)}, u32[]{:S(2)}, u32[]{:S(2)}) async-start(bf16[8,256,768]{2,1,0:T(8,128)(2,1)} %bitcast.149), calls=%async_computation | async-start | bytes 6291456 | tf_op jit(solution)/shard_map/all_to_all | solution.py:589
  199.4 273.6 %copy-start.35 = (f32[256]{0:T(256)S(1)}, f32[256]{0:T(256)}, u32[]{:S(2)}) copy-start(f32[256]{0:T(256)} %get-tuple-element.106) | copy-start | bytes 3076
  485.8 34.1 %copy-start.13 = (bf16[256,1536]{1,0:T(8,128)(2,1)}, bf16[256,1536]{1,0:T(8,128)(2,1)S(1)}, u32[]{:S(2)}) copy-start(bf16[256,1536]{1,0:T(8,128)(2,1)S(1)} %fusion.28) | copy-start | bytes 2359300
  489.5 18.0 %copy-start.32 = (f32[12,256]{1,0:T(8,128)S(1)}, f32[12,256]{1,0:T(8,128)}, u32[]{:S(2)}) copy-start(f32[12,256]{1,0:T(8,128)} %copy-done.31) | copy-start | bytes 36868
  493.8 18.1 %copy-start.37 = (f32[12,256]{1,0:T(8,128)}, f32[12,256]{1,0:T(8,128)S(1)}, u32[]{:S(2)}) copy-start(f32[12,256]{1,0:T(8,128)S(1)} %neg.7) | copy-start | bytes 36868
  513.8 42.5 %all-to-all-start.1 = ((bf16[8,256,768]{2,1,0:T(8,128)(2,1)}), bf16[8,256,768]{2,1,0:T(8,128)(2,1)}, u32[]{:S(2)}, u32[]{:S(2)}) async-start(bf16[8,256,768]{2,1,0:T(8,128)(2,1)} %bitcast.150), calls=%async_computation.1 | async-start | bytes 6291456 | tf_op jit(solution)/shard_map/all_to_all | solution.py:589
  556.2 349.4 %copy-start.42 = (f32[256]{0:T(256)S(1)}, f32[256]{0:T(256)}, u32[]{:S(2)}) copy-start(f32[256]{0:T(256)} %copy-done.41) | copy-start | bytes 3076
  556.2 349.4 %copy-start.14 = (bf16[256,1536]{1,0:T(8,128)(2,1)S(1)}, bf16[256,1536]{1,0:T(8,128)(2,1)}, u32[]{:S(2)}) copy-start(bf16[256,1536]{1,0:T(8,128)(2,1)} %copy-done.13) | copy-start | bytes 2359300
  556.2 349.4 %copy-start.18 = (bf16[1,256,1536]{2,1,0:T(8,128)(2,1)S(1)}, bf16[1,256,1536]{2,1,0:T(8,128)(2,1)}, u32[]{:S(2)}) copy-start(bf16[1,256,1536]{2,1,0:T(8,128)(2,1)} %param.11) | copy-start | bytes 2359300
  556.2 349.4 %copy-start.29 = (f32[256,1536]{1,0:T(8,128)S(1)}, f32[256,1536]{1,0:T(8,128)}, u32[]{:S(2)}) copy-start(f32[256,1536]{1,0:T(8,128)} %get-tuple-element.111) | copy-start | bytes 4718596
  748.1 54.2 %collective-permute-start.2 = (f32[384,1536]{1,0:T(8,128)S(1)}, f32[384,1536]{1,0:T(8,128)S(1)}, u32[]{:S(2)}, u32[]{:S(2)}) collective-permute-start(f32[384,1536]{1,0:T(8,128)S(1)} %get-tuple-element.36.refs_0_), channel_id=1, source_target_pairs={{0,2},{1,3},{2,0},{3,1},{4,6},{5,7},{6,4},{7,5},{8,10},{9,11},{10,... | collective-permute-start | bytes 7077896 | tf_op jit(solution)/shard_map/ppermute | solution.py:630
  748.2 55.5 %collective-permute-start.7 = (f32[384,1536]{1,0:T(8,128)S(1)}, f32[384,1536]{1,0:T(8,128)}, u32[]{:S(2)}, u32[]{:S(2)}) collective-permute-start(f32[384,1536]{1,0:T(8,128)S(1)} %get-tuple-element.37.refs_1_), channel_id=1, source_target_pairs={{0,4},{1,5},{2,6},{3,7},{4,0},{5,1},{6,2},{7,3},{8,12},{9,13},{10,... | collective-permute-start | bytes 7077896 | tf_op jit(solution)/shard_map/ppermute | solution.py:630
  748.7 102.8 %collective-permute-start.3 = (f32[384,1536]{1,0:T(8,128)S(1)}, f32[384,1536]{1,0:T(8,128)}, u32[]{:S(2)}, u32[]{:S(2)}) collective-permute-start(f32[384,1536]{1,0:T(8,128)S(1)} %get-tuple-element.37.refs_1_), channel_id=1, source_target_pairs={{0,2},{1,3},{2,0},{3,1},{4,6},{5,7},{6,4},{7,5},{8,10},{9,11},{10,... | collective-permute-start | bytes 7077896 | tf_op jit(solution)/shard_map/ppermute | solution.py:630
  750.7 102.3 %collective-permute-start.6 = (f32[384,1536]{1,0:T(8,128)S(1)}, f32[384,1536]{1,0:T(8,128)}, u32[]{:S(2)}, u32[]{:S(2)}) collective-permute-start(f32[384,1536]{1,0:T(8,128)S(1)} %get-tuple-element.36.refs_0_), channel_id=1, source_target_pairs={{0,4},{1,5},{2,6},{3,7},{4,0},{5,1},{6,2},{7,3},{8,12},{9,13},{10,... | collective-permute-start | bytes 7077896 | tf_op jit(solution)/shard_map/ppermute | solution.py:630
  752.2 102.2 %collective-permute-start = (f32[384,1536]{1,0:T(8,128)S(1)}, f32[384,1536]{1,0:T(8,128)S(1)}, u32[]{:S(2)}, u32[]{:S(2)}) collective-permute-start(f32[384,1536]{1,0:T(8,128)S(1)} %get-tuple-element.36.refs_0_), channel_id=1, source_target_pairs={{0,1},{1,0},{2,3},{3,2},{4,5},{5,4},{6,7},{7,6},{8,9},{9,8},{10,11... | collective-permute-start | bytes 7077896 | tf_op jit(solution)/shard_map/ppermute | solution.py:630
  802.3 54.1 %collective-permute-start.1 = (f32[384,1536]{1,0:T(8,128)S(1)}, f32[384,1536]{1,0:T(8,128)S(1)}, u32[]{:S(2)}, u32[]{:S(2)}) collective-permute-start(f32[384,1536]{1,0:T(8,128)S(1)} %get-tuple-element.37.refs_1_), channel_id=1, source_target_pairs={{0,1},{1,0},{2,3},{3,2},{4,5},{5,4},{6,7},{7,6},{8,9},{9,8},{10,11... | collective-permute-start | bytes 7077896 | tf_op jit(solution)/shard_map/ppermute | solution.py:630
  803.7 98.5 %collective-permute-start.10 = (f32[384,1536]{1,0:T(8,128)S(1)}, f32[384,1536]{1,0:T(8,128)}, u32[]{:S(2)}, u32[]{:S(2)}) collective-permute-start(f32[384,1536]{1,0:T(8,128)S(1)} %collective-permute-done.2.refs_4_), channel_id=1, source_target_pairs={{0,4},{1,5},{2,6},{3,7},{4,0},{5,1},{6,2},{7,3},{8,12},{9,13},{10,... | collective-permute-start | bytes 7077896 | tf_op jit(solution)/shard_map/ppermute | solution.py:630
  851.5 52.2 %collective-permute-start.11 = (f32[384,1536]{1,0:T(8,128)}, f32[384,1536]{1,0:T(8,128)}, u32[]{:S(2)}, u32[]{:S(2)}) collective-permute-start(f32[384,1536]{1,0:T(8,128)} %collective-permute-done.7.refs_9_), channel_id=1, source_target_pairs={{0,2},{1,3},{2,0},{3,1},{4,6},{5,7},{6,4},{7,5},{8,10},{9,11},{10,... | collective-permute-start | bytes 7077896 | tf_op jit(solution)/shard_map/ppermute | solution.py:630
  853.0 50.7 %collective-permute-start.4 = (f32[384,1536]{1,0:T(8,128)S(1)}, f32[384,1536]{1,0:T(8,128)S(1)}, u32[]{:S(2)}, u32[]{:S(2)}) collective-permute-start(f32[384,1536]{1,0:T(8,128)S(1)} %collective-permute-done.2.refs_4_), channel_id=1, source_target_pairs={{0,1},{1,0},{2,3},{3,2},{4,5},{5,4},{6,7},{7,6},{8,9},{9,8},{10,11... | collective-permute-start | bytes 7077896 | tf_op jit(solution)/shard_map/ppermute | solution.py:630
  855.8 53.0 %collective-permute-start.9 = (f32[384,1536]{1,0:T(8,128)}, f32[384,1536]{1,0:T(8,128)}, u32[]{:S(2)}, u32[]{:S(2)}) collective-permute-start(f32[384,1536]{1,0:T(8,128)} %collective-permute-done.7.refs_9_), channel_id=1, source_target_pairs={{0,1},{1,0},{2,3},{3,2},{4,5},{5,4},{6,7},{7,6},{8,9},{9,8},{10,11... | collective-permute-start | bytes 7077896 | tf_op jit(solution)/shard_map/ppermute | solution.py:630
  857.7 51.1 %collective-permute-start.5 = (f32[384,1536]{1,0:T(8,128)}, f32[384,1536]{1,0:T(8,128)}, u32[]{:S(2)}, u32[]{:S(2)}) collective-permute-start(f32[384,1536]{1,0:T(8,128)} %collective-permute-done.3.refs_5_), channel_id=1, source_target_pairs={{0,1},{1,0},{2,3},{3,2},{4,5},{5,4},{6,7},{7,6},{8,9},{9,8},{10,11... | collective-permute-start | bytes 7077896 | tf_op jit(solution)/shard_map/ppermute | solution.py:630
  902.1 6.7 collective-permute-start.8
  903.7 6.7 collective-permute-start.12
  905.1 8.7 collective-permute-start.13
  (42 other events, 138.1 us)
Sparse Core Ops, SparseCore 0:
  11.4 50.3 all-gather.4
  184.9 311.7 all-gather.6

commit v3 on v2

--- a/solution.py
+++ b/solution.py
@@ -78,8 +78,9 @@
 
 
 def dense_kernel(acts_xn_ref, acts_ao_ref, dsend_ref, gains_ref, router_ref, low_ref, high_ref, gains_out_ref, router_out_ref,
-                 dall, part, z_in, total, gain_buf, router_buf,
-                 d_send, d_recv, dp_send, dp_recv, z_send, z_recv, own_sem, g_send, g_recv, r_send, r_recv, s_send, s_recv):
+                 dall, stage, part, z_in, total, gain_buf, router_buf,
+                 d_send, d_recv, h_send, h_recv, o_send, o_recv, dp_send, dp_recv, z_send, z_recv, own_sem,
+                 g_send, g_recv, r_send, r_recv, s_send, s_recv):
     z = lax.axis_index('dp')
     ep = lax.axis_index('ep')
     core = lax.rem(ep, 2)
@@ -102,8 +103,22 @@
 
     rows_of = lambda e: pl.ds(pl.multiple_of(e * tokens, tokens), tokens)
     far = (x_dev, y_dev, xy_dev)
-    for i, dev in enumerate(far):
-        copy(dsend_ref.at[dev // 2], dall.at[rows_of(ep)], d_send.at[i], d_recv.at[i], z, dev).start()
+    halves = pl.ds(0, tokens // 2), pl.ds(tokens // 2, tokens // 2)
+    direct = lambda i: copy(dsend_ref.at[far[i] // 2], dall.at[rows_of(ep)], d_send.at[i], d_recv.at[i], z, far[i])
+    hop = lambda n: copy(dsend_ref.at[xy_dev // 2, halves[n], :], stage.at[n], h_send.at[n], h_recv.at[n], z, far[n])
+
+    def onward(n):
+        at = pl.ds(pl.multiple_of(far[n] * tokens + n * (tokens // 2), tokens // 2), tokens // 2)
+        return copy(stage.at[n], dall.at[at], o_send.at[n], o_recv.at[n], z, far[1 - n])
+
+    def landed(n):
+        at = pl.ds(pl.multiple_of(xy_dev * tokens + n * (tokens // 2), tokens // 2), tokens // 2)
+        return copy(stage.at[n], dall.at[at], o_send.at[n], o_recv.at[n], z, far[1 - n])
+
+    for n in range(2):
+        hop(n).start()
+    for i in range(2):
+        direct(i).start()
     copy(dsend_ref.at[quarter], dall.at[rows_of(ep)], dp_send.at[3], dp_recv.at[3], z, partner).start()
 
     world = router_ref.shape[0]
@@ -115,14 +130,14 @@
     def push_all(*args):
         def body(d, _):
             push(*args, d, lax.rem(me + d, world)).start()
-            return 0
+            return _
 
         lax.fori_loop(1, world, body, 0)
 
     def wait_all(pick, buf, s_sem, r_sem):
         def body(d, _):
             push(pick, buf, s_sem, r_sem, d, lax.rem(me + d, world)).wait()
-            return 0
+            return _
 
         lax.fori_loop(1, world, body, 0)
 
@@ -136,9 +151,16 @@
     push_all(*share_push)
 
     dall[rows_of(ep), :] = dsend_ref[quarter]
-    for i, dev in enumerate(far):
-        copy(dsend_ref.at[dev // 2], dall.at[rows_of(dev)], d_send.at[i], d_recv.at[i], z, dev).wait_recv()
-        copy(dall.at[rows_of(dev)], dall.at[rows_of(dev)], dp_send.at[i], dp_recv.at[i], z, partner).start()
+    to_core = lambda i: copy(dall.at[rows_of(far[i])], dall.at[rows_of(far[i])], dp_send.at[i], dp_recv.at[i], z, partner)
+    for n in range(2):
+        hop(n).wait_recv()
+        onward(n).start()
+    for i in range(2):
+        copy(dsend_ref.at[0], dall.at[rows_of(far[i])], d_send.at[i], d_recv.at[i], z, far[i]).wait_recv()
+        to_core(i).start()
+    for n in range(2):
+        landed(n).wait_recv()
+    to_core(2).start()
     for i, dev in enumerate(far + (ep,)):
         other = dev + 1 - 2 * core
         copy(dsend_ref.at[0], dall.at[rows_of(other)], dp_send.at[i], dp_recv.at[i], z, partner).wait_recv()
@@ -201,9 +223,12 @@
         for k in range(STEPS):
             up_copy(k).wait_send()
 
-    for i, dev in enumerate(far):
-        copy(dsend_ref.at[dev // 2], dall.at[rows_of(ep)], d_send.at[i], d_recv.at[i], z, dev).wait_send()
-        copy(dall.at[rows_of(dev)], dall.at[rows_of(dev)], dp_send.at[i], dp_recv.at[i], z, partner).wait_send()
+    for n in range(2):
+        direct(n).wait_send()
+        hop(n).wait_send()
+        onward(n).wait_send()
+    for i in range(3):
+        to_core(i).wait_send()
     copy(dsend_ref.at[quarter], dall.at[rows_of(ep)], dp_send.at[3], dp_recv.at[3], z, partner).wait_send()
 
     wait_all(*gain_push)
@@ -226,12 +251,13 @@
         out_specs=(any_spec, any_spec, vmem, vmem),
         scratch_shapes=[
             pltpu.VMEM((rows, width), jnp.bfloat16),
+            pltpu.VMEM((2, dsend.shape[1] // 2, width), jnp.bfloat16),
             pltpu.VMEM((STEPS, CHUNK, width), jnp.float32),
             pltpu.VMEM((STEPS, CHUNK, width), jnp.float32),
             pltpu.VMEM((STEPS, CHUNK, width), jnp.float32),
             pltpu.VMEM((world,) + gains.shape, jnp.float32),
             pltpu.VMEM(router.shape, jnp.float32),
-            dma((3,)), dma((3,)), dma((4,)), dma((4,)), dma((3, STEPS)), dma((3, STEPS)), dma((STEPS,)),
+            *[dma((2,))] * 6, *[dma((4,))] * 2, dma((3, STEPS)), dma((3, STEPS)), dma((STEPS,)),
             dma((world,)), dma((world,)), dma((world,)), dma((world,)), dma((world,)), dma((world,)),
         ],
         compiler_params=pltpu.CompilerParams(has_side_effects=True, vmem_limit_bytes=48 << 20),
@@ -368,14 +394,14 @@
     return (act * v).astype(BF16), d_u.astype(BF16), (d_act * act).astype(BF16)
 
 
-def moe_kernel(cap, xn_ref, dyc_ref, router_ref, up_ref, lin_ref, down_ref, back_ref, gate_back_ref, recv_out, d_recv_out,
-               xn_all, recv, d_recv, dy_rows, d_tok, gate_send, up_buf, lin_buf, down_buf, codes_buf, gates_buf,
-               w_sem, x_send, x_recv, p_send, p_recv, own_sem, row_sem, b_send, b_recv, g_send, g_recv):
+def moe_kernel(cap, own_ref, router_ref, up_ref, lin_ref, down_ref, back_ref, gate_back_ref, recv_out, d_recv_out, hid_out,
+               all_rows, recv, d_recv, dy_rows, d_tok, hid_buf, gate_send, up_buf, lin_buf, down_buf, codes_buf, gates_buf,
+               w_sem, x_send, x_recv, p_send, p_recv, own_sem, row_sem, hid_sem, b_send, b_recv, g_send, g_recv):
     z = lax.axis_index('dp')
     ep = lax.axis_index('ep')
     local_exp = up_ref.shape[0]
-    plane = xn_all.shape[0]
-    width = xn_ref.shape[1]
+    plane = all_rows.shape[0]
+    width = router_ref.shape[1]
     first = pl.multiple_of(ep * local_exp, local_exp)
     bits = (lax.rem(ep, 2), lax.rem(ep // 2, 2), ep // 4)
 
@@ -392,26 +418,44 @@
         return [pltpu.make_async_copy(src.at[e], dst.at[slot], w_sem.at[i, slot])
                 for i, (src, dst) in enumerate(((up_ref, up_buf), (lin_ref, lin_buf), (down_ref, down_buf)))]
 
-    for i in (1, 2, 3):
-        copy(xn_ref, xn_all.at[ep], x_send.at[i], x_recv.at[i], flipped(2 * i)).start()
-    copy(xn_ref, xn_all.at[ep], p_send.at[0], p_recv.at[0], flipped(1)).start()
+    for i in (1, 2):
+        copy(own_ref, all_rows.at[ep], x_send.at[i], x_recv.at[i], flipped(2 * i)).start()
+    copy(own_ref, all_rows.at[ep], p_send.at[0], p_recv.at[0], flipped(1)).start()
+    part = pl.ds(0, own_ref.shape[0] // 2), pl.ds(own_ref.shape[0] // 2, own_ref.shape[0] // 2)
+
+    def relay(n, src, dst):
+        ref = all_rows.at[src, part[n], :]
+        return copy(ref, ref, x_send.at[3 * n], x_recv.at[3 * n], dst)
+
+    def share(i):
+        ref = all_rows.at[flipped(2 * i)]
+        return copy(ref, ref, p_send.at[i], p_recv.at[i], flipped(1))
+
     for c in weights(0, 0):
         c.start()
-    xn_all[ep] = xn_ref[...]
+    all_rows[ep] = own_ref[...]
     router = router_ref[...]
 
     def pair(i, _):
         near = flipped(2 * i)
         other = flipped(2 * i + 1)
 
-        @pl.when(i > 0)
+        @pl.when(i == 1)
         def _():
-            copy(xn_ref, xn_all.at[near], x_send.at[i], x_recv.at[i], near).wait_recv()
-            copy(xn_all.at[near], xn_all.at[near], p_send.at[i], p_recv.at[i], flipped(1)).start()
-
-        copy(xn_ref, xn_all.at[other], p_send.at[i], p_recv.at[i], flipped(1)).wait_recv()
+            for n in (1, 2):
+                copy(own_ref, all_rows.at[flipped(2 * n)], x_send.at[n], x_recv.at[n], flipped(2 * n)).wait_recv()
+                relay(n - 1, flipped(2 * n), flipped(6 - 2 * n)).start()
+                share(n).start()
+
+        @pl.when(i == 3)
+        def _():
+            relay(0, flipped(6), flipped(4)).wait_recv()
+            relay(1, flipped(6), flipped(2)).wait_recv()
+            share(3).start()
+
+        copy(own_ref, all_rows.at[other], p_send.at[i], p_recv.at[i], flipped(1)).wait_recv()
         for j, src in enumerate((near, other)):
-            rows, dy, gate_slot = slot_rows(xn_all[src], dyc_ref[src], router, first, local_exp, cap, codes_buf.at[j], gates_buf.at[j])
+            rows, dy, gate_slot = slot_rows(all_rows[src, :, :width], all_rows[src, :, width:], router, first, local_exp, cap, codes_buf.at[j], gates_buf.at[j])
             at = pl.ds(pl.multiple_of(src * cap, cap), cap)
             recv[:, at, :] = rows.reshape(local_exp, cap, width)
             dy_rows[:, at, :] = dy.astype(BF16).reshape(local_exp, cap, width)
@@ -433,6 +477,9 @@
     def stay(e):
         return pltpu.make_async_copy(d_tok.at[e, pl.ds(pl.multiple_of(ep * cap, cap), cap), :], back_ref.at[first + e], own_sem.at[e])
 
+    def save(e):
+        return pltpu.make_async_copy(hid_buf.at[lax.rem(e, 2)], hid_out.at[e], hid_sem.at[lax.rem(e, 2)])
+
     def expert(e, _):
         slot = lax.rem(e, 2)
 
@@ -445,6 +492,13 @@
             c.wait()
         up, lin, down = up_buf[slot], lin_buf[slot], down_buf[slot]
         act, d_u, d_v = hidden_grads(recv[e], d_recv[e], up, lin, down)
+
+        @pl.when(e >= 2)
+        def _():
+            save(e - 2).wait()
+
+        for i, value in enumerate((act, d_u, d_v)):
+            hid_buf[slot, i] = value
         d_tok[e] = (dot_nt(d_u, up) + dot_nt(d_v, lin)).astype(BF16)
         y = dot_nn(act, down).astype(BF16).astype(F32)
         d_gate = jnp.sum(dy_rows[e].astype(F32) * y, axis=-1, keepdims=True)
@@ -455,9 +509,12 @@
         for d in (6, 7, 2, 3, 4, 5, 1):
             home(d, e).start()
         stay(e).start()
+        save(e).start()
         return 0
 
     lax.fori_loop(0, local_exp, expert, 0)
+    for e in (local_exp - 2, local_exp - 1):
+        save(e).wait()
 
     for c in keep:
         c.wait()
@@ -482,16 +539,19 @@
     for d in range(1, plane):
         copy(gate_send.at[0], gate_back_ref.at[flipped(d)], g_send.at[d], g_recv.at[d], flipped(d)).wait_recv()
         gate_home(d).wait_send()
+    for i in (1, 2):
+        copy(own_ref, all_rows.at[ep], x_send.at[i], x_recv.at[i], flipped(2 * i)).wait_send()
+        relay(i - 1, flipped(2 * i), flipped(6 - 2 * i)).wait_send()
     for i in (1, 2, 3):
-        copy(xn_ref, xn_all.at[ep], x_send.at[i], x_recv.at[i], flipped(2 * i)).wait_send()
-        copy(xn_all.at[flipped(2 * i)], xn_all.at[flipped(2 * i)], p_send.at[i], p_recv.at[i], flipped(1)).wait_send()
-    copy(xn_ref, xn_all.at[ep], p_send.at[0], p_recv.at[0], flipped(1)).wait_send()
-
-
-def moe_backward(xn, dyc_plane, router_t, w_up, w_lin, w_down, cap, planes):
-    plane, tokens = dyc_plane.shape[:2]
+        share(i).wait_send()
+    copy(own_ref, all_rows.at[ep], p_send.at[0], p_recv.at[0], flipped(1)).wait_send()
+
+
+def moe_backward(rows_own, router_t, w_up, w_lin, w_down, cap, planes):
+    tokens, lanes = rows_own.shape
     local_exp, width, hid = w_up.shape
     experts = router_t.shape[0]
+    plane = experts // local_exp
     rows = pltpu.VMEM((local_exp, plane * cap, width), BF16)
     vmem = pl.BlockSpec(memory_space=pltpu.VMEM)
     any_spec = pl.BlockSpec(memory_space=pl.ANY)
@@ -500,28 +560,32 @@
         functools.partial(moe_kernel, cap),
         out_shape=(jax.ShapeDtypeStruct((experts, cap, width), BF16), jax.ShapeDtypeStruct((plane, local_exp, 128), F32),
                    jax.ShapeDtypeStruct((local_exp, planes * plane * cap, width), BF16),
-                   jax.ShapeDtypeStruct((local_exp, planes * plane * cap, width), BF16)),
-        in_specs=[vmem, vmem, vmem, any_spec, any_spec, any_spec],
-        out_specs=(any_spec, vmem, any_spec, any_spec),
+                   jax.ShapeDtypeStruct((local_exp, planes * plane * cap, width), BF16),
+                   jax.ShapeDtypeStruct((local_exp, 3, plane * cap, hid), BF16)),
+        in_specs=[vmem, vmem, any_spec, any_spec, any_spec],
+        out_specs=(any_spec, vmem, any_spec, any_spec, any_spec),
         scratch_shapes=[
-            pltpu.VMEM((plane, tokens, width), BF16), rows, rows, rows, rows, pltpu.VMEM((plane, local_exp, 128), F32),
+            pltpu.VMEM((plane, tokens, lanes), BF16), rows, rows, rows, rows, pltpu.VMEM((2, 3, plane * cap, hid), BF16), pltpu.VMEM((plane, local_exp, 128), F32),
             pltpu.VMEM((2, width, hid), BF16), pltpu.VMEM((2, width, hid), BF16), pltpu.VMEM((2, hid, width), BF16),
             pltpu.VMEM((2, experts, tokens), F32), pltpu.VMEM((2, experts, tokens), F32),
-            dma((3, 2)), dma((4,)), dma((4,)), dma((4,)), dma((4,)), dma((local_exp,)), dma((2,)),
+            dma((3, 2)), *[dma((4,))] * 4, dma((local_exp,)), dma((2,)), dma((2,)),
             dma((plane, local_exp)), dma((plane, local_exp)), dma((plane,)), dma((plane,)),
         ],
         compiler_params=pltpu.CompilerParams(has_side_effects=True, vmem_limit_bytes=60 << 20),
         cost_estimate=pl.CostEstimate(flops=60 * 10**9, bytes_accessed=64 << 20, transcendentals=0),
         name='moe_backward',
-    )(xn, dyc_plane, router_t, w_up, w_lin, w_down)
-
-
-def weight_kernel(recv_ref, d_recv_ref, up_ref, lin_ref, down_ref, *rest):
+    )(rows_own, router_t, w_up, w_lin, w_down)
+
+
+def weight_kernel(recv_ref, d_recv_ref, hid_ref, up_ref, lin_ref, down_ref, *rest):
     g_up_ref, g_lin_ref, g_down_ref, act_buf, du_buf, dv_buf = rest[-6:]
     total = recv_ref.shape[1]
+    own = hid_ref.shape[2]
+    for i, buf in enumerate((act_buf, du_buf, dv_buf)):
+        buf[:own, :] = hid_ref[0, i]
     block = 256
 
-    @pl.loop(0, total // block)
+    @pl.loop(own // block, total // block)
     def _(i):
         rows = pl.ds(pl.multiple_of(i * block, block), block)
         act, d_u, d_v = hidden_grads(recv_ref[0, rows, :], d_recv_ref[0, rows, :], up_ref[0], lin_ref[0], down_ref[0])
@@ -540,7 +604,7 @@
         g_down_ref[0, :, c] = dot_tn(act_buf[...], d_recv_ref[0, :, c])
 
 
-def weight_grads(recv, d_recv, w_up, w_lin, w_down, first, count, grads=()):
+def weight_grads(recv, d_recv, hid_own, w_up, w_lin, w_down, first, count, grads=()):
     _, total, width = recv.shape
     hid = w_up.shape[2]
     rows = pl.BlockSpec((1, total, width), lambda e: (first + e, 0, 0))
@@ -551,14 +615,15 @@
         weight_kernel,
         grid=(count,),
         out_shape=(f32(w_up), f32(w_lin), f32(w_down)),
-        in_specs=[rows, rows, wide, wide, tall] + [pl.BlockSpec(memory_space=pl.ANY)] * len(grads),
+        in_specs=[rows, rows, pl.BlockSpec((1,) + hid_own.shape[1:], lambda e: (first + e, 0, 0, 0)), wide, wide, tall]
+        + [pl.BlockSpec(memory_space=pl.ANY)] * len(grads),
         out_specs=(wide, wide, tall),
         scratch_shapes=[pltpu.VMEM((total, hid), BF16)] * 3,
-        input_output_aliases={5 + i: i for i in range(len(grads))},
+        input_output_aliases={6 + i: i for i in range(len(grads))},
         compiler_params=pltpu.CompilerParams(vmem_limit_bytes=60 << 20),
         cost_estimate=pl.CostEstimate(flops=12 * count * total * width * hid, transcendentals=0, bytes_accessed=count * (20 << 20)),
         name='weight_grads',
-    )(recv, d_recv, w_up, w_lin, w_down, *grads)
+    )(recv, d_recv, hid_own, w_up, w_lin, w_down, *grads)
 
 
 def solution(mesh):
@@ -579,7 +644,6 @@
         dy_own = dy_in.reshape(tokens, width)
         lanes = jnp.zeros((tokens, HEAD - experts), BF16)
         dyc_own = jnp.concatenate([dy_own, codes.T, lanes], axis=1)
-        dyc_plane = lax.all_gather(dyc_own, 'ep')
         router_t = w_router.T
         planes = mesh.shape['dp']
 
@@ -599,7 +663,7 @@
 
         rows_own = jnp.concatenate([xn_two, dyc_own], axis=1)
         foreign = [lax.ppermute(rows_own, 'dp', [((z + r) % planes, z) for z in range(planes)]) for r in range(1, planes)]
-        d_back, gate_back, recv, d_recv = moe_backward(xn_two, dyc_plane, router_t, w_up, w_lin, w_down, cap, planes)
+        d_back, gate_back, recv, d_recv, hid_own = moe_backward(rows_own, router_t, w_up, w_lin, w_down, cap, planes)
         acts_ao = spread(after(attn_out, gate_back))
         d_gate_back = gate_back[:, :, :cap].reshape(experts, cap)
 
@@ -640,7 +704,7 @@
         recv, d_recv = dispatch_rows(foreign.reshape(-1, tokens, foreign.shape[-1]), router_t, recv, d_recv, ep_size * cap, cap)
         grads, first = (), 0
         for count in (local_exp // 4, local_exp // 4, local_exp // 2):
-            grads = weight_grads(recv, d_recv, w_up, w_lin, w_down, first, count, grads)
+            grads = weight_grads(recv, d_recv, hid_own, w_up, w_lin, w_down, first, count, grads)
             first += count
         grad_up, grad_lin, grad_down = grads
         grad_wqkv, grad_wo = assemble(pieces)

time: 1110 us -> 1100 us (level)
  waiting for transfers between devices: 298 us -> 328 us
  Pallas kernels: 634 us -> 605 us
  local copies, waits for them, and re-layouts: 61.5 us -> 50.4 us
    all_to_all x2, waiting for transfers between devices: 9.07 us -> 39.9 us  [spread(): lax.all_to_all(send, 'ep', 0, 0).reshape(ep_size * tokens, width // 2)]
    pallas_call x1, Pallas kernels: 272 us -> 254 us  [moe_backward(): pl.pallas_call(functools.partial(moe_kernel, cap), out_shape=(jax.ShapeDt...]
    transpose x2, local copies, waits for them, and re-layouts: 14.9 us -> 2.4 us  [spread(): halves = jnp.moveaxis(act.reshape(tokens, 2, width // 2), 1, 0)]
  transfers between devices with their start and end apart: 21 -> 20, of which waited for: 10 -> 11; matrix products, arithmetic and copies ran while one was open for 10% -> 6% of each run, Pallas kernels for 44% -> 43%
where the time goes in v3:
time: 1100 us; the launch traced here: 1090 us
  Pallas kernels  605 us (55%)
  waiting for transfers between devices  328 us (30%)
  matrix products  52.8 us (5%)
  local copies, waits for them, and re-layouts  50.4 us (5%)
  starting transfers between devices  23.3 us (2%)
  other arithmetic  15.7 us (1%)
  between operations  15.3 us (1%)
    pallas_call x1, Pallas kernels, moe_backward(): pl.pallas_call(functools.partial(moe_kernel, cap), out_shape=(jax.ShapeDt...  254 us
    pallas_call x1, Pallas kernels, dense_sums(): pl.pallas_call(dense_kernel, out_shape=(f32(HALF // 2, width), f32(HALF /...  192 us
    ppermute x14, waiting for transfers between devices, local(): lax.ppermute(arr, 'ep', [(e, e ^ bit) for e in range(ep_size)])  148 us
    ppermute x3, waiting for transfers between devices, local(): lax.ppermute(rows_own, 'dp', [((z + r) % planes, z) for z in range(planes)])  139 us
    pallas_call x3, Pallas kernels, weight_grads(): pl.pallas_call(weight_kernel, grid=(count,), out_shape=(f32(w_up), f32(w_...  105 us
    dot_general x16, matrix products, mm(): return jnp.einsum(spec, a, b, preferred_element_type=F32)  52.8 us
    all_to_all x2, waiting for transfers between devices, spread(): lax.all_to_all(send, 'ep', 0, 0).reshape(ep_size * tokens, width // 2)  39.9 us
    pallas_call x1, Pallas kernels, dispatch_rows(): pl.pallas_call(functools.partial(dispatch_kernel, local_exp, cap), grid=(...  31.6 us
  transfers between devices with their start and end apart: 20, of which 11 were waited for; matrix products, arithmetic and copies ran while one was open for 6% of the time, Pallas kernels for 43%

profile of v3, /device:TPU:0, one launch (start us, length us, event | category | flops | bytes accessed | tf_op | source)
XLA Modules:
  0.0 1090.1 jit_solution(6581198643631274765)
XLA Ops:
  12.1 10.2 convolution_convert_fusion
  22.3 2.8 copy.112
  34.5 3.8 concatenate.14.own_ref
  38.3 5.1 collective-permute-start.14
  44.4 35.5 %collective-permute-done.14 = bf16[256,3200]{1,0:T(8,128)(2,1)S(1)} collective-permute-done((bf16[256,3200]{1,0:T(8,128)(2,1)}, bf16[256,3200]{1,0:T(8,128)(2,1)S(1)}, u32[]{:S(2)}, u32[]{:S(2)}) %collective-permute-start.14) | collective-permute-done | bytes 1638432 | tf_op jit(solution)/shard_map/ppermute | solution.py:665
  80.0 103.9 %collective-permute-done.15 = bf16[256,3200]{1,0:T(8,128)(2,1)S(1)} collective-permute-done((bf16[256,3200]{1,0:T(8,128)(2,1)}, bf16[256,3200]{1,0:T(8,128)(2,1)S(1)}, u32[]{:S(2)}, u32[]{:S(2)}) %collective-permute-start.15) | collective-permute-done | bytes 1638432 | tf_op jit(solution)/shard_map/ppermute | solution.py:665
  183.9 2.9 pad_maximum_fusion
  186.8 254.0 %moe_backward.1 = (bf16[64,32,1536]{2,1,0:T(8,128)(2,1)}, f32[8,8,128]{2,1,0:T(8,128)}, bf16[8,1024,1536]{2,1,0:T(8,128)(2,1)}, bf16[8,1024,1536]{2,1,0:T(8,128)(2,1)}, bf16[8,3,256,512]{3,2,1,0:T(8,128)(2,1)}) custom-call(bf16[256,3200]{1,0:T(8,128)(2,1)} %concatenate.14.own_ref, bf16[64,1536]{1,0:T(8,128)(2,1)} %bitcast.161, bf16[8,1536,512]{2,1,0:T(8,128)(2,1)} %up_ref.7, ...), custom_call_target="tpu_custom_call" | custom-call | flops 60000002048 | bytes 67108864 | tf_op jit(solution)/shard_map/moe_backward/pallas_call | solution.py:559
  440.9 2.3 copy.130
  443.2 3.0 broadcast_in_dim.92
  446.2 4.6 all-to-all-start.1
  450.8 3.3 reshape.270
  458.0 10.2 fusion.9
  473.7 3.1 fusion.8
  478.0 3.1 fusion.40
  481.2 31.5 %all-to-all-done.1 = bf16[8,256,768]{2,1,0:T(8,128)(2,1)} async-done(((bf16[8,256,768]{2,1,0:T(8,128)(2,1)}), bf16[8,256,768]{2,1,0:T(8,128)(2,1)}, u32[]{:S(2)}, u32[]{:S(2)}) %all-to-all-start.1) | async-done | bytes 3145760 | tf_op jit(solution)/shard_map/all_to_all | solution.py:653
  514.6 4.6 all-to-all-start
  526.0 2.7 fusion.39
  530.3 3.0 copy.131
  535.6 11.0 %fusion.24 = (f32[1536]{0:T(1024)S(1)}, f32[256]{0:T(256)S(1)}, f32[256,1536]{1,0:T(8,128)}) fusion(bf16[1,256,1536]{2,1,0:T(8,128)(2,1)} %param.11, f32[256]{0:T(256)S(1)} %copy-done.41, f32[1536]{0:T(1024)S(1)} %convert_element_type.139, bf16[256,4608]{0,1:T(8,128)(2,1)} %bitcast.152, bf16[1536,4608]{1,0:T(8,128)(2,1)} %param.15), kind=kOutput, calls=%fused_computation.49 | convolution fusion | flops 3627415808 | bytes 18888704 | tf_op jit(solution)/shard_map/bse,de->bsd/dot_general | solution.py:20
  548.6 8.4 all-to-all-done
  557.0 192.4 %dense_sums.1 = (f32[384,1536]{1,0:T(8,128)S(1)}, f32[384,1536]{1,0:T(8,128)S(1)}, f32[24,128]{1,0:T(8,128)S(1)}, f32[32,24,128]{2,1,0:T(8,128)S(1)}) custom-call(bf16[2048,768]{1,0:T(8,128)(2,1)} %bitcast.38.acts_xn_ref, bf16[2048,768]{1,0:T(8,128)(2,1)} %bitcast.44.acts_ao_ref, bf16[4,256,1536]{2,1,0:T(8,128)(2,1)} %pad_maximum_fusion.1.dsend_ref, ...), custom_call_target="tpu_custom_call" | custom-call | flops 99999997952 | bytes 41943040 | tf_op jit(solution)/shard_map/dense_sums/pallas_call | solution.py:247
  753.6 50.1 %collective-permute-done.2.refs_4_ = f32[384,1536]{1,0:T(8,128)S(1)} collective-permute-done((f32[384,1536]{1,0:T(8,128)S(1)}, f32[384,1536]{1,0:T(8,128)S(1)}, u32[]{:S(2)}, u32[]{:S(2)}) %collective-permute-start.2) | collective-permute-done | bytes 2359328 | tf_op jit(solution)/shard_map/ppermute | solution.py:694
  806.5 45.7 %collective-permute-done.3.refs_5_ = f32[384,1536]{1,0:T(8,128)} collective-permute-done((f32[384,1536]{1,0:T(8,128)S(1)}, f32[384,1536]{1,0:T(8,128)}, u32[]{:S(2)}, u32[]{:S(2)}) %collective-permute-start.3) | collective-permute-done | bytes 2359328 | tf_op jit(solution)/shard_map/ppermute | solution.py:694
  860.6 43.5 %collective-permute-done.10.refs_12_ = f32[384,1536]{1,0:T(8,128)} collective-permute-done((f32[384,1536]{1,0:T(8,128)S(1)}, f32[384,1536]{1,0:T(8,128)}, u32[]{:S(2)}, u32[]{:S(2)}) %collective-permute-start.10) | collective-permute-done | bytes 2359328 | tf_op jit(solution)/shard_map/ppermute | solution.py:694
  909.3 3.1 collective-permute-done.12.refs_14_
  912.4 3.4 collective-permute-done.13.refs_15_
  924.1 21.8 %assemble.1 = (f32[1536,4608]{1,0:T(8,128)}, f32[1536,1536]{1,0:T(8,128)}) custom-call(f32[384,1536]{1,0:T(8,128)S(1)} %get-tuple-element.37.refs_0_, f32[384,1536]{1,0:T(8,128)S(1)} %copy-done.1, f32[384,1536]{1,0:T(8,128)S(1)} %copy-done.5, f32[384,1536]{1,0:T(8,128)S(1)} %copy-done.7, f32[384,1536]{1,0:T(8,128)S(1)} %copy-done.3, ...), custom_call_target="tpu_custom_call" | custom-call | flops 20000000000 | bytes 83886080 | tf_op jit(solution)/shard_map/assemble/pallas_call | solution.py:307
  945.9 31.6 %dispatch_rows.1 = (bf16[8,1024,1536]{2,1,0:T(8,128)(2,1)}, bf16[8,1024,1536]{2,1,0:T(8,128)(2,1)}) custom-call(bf16[24,256,3200]{2,1,0:T(8,128)(2,1)} %all-gather.3.cloned.1.call-done, bf16[64,1536]{1,0:T(8,128)(2,1)} %bitcast.162, bf16[8,1024,1536]{2,1,0:T(8,128)(2,1)} %get-tuple-element.43.recv_in, ...), custom_call_target="tpu_custom_call", output_to_operand_aliasing={{0}: (2, {}), {1}: (3, {})} | custom-call | flops 9663676416 | bytes 75497472 | tf_op jit(solution)/shard_map/dispatch_rows/pallas_call | solution.py:372
  977.5 28.2 %weight_grads.3 = (f32[8,1536,512]{2,1,0:T(8,128)}, f32[8,1536,512]{2,1,0:T(8,128)}, f32[8,512,1536]{2,1,0:T(8,128)}) custom-call(bf16[8,1024,1536]{2,1,0:T(8,128)(2,1)} %get-tuple-element.45.recv_ref, bf16[8,1024,1536]{2,1,0:T(8,128)(2,1)} %get-tuple-element.46.d_recv_ref, bf16[8,3,256,512]{3,2,1,0:T(8,128)(2,1)} %get-tuple-element.47.hid_ref, ...), custom_call_target="tpu_custom_call" | custom-call | flops 19327352832 | bytes 41943040 | tf_op jit(solution)/shard_map/weight_grads/pallas_call | solution.py:614
  1005.7 28.3 %weight_grads.4 = (f32[8,1536,512]{2,1,0:T(8,128)}, f32[8,1536,512]{2,1,0:T(8,128)}, f32[8,512,1536]{2,1,0:T(8,128)}) custom-call(bf16[8,1024,1536]{2,1,0:T(8,128)(2,1)} %get-tuple-element.45.recv_ref, bf16[8,1024,1536]{2,1,0:T(8,128)(2,1)} %get-tuple-element.46.d_recv_ref, ...), custom_call_target="tpu_custom_call", output_to_operand_aliasing={{0}: (6, {}), {1}: (7, {}), {2}: (8, {})} | custom-call | flops 19327352832 | bytes 41943040 | tf_op jit(solution)/shard_map/weight_grads/pallas_call | solution.py:614
  1034.0 48.8 %weight_grads.5 = (f32[8,1536,512]{2,1,0:T(8,128)}, f32[8,1536,512]{2,1,0:T(8,128)}, f32[8,512,1536]{2,1,0:T(8,128)}) custom-call(bf16[8,1024,1536]{2,1,0:T(8,128)(2,1)} %get-tuple-element.45.recv_ref, bf16[8,1024,1536]{2,1,0:T(8,128)(2,1)} %get-tuple-element.46.d_recv_ref, ...), custom_call_target="tpu_custom_call", output_to_operand_aliasing={{0}: (6, {}), {1}: (7, {}), {2}: (8, {})} | custom-call | flops 38654705664 | bytes 83886080 | tf_op jit(solution)/shard_map/weight_grads/pallas_call | solution.py:614
  (189 shorter events, 68.7 us)
Async XLA Ops:
  7.2 938.7 %all-gather.3.cloned.1.call-start = ((), (), s32[]{:S(2)}) async-start(), calls=%async_computation.2 | async-start | bytes 44236800 | tf_op jit(solution)/shard_map/all_gather | solution.py:682
  9.2 13.2 %copy-start.40 = (f32[256]{0:T(256)}, f32[256]{0:T(256)S(1)}, u32[]{:S(2)}) copy-start(f32[256]{0:T(256)S(1)} %fusion.57) | copy-start | bytes 3076
  34.5 419.7 %copy-start.19 = (bf16[256,1536]{1,0:T(8,128)(2,1)}, bf16[256,1536]{1,0:T(8,128)(2,1)S(1)}, u32[]{:S(2)}) copy-start(bf16[256,1536]{1,0:T(8,128)(2,1)S(1)} %fusion.25) | copy-start | bytes 2359300
  38.3 41.6 %collective-permute-start.14 = (bf16[256,3200]{1,0:T(8,128)(2,1)}, bf16[256,3200]{1,0:T(8,128)(2,1)S(1)}, u32[]{:S(2)}, u32[]{:S(2)}) collective-permute-start(bf16[256,3200]{1,0:T(8,128)(2,1)} %concatenate.14.own_ref), channel_id=1, source_target_pairs={{8,0},{16,8},{24,16},{0,24},{9,1},{17,9},{25,17},{1,25},{10,2},{18... | collective-permute-start | bytes 4915208 | tf_op jit(solution)/shard_map/ppermute | solution.py:665
  43.4 140.5 %collective-permute-start.15 = (bf16[256,3200]{1,0:T(8,128)(2,1)}, bf16[256,3200]{1,0:T(8,128)(2,1)S(1)}, u32[]{:S(2)}, u32[]{:S(2)}) collective-permute-start(bf16[256,3200]{1,0:T(8,128)(2,1)} %concatenate.14.own_ref), channel_id=1, source_target_pairs={{16,0},{24,8},{0,16},{8,24},{17,1},{25,9},{1,17},{9,25},{18,2},{26... | collective-permute-start | bytes 4915208 | tf_op jit(solution)/shard_map/ppermute | solution.py:665
  43.4 140.5 %collective-permute-start.16 = (bf16[256,3200]{1,0:T(8,128)(2,1)}, bf16[256,3200]{1,0:T(8,128)(2,1)S(1)}, u32[]{:S(2)}, u32[]{:S(2)}) collective-permute-start(bf16[256,3200]{1,0:T(8,128)(2,1)} %concatenate.14.own_ref), channel_id=1, source_target_pairs={{24,0},{0,8},{8,16},{16,24},{25,1},{1,9},{9,17},{17,25},{26,2},{2,... | collective-permute-start | bytes 4915208 | tf_op jit(solution)/shard_map/ppermute | solution.py:665
  446.2 66.5 %all-to-all-start.1 = ((bf16[8,256,768]{2,1,0:T(8,128)(2,1)}), bf16[8,256,768]{2,1,0:T(8,128)(2,1)}, u32[]{:S(2)}, u32[]{:S(2)}) async-start(bf16[8,256,768]{2,1,0:T(8,128)(2,1)} %bitcast.148), calls=%async_computation.1 | async-start | bytes 6291456 | tf_op jit(solution)/shard_map/all_to_all | solution.py:653
  456.0 12.2 %copy-start.34 = (f32[256]{0:T(256)}, f32[256]{0:T(256)S(1)}, u32[]{:S(2)}) copy-start(f32[256]{0:T(256)S(1)} %get-tuple-element.97) | copy-start | bytes 3076
  457.7 10.6 copy-start.42
  458.0 12.0 %slice-start.2 = ((s8[4718592]{0:T(1024)(128)(4,1)}), s8[4194304]{0:T(1024)(128)(4,1)S(1)}, s32[]{:S(2)}) async-start(s8[4718592]{0:T(1024)(128)(4,1)} %bitcast.171), calls=%async_computation.5 | async-start | bytes 8388608
  458.0 11.9 %slice-start.3 = ((s8[4718592]{0:T(1024)(128)(4,1)}), s8[524288]{0:T(1024)(128)(4,1)S(1)}, s32[]{:S(2)}) async-start(s8[4718592]{0:T(1024)(128)(4,1)} %bitcast.171), calls=%async_computation.6 | async-start | bytes 1048576
  470.0 51.4 %copy-start.14 = (bf16[256,1536]{1,0:T(8,128)(2,1)}, bf16[256,1536]{1,0:T(8,128)(2,1)S(1)}, u32[]{:S(2)}) copy-start(bf16[256,1536]{1,0:T(8,128)(2,1)S(1)} %fusion.28) | copy-start | bytes 2359300
  514.6 42.5 %all-to-all-start = ((bf16[8,256,768]{2,1,0:T(8,128)(2,1)}), bf16[8,256,768]{2,1,0:T(8,128)(2,1)}, u32[]{:S(2)}, u32[]{:S(2)}) async-start(bf16[8,256,768]{2,1,0:T(8,128)(2,1)} %bitcast.149), calls=%async_computation | async-start | bytes 6291456 | tf_op jit(solution)/shard_map/all_to_all | solution.py:653
  535.6 11.0 %copy-start.21 = (bf16[256,4,384]{2,0,1:T(8,128)(2,1)S(1)}, bf16[256,4,384]{2,0,1:T(8,128)(2,1)}, u32[]{:S(2)}) copy-start(bf16[256,4,384]{2,0,1:T(8,128)(2,1)} %copy.133) | copy-start | bytes 2359300
  557.0 349.0 %copy-start.39 = (f32[256]{0:T(256)S(1)}, f32[256]{0:T(256)}, u32[]{:S(2)}) copy-start(f32[256]{0:T(256)} %copy-done.38) | copy-start | bytes 3076
  557.0 349.0 %copy-start.15 = (bf16[256,1536]{1,0:T(8,128)(2,1)S(1)}, bf16[256,1536]{1,0:T(8,128)(2,1)}, u32[]{:S(2)}) copy-start(bf16[256,1536]{1,0:T(8,128)(2,1)} %copy-done.14) | copy-start | bytes 2359300
  557.0 349.0 %copy-start.17 = (bf16[1,256,1536]{2,1,0:T(8,128)(2,1)S(1)}, bf16[1,256,1536]{2,1,0:T(8,128)(2,1)}, u32[]{:S(2)}) copy-start(bf16[1,256,1536]{2,1,0:T(8,128)(2,1)} %param.11) | copy-start | bytes 2359300
  557.0 349.0 %copy-start.28 = (f32[256,1536]{1,0:T(8,128)S(1)}, f32[256,1536]{1,0:T(8,128)}, u32[]{:S(2)}) copy-start(f32[256,1536]{1,0:T(8,128)} %get-tuple-element.113) | copy-start | bytes 4718596
  749.5 54.2 %collective-permute-start.2 = (f32[384,1536]{1,0:T(8,128)S(1)}, f32[384,1536]{1,0:T(8,128)S(1)}, u32[]{:S(2)}, u32[]{:S(2)}) collective-permute-start(f32[384,1536]{1,0:T(8,128)S(1)} %get-tuple-element.37.refs_0_), channel_id=1, source_target_pairs={{0,2},{1,3},{2,0},{3,1},{4,6},{5,7},{6,4},{7,5},{8,10},{9,11},{10,... | collective-permute-start | bytes 7077896 | tf_op jit(solution)/shard_map/ppermute | solution.py:694
  751.1 54.2 %collective-permute-start.7 = (f32[384,1536]{1,0:T(8,128)S(1)}, f32[384,1536]{1,0:T(8,128)}, u32[]{:S(2)}, u32[]{:S(2)}) collective-permute-start(f32[384,1536]{1,0:T(8,128)S(1)} %get-tuple-element.38.refs_1_), channel_id=1, source_target_pairs={{0,4},{1,5},{2,6},{3,7},{4,0},{5,1},{6,2},{7,3},{8,12},{9,13},{10,... | collective-permute-start | bytes 7077896 | tf_op jit(solution)/shard_map/ppermute | solution.py:694
  751.7 100.5 %collective-permute-start.3 = (f32[384,1536]{1,0:T(8,128)S(1)}, f32[384,1536]{1,0:T(8,128)}, u32[]{:S(2)}, u32[]{:S(2)}) collective-permute-start(f32[384,1536]{1,0:T(8,128)S(1)} %get-tuple-element.38.refs_1_), channel_id=1, source_target_pairs={{0,2},{1,3},{2,0},{3,1},{4,6},{5,7},{6,4},{7,5},{8,10},{9,11},{10,... | collective-permute-start | bytes 7077896 | tf_op jit(solution)/shard_map/ppermute | solution.py:694
  753.0 102.8 %collective-permute-start.6 = (f32[384,1536]{1,0:T(8,128)S(1)}, f32[384,1536]{1,0:T(8,128)}, u32[]{:S(2)}, u32[]{:S(2)}) collective-permute-start(f32[384,1536]{1,0:T(8,128)S(1)} %get-tuple-element.37.refs_0_), channel_id=1, source_target_pairs={{0,4},{1,5},{2,6},{3,7},{4,0},{5,1},{6,2},{7,3},{8,12},{9,13},{10,... | collective-permute-start | bytes 7077896 | tf_op jit(solution)/shard_map/ppermute | solution.py:694
  753.6 103.7 %collective-permute-start = (f32[384,1536]{1,0:T(8,128)S(1)}, f32[384,1536]{1,0:T(8,128)S(1)}, u32[]{:S(2)}, u32[]{:S(2)}) collective-permute-start(f32[384,1536]{1,0:T(8,128)S(1)} %get-tuple-element.37.refs_0_), channel_id=1, source_target_pairs={{0,1},{1,0},{2,3},{3,2},{4,5},{5,4},{6,7},{7,6},{8,9},{9,8},{10,11... | collective-permute-start | bytes 7077896 | tf_op jit(solution)/shard_map/ppermute | solution.py:694
  803.6 55.6 %collective-permute-start.1 = (f32[384,1536]{1,0:T(8,128)S(1)}, f32[384,1536]{1,0:T(8,128)S(1)}, u32[]{:S(2)}, u32[]{:S(2)}) collective-permute-start(f32[384,1536]{1,0:T(8,128)S(1)} %get-tuple-element.38.refs_1_), channel_id=1, source_target_pairs={{0,1},{1,0},{2,3},{3,2},{4,5},{5,4},{6,7},{7,6},{8,9},{9,8},{10,11... | collective-permute-start | bytes 7077896 | tf_op jit(solution)/shard_map/ppermute | solution.py:694
  805.3 98.8 %collective-permute-start.10 = (f32[384,1536]{1,0:T(8,128)S(1)}, f32[384,1536]{1,0:T(8,128)}, u32[]{:S(2)}, u32[]{:S(2)}) collective-permute-start(f32[384,1536]{1,0:T(8,128)S(1)} %collective-permute-done.2.refs_4_), channel_id=1, source_target_pairs={{0,4},{1,5},{2,6},{3,7},{4,0},{5,1},{6,2},{7,3},{8,12},{9,13},{10,... | collective-permute-start | bytes 7077896 | tf_op jit(solution)/shard_map/ppermute | solution.py:694
  852.3 51.9 %collective-permute-start.11 = (f32[384,1536]{1,0:T(8,128)}, f32[384,1536]{1,0:T(8,128)}, u32[]{:S(2)}, u32[]{:S(2)}) collective-permute-start(f32[384,1536]{1,0:T(8,128)} %collective-permute-done.7.refs_9_), channel_id=1, source_target_pairs={{0,2},{1,3},{2,0},{3,1},{4,6},{5,7},{6,4},{7,5},{8,10},{9,11},{10,... | collective-permute-start | bytes 7077896 | tf_op jit(solution)/shard_map/ppermute | solution.py:694
  855.9 48.8 %collective-permute-start.4 = (f32[384,1536]{1,0:T(8,128)S(1)}, f32[384,1536]{1,0:T(8,128)S(1)}, u32[]{:S(2)}, u32[]{:S(2)}) collective-permute-start(f32[384,1536]{1,0:T(8,128)S(1)} %collective-permute-done.2.refs_4_), channel_id=1, source_target_pairs={{0,1},{1,0},{2,3},{3,2},{4,5},{5,4},{6,7},{7,6},{8,9},{9,8},{10,11... | collective-permute-start | bytes 7077896 | tf_op jit(solution)/shard_map/ppermute | solution.py:694
  858.7 50.6 %collective-permute-start.9 = (f32[384,1536]{1,0:T(8,128)}, f32[384,1536]{1,0:T(8,128)}, u32[]{:S(2)}, u32[]{:S(2)}) collective-permute-start(f32[384,1536]{1,0:T(8,128)} %collective-permute-done.7.refs_9_), channel_id=1, source_target_pairs={{0,1},{1,0},{2,3},{3,2},{4,5},{5,4},{6,7},{7,6},{8,9},{9,8},{10,11... | collective-permute-start | bytes 7077896 | tf_op jit(solution)/shard_map/ppermute | solution.py:694
  860.6 48.7 %collective-permute-start.5 = (f32[384,1536]{1,0:T(8,128)}, f32[384,1536]{1,0:T(8,128)}, u32[]{:S(2)}, u32[]{:S(2)}) collective-permute-start(f32[384,1536]{1,0:T(8,128)} %collective-permute-done.3.refs_5_), channel_id=1, source_target_pairs={{0,1},{1,0},{2,3},{3,2},{4,5},{5,4},{6,7},{7,6},{8,9},{9,8},{10,11... | collective-permute-start | bytes 7077896 | tf_op jit(solution)/shard_map/ppermute | solution.py:694
  904.1 5.2 collective-permute-start.8
  904.1 8.2 collective-permute-start.12
  906.0 9.7 collective-permute-start.13
  (41 other events, 121.6 us)
Sparse Core Ops, SparseCore 0:
  186.9 320.2 all-gather.2

commit v4 on v3

--- a/solution.py
+++ b/solution.py
@@ -173,7 +173,7 @@
         ref = low_ref if k < STEPS // 2 else high_ref
         return pltpu.make_async_copy(total.at[k], ref.at[pl.ds(k % (STEPS // 2) * CHUNK, CHUNK), :], own_sem.at[k])
 
-    for i in range(STEPS + 3):
+    for i in range(STEPS + 7):
         k = i
         if k < STEPS and k * CHUNK % BLOCK == 0:
             cols = slice(k * CHUNK, k * CHUNK + BLOCK)
@@ -187,7 +187,7 @@
         if i == 8:
             push_all(*total_push)
         a = i - 1
-        t = i - 2
+        t = i - 3
 
         @pl.when(inner)
         def _():
@@ -205,9 +205,9 @@
         def _():
             if k < STEPS:
                 up_copy(k).start()
-            if 0 <= i - 3 < STEPS:
-                down_copy(i - 3).wait_recv()
-                own_copy(i - 3).start()
+            if 0 <= i - 7 < STEPS:
+                down_copy(i - 7).wait_recv()
+                own_copy(i - 7).start()
 
     for k in range(STEPS):
         own_copy(k).wait()

time: 1100 us -> 1100 us (level)
  transfers between devices with their start and end apart: 20 -> 20, of which waited for: 11 -> 12; matrix products, arithmetic and copies ran while one was open for 6% -> 6% of each run, Pallas kernels for 43% -> 43%
where the time goes in v4:
time: 1100 us; the launch traced here: 1090 us
  Pallas kernels  609 us (55%)
  waiting for transfers between devices  329 us (30%)
  matrix products  52.8 us (5%)
  local copies, waits for them, and re-layouts  50.4 us (5%)
  starting transfers between devices  23.3 us (2%)
  other arithmetic  15.7 us (1%)
  between operations  15.3 us (1%)
    pallas_call x1, Pallas kernels, moe_backward(): pl.pallas_call(functools.partial(moe_kernel, cap), out_shape=(jax.ShapeDt...  254 us
    pallas_call x1, Pallas kernels, dense_sums(): pl.pallas_call(dense_kernel, out_shape=(f32(HALF // 2, width), f32(HALF /...  196 us
    ppermute x14, waiting for transfers between devices, local(): lax.ppermute(arr, 'ep', [(e, e ^ bit) for e in range(ep_size)])  149 us
    ppermute x3, waiting for transfers between devices, local(): lax.ppermute(rows_own, 'dp', [((z + r) % planes, z) for z in range(planes)])  139 us
    pallas_call x3, Pallas kernels, weight_grads(): pl.pallas_call(weight_kernel, grid=(count,), out_shape=(f32(w_up), f32(w_...  105 us
    dot_general x16, matrix products, mm(): return jnp.einsum(spec, a, b, preferred_element_type=F32)  52.8 us
    all_to_all x2, waiting for transfers between devices, spread(): lax.all_to_all(send, 'ep', 0, 0).reshape(ep_size * tokens, width // 2)  39.9 us
    pallas_call x1, Pallas kernels, dispatch_rows(): pl.pallas_call(functools.partial(dispatch_kernel, local_exp, cap), grid=(...  31.6 us
  transfers between devices with their start and end apart: 20, of which 12 were waited for; matrix products, arithmetic and copies ran while one was open for 6% of the time, Pallas kernels for 43%

profile of v4, /device:TPU:0, one launch (start us, length us, event | category | flops | bytes accessed | tf_op | source)
XLA Modules:
  0.0 1094.8 jit_solution(866395920000435342)
XLA Ops:
  12.1 10.2 convolution_convert_fusion
  22.3 2.8 copy.112
  34.5 3.8 concatenate.14.own_ref
  38.3 5.1 collective-permute-start.14
  44.4 35.5 %collective-permute-done.14 = bf16[256,3200]{1,0:T(8,128)(2,1)S(1)} collective-permute-done((bf16[256,3200]{1,0:T(8,128)(2,1)}, bf16[256,3200]{1,0:T(8,128)(2,1)S(1)}, u32[]{:S(2)}, u32[]{:S(2)}) %collective-permute-start.14) | collective-permute-done | bytes 1638432 | tf_op jit(solution)/shard_map/ppermute | solution.py:665
  80.0 103.9 %collective-permute-done.15 = bf16[256,3200]{1,0:T(8,128)(2,1)S(1)} collective-permute-done((bf16[256,3200]{1,0:T(8,128)(2,1)}, bf16[256,3200]{1,0:T(8,128)(2,1)S(1)}, u32[]{:S(2)}, u32[]{:S(2)}) %collective-permute-start.15) | collective-permute-done | bytes 1638432 | tf_op jit(solution)/shard_map/ppermute | solution.py:665
  183.9 2.9 pad_maximum_fusion
  186.8 254.0 %moe_backward.1 = (bf16[64,32,1536]{2,1,0:T(8,128)(2,1)}, f32[8,8,128]{2,1,0:T(8,128)}, bf16[8,1024,1536]{2,1,0:T(8,128)(2,1)}, bf16[8,1024,1536]{2,1,0:T(8,128)(2,1)}, bf16[8,3,256,512]{3,2,1,0:T(8,128)(2,1)}) custom-call(bf16[256,3200]{1,0:T(8,128)(2,1)} %concatenate.14.own_ref, bf16[64,1536]{1,0:T(8,128)(2,1)} %bitcast.161, bf16[8,1536,512]{2,1,0:T(8,128)(2,1)} %up_ref.7, ...), custom_call_target="tpu_custom_call" | custom-call | flops 60000002048 | bytes 67108864 | tf_op jit(solution)/shard_map/moe_backward/pallas_call | solution.py:559
  440.9 2.3 copy.130
  443.2 3.0 broadcast_in_dim.92
  446.2 4.6 all-to-all-start.1
  450.8 3.3 reshape.270
  458.0 10.2 fusion.9
  470.0 2.3 convolution_convert_fusion.2
  473.7 3.1 fusion.8
  478.0 3.1 fusion.40
  481.2 31.5 %all-to-all-done.1 = bf16[8,256,768]{2,1,0:T(8,128)(2,1)} async-done(((bf16[8,256,768]{2,1,0:T(8,128)(2,1)}), bf16[8,256,768]{2,1,0:T(8,128)(2,1)}, u32[]{:S(2)}, u32[]{:S(2)}) %all-to-all-start.1) | async-done | bytes 3145760 | tf_op jit(solution)/shard_map/all_to_all | solution.py:653
  514.6 4.6 all-to-all-start
  526.0 2.7 fusion.39
  530.3 3.0 copy.131
  535.6 11.0 %fusion.24 = (f32[1536]{0:T(1024)S(1)}, f32[256]{0:T(256)S(1)}, f32[256,1536]{1,0:T(8,128)}) fusion(bf16[1,256,1536]{2,1,0:T(8,128)(2,1)} %param.11, f32[256]{0:T(256)S(1)} %copy-done.41, f32[1536]{0:T(1024)S(1)} %convert_element_type.139, bf16[256,4608]{0,1:T(8,128)(2,1)} %bitcast.152, bf16[1536,4608]{1,0:T(8,128)(2,1)} %param.15), kind=kOutput, calls=%fused_computation.49 | convolution fusion | flops 3627415808 | bytes 18888704 | tf_op jit(solution)/shard_map/bse,de->bsd/dot_general | solution.py:20
  548.6 8.4 all-to-all-done
  557.0 196.1 %dense_sums.1 = (f32[384,1536]{1,0:T(8,128)S(1)}, f32[384,1536]{1,0:T(8,128)S(1)}, f32[24,128]{1,0:T(8,128)S(1)}, f32[32,24,128]{2,1,0:T(8,128)S(1)}) custom-call(bf16[2048,768]{1,0:T(8,128)(2,1)} %bitcast.38.acts_xn_ref, bf16[2048,768]{1,0:T(8,128)(2,1)} %bitcast.44.acts_ao_ref, bf16[4,256,1536]{2,1,0:T(8,128)(2,1)} %pad_maximum_fusion.1.dsend_ref, ...), custom_call_target="tpu_custom_call" | custom-call | flops 99999997952 | bytes 41943040 | tf_op jit(solution)/shard_map/dense_sums/pallas_call | solution.py:247
  757.2 50.1 %collective-permute-done.2.refs_4_ = f32[384,1536]{1,0:T(8,128)S(1)} collective-permute-done((f32[384,1536]{1,0:T(8,128)S(1)}, f32[384,1536]{1,0:T(8,128)S(1)}, u32[]{:S(2)}, u32[]{:S(2)}) %collective-permute-start.2) | collective-permute-done | bytes 2359328 | tf_op jit(solution)/shard_map/ppermute | solution.py:694
  810.2 46.9 %collective-permute-done.3.refs_5_ = f32[384,1536]{1,0:T(8,128)} collective-permute-done((f32[384,1536]{1,0:T(8,128)S(1)}, f32[384,1536]{1,0:T(8,128)}, u32[]{:S(2)}, u32[]{:S(2)}) %collective-permute-start.3) | collective-permute-done | bytes 2359328 | tf_op jit(solution)/shard_map/ppermute | solution.py:694
  864.2 44.7 %collective-permute-done.10.refs_12_ = f32[384,1536]{1,0:T(8,128)} collective-permute-done((f32[384,1536]{1,0:T(8,128)S(1)}, f32[384,1536]{1,0:T(8,128)}, u32[]{:S(2)}, u32[]{:S(2)}) %collective-permute-start.10) | collective-permute-done | bytes 2359328 | tf_op jit(solution)/shard_map/ppermute | solution.py:694
  917.1 3.4 collective-permute-done.13.refs_15_
  928.8 21.8 %assemble.1 = (f32[1536,4608]{1,0:T(8,128)}, f32[1536,1536]{1,0:T(8,128)}) custom-call(f32[384,1536]{1,0:T(8,128)S(1)} %get-tuple-element.37.refs_0_, f32[384,1536]{1,0:T(8,128)S(1)} %copy-done.1, f32[384,1536]{1,0:T(8,128)S(1)} %copy-done.5, f32[384,1536]{1,0:T(8,128)S(1)} %copy-done.7, f32[384,1536]{1,0:T(8,128)S(1)} %copy-done.3, ...), custom_call_target="tpu_custom_call" | custom-call | flops 20000000000 | bytes 83886080 | tf_op jit(solution)/shard_map/assemble/pallas_call | solution.py:307
  950.6 31.6 %dispatch_rows.1 = (bf16[8,1024,1536]{2,1,0:T(8,128)(2,1)}, bf16[8,1024,1536]{2,1,0:T(8,128)(2,1)}) custom-call(bf16[24,256,3200]{2,1,0:T(8,128)(2,1)} %all-gather.3.cloned.1.call-done, bf16[64,1536]{1,0:T(8,128)(2,1)} %bitcast.162, bf16[8,1024,1536]{2,1,0:T(8,128)(2,1)} %get-tuple-element.43.recv_in, ...), custom_call_target="tpu_custom_call", output_to_operand_aliasing={{0}: (2, {}), {1}: (3, {})} | custom-call | flops 9663676416 | bytes 75497472 | tf_op jit(solution)/shard_map/dispatch_rows/pallas_call | solution.py:372
  982.2 28.2 %weight_grads.3 = (f32[8,1536,512]{2,1,0:T(8,128)}, f32[8,1536,512]{2,1,0:T(8,128)}, f32[8,512,1536]{2,1,0:T(8,128)}) custom-call(bf16[8,1024,1536]{2,1,0:T(8,128)(2,1)} %get-tuple-element.45.recv_ref, bf16[8,1024,1536]{2,1,0:T(8,128)(2,1)} %get-tuple-element.46.d_recv_ref, bf16[8,3,256,512]{3,2,1,0:T(8,128)(2,1)} %get-tuple-element.47.hid_ref, ...), custom_call_target="tpu_custom_call" | custom-call | flops 19327352832 | bytes 41943040 | tf_op jit(solution)/shard_map/weight_grads/pallas_call | solution.py:614
  1010.4 28.3 %weight_grads.4 = (f32[8,1536,512]{2,1,0:T(8,128)}, f32[8,1536,512]{2,1,0:T(8,128)}, f32[8,512,1536]{2,1,0:T(8,128)}) custom-call(bf16[8,1024,1536]{2,1,0:T(8,128)(2,1)} %get-tuple-element.45.recv_ref, bf16[8,1024,1536]{2,1,0:T(8,128)(2,1)} %get-tuple-element.46.d_recv_ref, ...), custom_call_target="tpu_custom_call", output_to_operand_aliasing={{0}: (6, {}), {1}: (7, {}), {2}: (8, {})} | custom-call | flops 19327352832 | bytes 41943040 | tf_op jit(solution)/shard_map/weight_grads/pallas_call | solution.py:614
  1038.7 48.8 %weight_grads.5 = (f32[8,1536,512]{2,1,0:T(8,128)}, f32[8,1536,512]{2,1,0:T(8,128)}, f32[8,512,1536]{2,1,0:T(8,128)}) custom-call(bf16[8,1024,1536]{2,1,0:T(8,128)(2,1)} %get-tuple-element.45.recv_ref, bf16[8,1024,1536]{2,1,0:T(8,128)(2,1)} %get-tuple-element.46.d_recv_ref, ...), custom_call_target="tpu_custom_call", output_to_operand_aliasing={{0}: (6, {}), {1}: (7, {}), {2}: (8, {})} | custom-call | flops 38654705664 | bytes 83886080 | tf_op jit(solution)/shard_map/weight_grads/pallas_call | solution.py:614
  (189 shorter events, 68.2 us)
Async XLA Ops:
  7.2 943.4 %all-gather.3.cloned.1.call-start = ((), (), s32[]{:S(2)}) async-start(), calls=%async_computation.2 | async-start | bytes 44236800 | tf_op jit(solution)/shard_map/all_gather | solution.py:682
  9.2 13.2 %copy-start.40 = (f32[256]{0:T(256)}, f32[256]{0:T(256)S(1)}, u32[]{:S(2)}) copy-start(f32[256]{0:T(256)S(1)} %fusion.57) | copy-start | bytes 3076
  34.5 419.7 %copy-start.19 = (bf16[256,1536]{1,0:T(8,128)(2,1)}, bf16[256,1536]{1,0:T(8,128)(2,1)S(1)}, u32[]{:S(2)}) copy-start(bf16[256,1536]{1,0:T(8,128)(2,1)S(1)} %fusion.25) | copy-start | bytes 2359300
  38.3 41.6 %collective-permute-start.14 = (bf16[256,3200]{1,0:T(8,128)(2,1)}, bf16[256,3200]{1,0:T(8,128)(2,1)S(1)}, u32[]{:S(2)}, u32[]{:S(2)}) collective-permute-start(bf16[256,3200]{1,0:T(8,128)(2,1)} %concatenate.14.own_ref), channel_id=1, source_target_pairs={{8,0},{16,8},{24,16},{0,24},{9,1},{17,9},{25,17},{1,25},{10,2},{18... | collective-permute-start | bytes 4915208 | tf_op jit(solution)/shard_map/ppermute | solution.py:665
  43.4 140.5 %collective-permute-start.15 = (bf16[256,3200]{1,0:T(8,128)(2,1)}, bf16[256,3200]{1,0:T(8,128)(2,1)S(1)}, u32[]{:S(2)}, u32[]{:S(2)}) collective-permute-start(bf16[256,3200]{1,0:T(8,128)(2,1)} %concatenate.14.own_ref), channel_id=1, source_target_pairs={{16,0},{24,8},{0,16},{8,24},{17,1},{25,9},{1,17},{9,25},{18,2},{26... | collective-permute-start | bytes 4915208 | tf_op jit(solution)/shard_map/ppermute | solution.py:665
  43.4 140.5 %collective-permute-start.16 = (bf16[256,3200]{1,0:T(8,128)(2,1)}, bf16[256,3200]{1,0:T(8,128)(2,1)S(1)}, u32[]{:S(2)}, u32[]{:S(2)}) collective-permute-start(bf16[256,3200]{1,0:T(8,128)(2,1)} %concatenate.14.own_ref), channel_id=1, source_target_pairs={{24,0},{0,8},{8,16},{16,24},{25,1},{1,9},{9,17},{17,25},{26,2},{2,... | collective-permute-start | bytes 4915208 | tf_op jit(solution)/shard_map/ppermute | solution.py:665
  446.2 66.5 %all-to-all-start.1 = ((bf16[8,256,768]{2,1,0:T(8,128)(2,1)}), bf16[8,256,768]{2,1,0:T(8,128)(2,1)}, u32[]{:S(2)}, u32[]{:S(2)}) async-start(bf16[8,256,768]{2,1,0:T(8,128)(2,1)} %bitcast.148), calls=%async_computation.1 | async-start | bytes 6291456 | tf_op jit(solution)/shard_map/all_to_all | solution.py:653
  456.0 12.2 %copy-start.34 = (f32[256]{0:T(256)}, f32[256]{0:T(256)S(1)}, u32[]{:S(2)}) copy-start(f32[256]{0:T(256)S(1)} %get-tuple-element.97) | copy-start | bytes 3076
  457.7 10.6 copy-start.42
  458.0 12.0 %slice-start.2 = ((s8[4718592]{0:T(1024)(128)(4,1)}), s8[4194304]{0:T(1024)(128)(4,1)S(1)}, s32[]{:S(2)}) async-start(s8[4718592]{0:T(1024)(128)(4,1)} %bitcast.171), calls=%async_computation.5 | async-start | bytes 8388608
  458.0 11.9 %slice-start.3 = ((s8[4718592]{0:T(1024)(128)(4,1)}), s8[524288]{0:T(1024)(128)(4,1)S(1)}, s32[]{:S(2)}) async-start(s8[4718592]{0:T(1024)(128)(4,1)} %bitcast.171), calls=%async_computation.6 | async-start | bytes 1048576
  470.0 51.4 %copy-start.14 = (bf16[256,1536]{1,0:T(8,128)(2,1)}, bf16[256,1536]{1,0:T(8,128)(2,1)S(1)}, u32[]{:S(2)}) copy-start(bf16[256,1536]{1,0:T(8,128)(2,1)S(1)} %fusion.28) | copy-start | bytes 2359300
  514.6 42.5 %all-to-all-start = ((bf16[8,256,768]{2,1,0:T(8,128)(2,1)}), bf16[8,256,768]{2,1,0:T(8,128)(2,1)}, u32[]{:S(2)}, u32[]{:S(2)}) async-start(bf16[8,256,768]{2,1,0:T(8,128)(2,1)} %bitcast.149), calls=%async_computation | async-start | bytes 6291456 | tf_op jit(solution)/shard_map/all_to_all | solution.py:653
  535.6 11.0 %copy-start.21 = (bf16[256,4,384]{2,0,1:T(8,128)(2,1)S(1)}, bf16[256,4,384]{2,0,1:T(8,128)(2,1)}, u32[]{:S(2)}) copy-start(bf16[256,4,384]{2,0,1:T(8,128)(2,1)} %copy.133) | copy-start | bytes 2359300
  557.0 354.7 %copy-start.39 = (f32[256]{0:T(256)S(1)}, f32[256]{0:T(256)}, u32[]{:S(2)}) copy-start(f32[256]{0:T(256)} %copy-done.38) | copy-start | bytes 3076
  557.0 354.7 %copy-start.15 = (bf16[256,1536]{1,0:T(8,128)(2,1)S(1)}, bf16[256,1536]{1,0:T(8,128)(2,1)}, u32[]{:S(2)}) copy-start(bf16[256,1536]{1,0:T(8,128)(2,1)} %copy-done.14) | copy-start | bytes 2359300
  557.0 354.7 %copy-start.17 = (bf16[1,256,1536]{2,1,0:T(8,128)(2,1)S(1)}, bf16[1,256,1536]{2,1,0:T(8,128)(2,1)}, u32[]{:S(2)}) copy-start(bf16[1,256,1536]{2,1,0:T(8,128)(2,1)} %param.11) | copy-start | bytes 2359300
  557.0 354.7 %copy-start.28 = (f32[256,1536]{1,0:T(8,128)S(1)}, f32[256,1536]{1,0:T(8,128)}, u32[]{:S(2)}) copy-start(f32[256,1536]{1,0:T(8,128)} %get-tuple-element.113) | copy-start | bytes 4718596
  753.1 54.2 %collective-permute-start.2 = (f32[384,1536]{1,0:T(8,128)S(1)}, f32[384,1536]{1,0:T(8,128)S(1)}, u32[]{:S(2)}, u32[]{:S(2)}) collective-permute-start(f32[384,1536]{1,0:T(8,128)S(1)} %get-tuple-element.37.refs_0_), channel_id=1, source_target_pairs={{0,2},{1,3},{2,0},{3,1},{4,6},{5,7},{6,4},{7,5},{8,10},{9,11},{10,... | collective-permute-start | bytes 7077896 | tf_op jit(solution)/shard_map/ppermute | solution.py:694
  754.6 54.2 %collective-permute-start.7 = (f32[384,1536]{1,0:T(8,128)S(1)}, f32[384,1536]{1,0:T(8,128)}, u32[]{:S(2)}, u32[]{:S(2)}) collective-permute-start(f32[384,1536]{1,0:T(8,128)S(1)} %get-tuple-element.38.refs_1_), channel_id=1, source_target_pairs={{0,4},{1,5},{2,6},{3,7},{4,0},{5,1},{6,2},{7,3},{8,12},{9,13},{10,... | collective-permute-start | bytes 7077896 | tf_op jit(solution)/shard_map/ppermute | solution.py:694
  755.2 101.9 %collective-permute-start.3 = (f32[384,1536]{1,0:T(8,128)S(1)}, f32[384,1536]{1,0:T(8,128)}, u32[]{:S(2)}, u32[]{:S(2)}) collective-permute-start(f32[384,1536]{1,0:T(8,128)S(1)} %get-tuple-element.38.refs_1_), channel_id=1, source_target_pairs={{0,2},{1,3},{2,0},{3,1},{4,6},{5,7},{6,4},{7,5},{8,10},{9,11},{10,... | collective-permute-start | bytes 7077896 | tf_op jit(solution)/shard_map/ppermute | solution.py:694
  756.7 102.8 %collective-permute-start.6 = (f32[384,1536]{1,0:T(8,128)S(1)}, f32[384,1536]{1,0:T(8,128)}, u32[]{:S(2)}, u32[]{:S(2)}) collective-permute-start(f32[384,1536]{1,0:T(8,128)S(1)} %get-tuple-element.37.refs_0_), channel_id=1, source_target_pairs={{0,4},{1,5},{2,6},{3,7},{4,0},{5,1},{6,2},{7,3},{8,12},{9,13},{10,... | collective-permute-start | bytes 7077896 | tf_op jit(solution)/shard_map/ppermute | solution.py:694
  757.2 103.6 %collective-permute-start = (f32[384,1536]{1,0:T(8,128)S(1)}, f32[384,1536]{1,0:T(8,128)S(1)}, u32[]{:S(2)}, u32[]{:S(2)}) collective-permute-start(f32[384,1536]{1,0:T(8,128)S(1)} %get-tuple-element.37.refs_0_), channel_id=1, source_target_pairs={{0,1},{1,0},{2,3},{3,2},{4,5},{5,4},{6,7},{7,6},{8,9},{9,8},{10,11... | collective-permute-start | bytes 7077896 | tf_op jit(solution)/shard_map/ppermute | solution.py:694
  807.3 55.5 %collective-permute-start.1 = (f32[384,1536]{1,0:T(8,128)S(1)}, f32[384,1536]{1,0:T(8,128)S(1)}, u32[]{:S(2)}, u32[]{:S(2)}) collective-permute-start(f32[384,1536]{1,0:T(8,128)S(1)} %get-tuple-element.38.refs_1_), channel_id=1, source_target_pairs={{0,1},{1,0},{2,3},{3,2},{4,5},{5,4},{6,7},{7,6},{8,9},{9,8},{10,11... | collective-permute-start | bytes 7077896 | tf_op jit(solution)/shard_map/ppermute | solution.py:694
  808.9 100.0 %collective-permute-start.10 = (f32[384,1536]{1,0:T(8,128)S(1)}, f32[384,1536]{1,0:T(8,128)}, u32[]{:S(2)}, u32[]{:S(2)}) collective-permute-start(f32[384,1536]{1,0:T(8,128)S(1)} %collective-permute-done.2.refs_4_), channel_id=1, source_target_pairs={{0,4},{1,5},{2,6},{3,7},{4,0},{5,1},{6,2},{7,3},{8,12},{9,13},{10,... | collective-permute-start | bytes 7077896 | tf_op jit(solution)/shard_map/ppermute | solution.py:694
  857.1 52.7 %collective-permute-start.11 = (f32[384,1536]{1,0:T(8,128)}, f32[384,1536]{1,0:T(8,128)}, u32[]{:S(2)}, u32[]{:S(2)}) collective-permute-start(f32[384,1536]{1,0:T(8,128)} %collective-permute-done.7.refs_9_), channel_id=1, source_target_pairs={{0,2},{1,3},{2,0},{3,1},{4,6},{5,7},{6,4},{7,5},{8,10},{9,11},{10,... | collective-permute-start | bytes 7077896 | tf_op jit(solution)/shard_map/ppermute | solution.py:694
  859.4 50.4 %collective-permute-start.4 = (f32[384,1536]{1,0:T(8,128)S(1)}, f32[384,1536]{1,0:T(8,128)S(1)}, u32[]{:S(2)}, u32[]{:S(2)}) collective-permute-start(f32[384,1536]{1,0:T(8,128)S(1)} %collective-permute-done.2.refs_4_), channel_id=1, source_target_pairs={{0,1},{1,0},{2,3},{3,2},{4,5},{5,4},{6,7},{7,6},{8,9},{9,8},{10,11... | collective-permute-start | bytes 7077896 | tf_op jit(solution)/shard_map/ppermute | solution.py:694
  862.2 52.7 %collective-permute-start.9 = (f32[384,1536]{1,0:T(8,128)}, f32[384,1536]{1,0:T(8,128)}, u32[]{:S(2)}, u32[]{:S(2)}) collective-permute-start(f32[384,1536]{1,0:T(8,128)} %collective-permute-done.7.refs_9_), channel_id=1, source_target_pairs={{0,1},{1,0},{2,3},{3,2},{4,5},{5,4},{6,7},{7,6},{8,9},{9,8},{10,11... | collective-permute-start | bytes 7077896 | tf_op jit(solution)/shard_map/ppermute | solution.py:694
  864.1 50.8 %collective-permute-start.5 = (f32[384,1536]{1,0:T(8,128)}, f32[384,1536]{1,0:T(8,128)}, u32[]{:S(2)}, u32[]{:S(2)}) collective-permute-start(f32[384,1536]{1,0:T(8,128)} %collective-permute-done.3.refs_5_), channel_id=1, source_target_pairs={{0,1},{1,0},{2,3},{3,2},{4,5},{5,4},{6,7},{7,6},{8,9},{9,8},{10,11... | collective-permute-start | bytes 7077896 | tf_op jit(solution)/shard_map/ppermute | solution.py:694
  908.8 6.1 collective-permute-start.8
  909.8 7.3 collective-permute-start.12
  911.2 9.2 collective-permute-start.13
  (41 other events, 121.6 us)
Sparse Core Ops, SparseCore 0:
  186.9 320.2 all-gather.2
